TPU v7x, 32 devices: a whole 2x2x4 slice. The times are simulated.
32 devices in a mesh: tm: 4 (over z), space: 8 (over y, x, core).
Axes of the slice: x: 2, y: 2, z: 4, core: 2. Of those that a mesh axis runs over, the one named last changes fastest.
Arguments:
- initial: float32 [32, 256, 512], P('space'), may hold values from -6 to 6
- iterate: float32 [4, 32, 256, 512], P('tm', 'space'), may hold values from -6 to 6
- diffusivity: float32 [32, 256, 512], P('space'), may hold values from 0.25 to 1
Outputs:
- corrected: float32 [4, 32, 256, 512], P('tm', 'space')
All inputs are finite; a program needn't handle non-finite values.
Results may differ from a plain program's by a relative error of at most 0.0001.
Values sent between devices are 32-bit elements; how exact they have to be, the bound alone decides.
No kernel may reach another device: no remote copies, remote signals or barrier semaphores. Data moves between devices by JAX's collectives and lax.ppermute only.
A program may use at most 128 MiB of HBM per device.

v0:
```python
import jax
import jax.numpy as jnp
from jax import lax
from jax.sharding import PartitionSpec as P

STEPS = 4


courant = 0.15


def extended(cells, sides, width):
    for axis, dim in sides:
        count = lax.axis_size(axis)
        ends = count - 1
        head = lax.slice_in_dim(cells, 0, width, axis=dim)
        tail = lax.slice_in_dim(cells, cells.shape[dim] - width, cells.shape[dim], axis=dim)
        cells = jnp.concatenate(
            [
                lax.ppermute(tail, axis, [(i, (i + 1) % count) for i in range(ends)]),
                cells,
                lax.ppermute(head, axis, [((i + 1) % count, i) for i in range(ends)]),
            ],
            axis=dim,
        )
    return cells


def shifted(x, axis, by):
    devices = lax.axis_size(axis)
    pairs = [(i, i + by) for i in range(devices) if 0 <= i + by < devices]
    return lax.ppermute(x, axis, pairs)


def advance(values, diffusivity):
    center = values[1:-1]
    coeff = diffusivity[1:-1]
    flux = (coeff + diffusivity[2:]) * (values[2:] - center) + (coeff + diffusivity[:-2]) * (
        values[:-2] - center
    )
    side_values = jnp.pad(center, ((0, 0), (1, 1), (0, 0)))
    side_coeff = jnp.pad(coeff, ((0, 0), (1, 1), (0, 0)))
    flux = (
        flux
        + (coeff + side_coeff[:, 2:]) * (side_values[:, 2:] - center)
        + (coeff + side_coeff[:, :-2]) * (side_values[:, :-2] - center)
    )
    cross_values = jnp.pad(center, ((0, 0), (0, 0), (1, 1)))
    cross_coeff = jnp.pad(coeff, ((0, 0), (0, 0), (1, 1)))
    flux = (
        flux
        + (coeff + cross_coeff[:, :, 2:]) * (cross_values[:, :, 2:] - center)
        + (coeff + cross_coeff[:, :, :-2]) * (cross_values[:, :, :-2] - center)
    )
    return center + 0.5 * courant * flux


def pair_matrix(width):
    fine_index = jnp.arange(width, dtype=jnp.int32)[:, None] // 2
    coarse_index = jnp.arange(width // 2, dtype=jnp.int32)[None, :]
    return (fine_index == coarse_index).astype(jnp.float32)


def restrict(values):
    depth_z, depth_y, depth_x = values.shape
    summed = values.reshape(depth_z // 2, 2, depth_y // 2, 2, depth_x).sum(axis=(1, 3))
    pairing = pair_matrix(depth_x)
    return 0.125 * jnp.dot(summed, pairing, precision=lax.Precision.HIGHEST)


def prolong(values):
    depth_z, depth_y, depth_x = values.shape
    pairing = pair_matrix(2 * depth_x)
    widened = jnp.dot(values, pairing.T, precision=lax.Precision.HIGHEST)
    spread = jnp.broadcast_to(widened[:, None, :, None, :], (depth_z, 2, depth_y, 2, 2 * depth_x))
    return spread.reshape(2 * depth_z, 2 * depth_y, 2 * depth_x)


def coarse_step(error, coarse_wide):
    padded = extended(error, (("space", 0),), 1)
    return advance(padded, coarse_wide)


def local(initial, iterate, diffusivity):
    planes = initial.shape[0]
    previous = shifted(iterate, "tm", 1)
    leading = lax.axis_index("tm") == 0
    begin_state = jnp.where(leading, initial, previous[0])
    margin = 2
    diff_wide = extended(diffusivity, (("space", 0),), margin)
    state = begin_state
    local_diff = diff_wide[margin - 1 : margin + planes + 1]
    for number in range(STEPS):
        padded = extended(state, (("space", 0),), 1)
        state = advance(padded, local_diff)
    residual = state - iterate[0]
    coarse_wide = restrict(diff_wide)
    restricted = restrict(residual)
    error = restricted
    power = restricted
    for offset in range(1, lax.axis_size("tm")):
        power = coarse_step(power, coarse_wide)
        error = error + shifted(power, "tm", offset)
    corrected = iterate[0] + prolong(error)
    return corrected[None]


def solution(mesh):
    placed = (P("space", None, None), P("tm", "space", None, None), P("space", None, None))
    return jax.shard_map(
        local, mesh=mesh, in_specs=placed, out_specs=P("tm", "space", None, None), check_vma=False
    )
```

profile of v0, /device:TPU:28, one launch (start us, length us, event | category | flops | bytes accessed | tf_op | source)
XLA Modules:
  0.0 226.3 jit_solution(3150281126101812306)
XLA Ops:
  0.0 1.4 collective-permute-start
  1.4 3.0 %fusion.145 = (f32[2,256,512]{2,1,0:T(8,128)}, f32[2,256,512]{2,1,0:T(8,128)}) fusion(f32[4,256,512]{2,1,0:T(8,128)} %param.5), kind=kLoop, calls=%fused_computation.195 | loop fusion | bytes 4194304 | tf_op jit(solution)/shard_map/slice | solution.py:17
  4.5 2.8 %collective-permute-start.1 = (f32[2,256,512]{2,1,0:T(8,128)}, f32[2,256,512]{2,1,0:T(8,128)S(1)}, u32[]{:S(2)}, u32[]{:S(2)}) collective-permute-start(f32[2,256,512]{2,1,0:T(8,128)} %get-tuple-element.17), channel_id=1, source_target_pairs={{1,0},{2,1},{3,2},{4,3},{5,4},{6,5},{7,6},{9,8},{10,9},{11,10},{12... | collective-permute-start | bytes 3145736 | tf_op jit(solution)/shard_map/ppermute | solution.py:22
  7.2 1.9 collective-permute-start.3
  9.2 40.5 %collective-permute-done = f32[1,4,256,512]{3,2,1,0:T(8,128)} collective-permute-done((f32[1,4,256,512]{3,2,1,0:T(8,128)}, f32[1,4,256,512]{3,2,1,0:T(8,128)}, u32[]{:S(2)}, u32[]{:S(2)}) %collective-permute-start) | collective-permute-done | bytes 2097184 | tf_op jit(solution)/shard_map/ppermute | solution.py:32
  49.7 2.1 bitcast_select_fusion
  51.8 0.0 copy-start.5
  51.8 0.0 copy-start
  51.8 0.1 fusion.146
  51.9 2.2 collective-permute-start.2
  54.1 2.4 %collective-permute-start.4 = (f32[1,256,512]{2,1,0:T(8,128)S(1)}, f32[1,256,512]{2,1,0:T(8,128)S(1)}, u32[]{:S(2)}, u32[]{:S(2)}) collective-permute-start(f32[1,256,512]{2,1,0:T(8,128)S(1)} %get-tuple-element.19), channel_id=1, source_target_pairs={{0,1},{1,2},{2,3},{3,4},{4,5},{5,6},{6,7},{8,9},{9,10},{10,11},{11... | collective-permute-start | bytes 1572872 | tf_op jit(solution)/shard_map/ppermute | solution.py:20
  56.5 0.0 collective-permute-done.1
  56.5 0.0 collective-permute-done.3
  56.5 7.0 %collective-permute-done.2 = f32[1,256,512]{2,1,0:T(8,128)S(1)} collective-permute-done((f32[1,256,512]{2,1,0:T(8,128)S(1)}, f32[1,256,512]{2,1,0:T(8,128)S(1)}, u32[]{:S(2)}, u32[]{:S(2)}) %collective-permute-start.2) | collective-permute-done | bytes 524320 | tf_op jit(solution)/shard_map/ppermute | solution.py:22
  63.5 4.7 %collective-permute-done.4 = f32[1,256,512]{2,1,0:T(8,128)S(1)} collective-permute-done((f32[1,256,512]{2,1,0:T(8,128)S(1)}, f32[1,256,512]{2,1,0:T(8,128)S(1)}, u32[]{:S(2)}, u32[]{:S(2)}) %collective-permute-start.4) | collective-permute-done | bytes 524320 | tf_op jit(solution)/shard_map/ppermute | solution.py:20
  68.3 9.7 %fusion.7 = (f32[4,256,512]{2,1,0:T(8,128)}, f32[4,256,512]{2,1,0:T(8,128)S(1)}, f32[4,256,512]{2,1,0:T(8,128)S(1)}, f32[4,256,512]{2,1,0:T(8,128)S(1)}, f32[4,256,512]{2,1,0:T(8,128)}) fusion(f32[4,256,512]{2,1,0:T(8,128)} %copy-done.5, f32[1,256,512]{2,1,0:T(8,128)S(1)} %collective-permute-done.4, f32[1,256,512]{2,1,0:T(8,128)S(1)} %collective-permute-done.2, ...), kind=kLoop, calls=%fused_computation.18 | loop fusion | flops 15204352 | bytes 17825792 | tf_op jit(solution)/shard_map/add | solution.py:55
  78.0 2.2 fusion.144
  80.3 2.2 collective-permute-start.5
  82.4 2.4 %collective-permute-start.6 = (f32[1,256,512]{2,1,0:T(8,128)S(1)}, f32[1,256,512]{2,1,0:T(8,128)S(1)}, u32[]{:S(2)}, u32[]{:S(2)}) collective-permute-start(f32[1,256,512]{2,1,0:T(8,128)S(1)} %get-tuple-element.15), channel_id=1, source_target_pairs={{0,1},{1,2},{2,3},{3,4},{4,5},{5,6},{6,7},{8,9},{9,10},{10,11},{11... | collective-permute-start | bytes 1572872 | tf_op jit(solution)/shard_map/ppermute | solution.py:20
  84.9 7.9 %collective-permute-done.5 = f32[1,256,512]{2,1,0:T(8,128)S(1)} collective-permute-done((f32[1,256,512]{2,1,0:T(8,128)S(1)}, f32[1,256,512]{2,1,0:T(8,128)S(1)}, u32[]{:S(2)}, u32[]{:S(2)}) %collective-permute-start.5) | collective-permute-done | bytes 524320 | tf_op jit(solution)/shard_map/ppermute | solution.py:22
  92.8 1.0 collective-permute-done.6
  93.8 8.1 %fusion.15 = f32[4,256,512]{2,1,0:T(8,128)S(1)} fusion(f32[4,256,512]{2,1,0:T(8,128)} %get-tuple-element.5, f32[4,256,512]{2,1,0:T(8,128)S(1)} %copy-done.4, f32[4,256,512]{2,1,0:T(8,128)S(1)} %get-tuple-element.8, f32[1,256,512]{2,1,0:T(8,128)S(1)} %collective-permute-done.6, f32[1,256,512]{2,1,0:T(8,128)S(1)} %collective-permute-done.5, ...), kind=kLoop, calls=%fused_computation.26 | loop fusion | flops 13107200 | bytes 17825792 | tf_op jit(solution)/shard_map/add | solution.py:55
  102.0 0.1 fusion.143
  102.0 3.7 %collective-permute-start.7 = (f32[1,256,512]{2,1,0:T(8,128)S(1)}, f32[1,256,512]{2,1,0:T(8,128)S(1)}, u32[]{:S(2)}, u32[]{:S(2)}) collective-permute-start(f32[1,256,512]{2,1,0:T(8,128)S(1)} %get-tuple-element.12), channel_id=1, source_target_pairs={{1,0},{2,1},{3,2},{4,3},{5,4},{6,5},{7,6},{9,8},{10,9},{11,10},{12... | collective-permute-start | bytes 1572872 | tf_op jit(solution)/shard_map/ppermute | solution.py:22
  105.7 1.9 collective-permute-start.8
  107.7 7.4 %collective-permute-done.7 = f32[1,256,512]{2,1,0:T(8,128)S(1)} collective-permute-done((f32[1,256,512]{2,1,0:T(8,128)S(1)}, f32[1,256,512]{2,1,0:T(8,128)S(1)}, u32[]{:S(2)}, u32[]{:S(2)}) %collective-permute-start.7) | collective-permute-done | bytes 524320 | tf_op jit(solution)/shard_map/ppermute | solution.py:22
  115.1 2.1 collective-permute-done.8
  117.1 4.8 %fusion.23 = f32[4,256,512]{2,1,0:T(8,128)S(1)} fusion(f32[4,256,512]{2,1,0:T(8,128)S(1)} %fusion.15, f32[4,256,512]{2,1,0:T(8,128)S(1)} %copy-done.4, f32[4,256,512]{2,1,0:T(8,128)S(1)} %get-tuple-element.8, f32[1,256,512]{2,1,0:T(8,128)S(1)} %collective-permute-done.8, f32[1,256,512]{2,1,0:T(8,128)S(1)} %collective-permute-done.7, ...), kind=kLoop, calls=%fused_computation.34 | loop fusion | flops 13107200 | bytes 17825792 | tf_op jit(solution)/shard_map/add | solution.py:55
  122.0 0.0 copy-start.6
  122.0 1.3 copy-done.6
  123.3 1.1 fusion.142
  124.3 2.9 %collective-permute-start.10 = (f32[1,256,512]{2,1,0:T(8,128)}, f32[1,256,512]{2,1,0:T(8,128)}, u32[]{:S(2)}, u32[]{:S(2)}) collective-permute-start(f32[1,256,512]{2,1,0:T(8,128)} %get-tuple-element.11), channel_id=1, source_target_pairs={{0,1},{1,2},{2,3},{3,4},{4,5},{5,6},{6,7},{8,9},{9,10},{10,11},{11... | collective-permute-start | bytes 1572872 | tf_op jit(solution)/shard_map/ppermute | solution.py:20
  127.2 3.7 %collective-permute-start.9 = (f32[1,256,512]{2,1,0:T(8,128)}, f32[1,256,512]{2,1,0:T(8,128)}, u32[]{:S(2)}, u32[]{:S(2)}) collective-permute-start(f32[1,256,512]{2,1,0:T(8,128)} %get-tuple-element.10), channel_id=1, source_target_pairs={{1,0},{2,1},{3,2},{4,3},{5,4},{6,5},{7,6},{9,8},{10,9},{11,10},{12... | collective-permute-start | bytes 1572872 | tf_op jit(solution)/shard_map/ppermute | solution.py:22
  131.0 4.0 %pad_maximum_fusion = f32[8,256,512]{2,1,0:T(8,128)} fusion(f32[2,256,512]{2,1,0:T(8,128)S(1)} %collective-permute-done.1, f32[4,256,512]{2,1,0:T(8,128)S(1)} %copy-done, f32[2,256,512]{2,1,0:T(8,128)} %collective-permute-done.3), kind=kLoop, calls=%fused_computation | loop fusion | flops 2097152 | bytes 8388608 | tf_op jit(solution)/shard_map/concatenate | solution.py:18
  135.0 5.8 %reshape.49 = f32[4,2,128,2,512]{4,3,2,1,0:T(2,128)} reshape(f32[8,256,512]{2,1,0:T(8,128)} %pad_maximum_fusion) | data formatting | bytes 8388608 | tf_op jit(solution)/shard_map/reshape | solution.py:66
  140.8 6.2 %reduce_sum.19 = f32[4,128,512]{2,1,0:T(8,128)} reduce(f32[4,2,128,2,512]{4,3,2,1,0:T(2,128)} %reshape.49, f32[]{:T(128)} %constant.30.clone.1), dimensions={1,3}, to_apply=%region_1.2 | reduce | flops 786432 | bytes 5242884 | tf_op jit(solution)/shard_map/reduce_sum | solution.py:66
  147.1 0.0 collective-permute-done.10
  147.1 12.6 %fusion.32 = f32[4,256,512]{2,1,0:T(8,128)} fusion(f32[4,256,512]{2,1,0:T(8,128)} %copy-done.6, f32[4,256,512]{2,1,0:T(8,128)} %get-tuple-element.9, f32[4,256,512]{2,1,0:T(8,128)} %copy-done.3, f32[1,256,512]{2,1,0:T(8,128)} %collective-permute-done.10, f32[1,256,512]{2,1,0:T(8,128)} %collective-permute-done.9, f32[1,4,256,512]{3,2,1,0:T(8,128)} %param.4, ...), kind=kLoop, calls=%fused_computation.43 | loop fusion | flops 13631488 | bytes 19922944 | tf_op jit(solution)/shard_map/sub | solution.py:96
  159.6 2.5 %reshape.48 = f32[2,2,128,2,512]{4,3,2,1,0:T(2,128)S(1)} reshape(f32[4,256,512]{2,1,0:T(8,128)} %fusion.32) | data formatting | bytes 4194304 | tf_op jit(solution)/shard_map/reshape | solution.py:66
  162.2 2.5 %reduce_sum.18 = f32[2,128,512]{2,1,0:T(8,128)} reduce(f32[2,2,128,2,512]{4,3,2,1,0:T(2,128)S(1)} %reshape.48, f32[]{:T(128)} %constant.30.clone.1), dimensions={1,3}, to_apply=%region_0.1 | reduce | flops 393216 | bytes 2621444 | tf_op jit(solution)/shard_map/reduce_sum | solution.py:66
  164.7 1.5 convolution_multiply_fusion.1
  166.3 1.9 collective-permute-start.11
  168.2 2.8 %collective-permute-start.12 = (f32[1,128,256]{2,1,0:T(8,128)S(1)}, f32[1,128,256]{2,1,0:T(8,128)S(1)}, u32[]{:S(2)}, u32[]{:S(2)}) collective-permute-start(f32[1,128,256]{2,1,0:T(8,128)S(1)} %get-tuple-element.25), channel_id=1, source_target_pairs={{0,1},{1,2},{2,3},{3,4},{4,5},{5,6},{6,7},{8,9},{9,10},{10,11},{11... | collective-permute-start | bytes 393224 | tf_op jit(solution)/shard_map/ppermute | solution.py:20
  171.0 0.7 convolution_multiply_fusion
  171.8 3.6 %collective-permute-done.12 = f32[1,128,256]{2,1,0:T(8,128)S(1)} collective-permute-done((f32[1,128,256]{2,1,0:T(8,128)S(1)}, f32[1,128,256]{2,1,0:T(8,128)S(1)}, u32[]{:S(2)}, u32[]{:S(2)}) %collective-permute-start.12) | collective-permute-done | bytes 131104 | tf_op jit(solution)/shard_map/ppermute | solution.py:20
  175.4 0.4 fusion.79
  175.8 1.9 collective-permute-start.14
  177.7 2.4 %collective-permute-start.15 = (f32[1,128,256]{2,1,0:T(8,128)S(1)}, f32[1,128,256]{2,1,0:T(8,128)S(1)}, u32[]{:S(2)}, u32[]{:S(2)}) collective-permute-start(f32[1,128,256]{2,1,0:T(8,128)S(1)} %get-tuple-element.23), channel_id=1, source_target_pairs={{0,1},{1,2},{2,3},{3,4},{4,5},{5,6},{6,7},{8,9},{9,10},{10,11},{11... | collective-permute-start | bytes 393224 | tf_op jit(solution)/shard_map/ppermute | solution.py:20
  180.1 0.1 collective-permute-done.14
  180.2 4.7 %collective-permute-done.15 = f32[1,128,256]{2,1,0:T(8,128)S(1)} collective-permute-done((f32[1,128,256]{2,1,0:T(8,128)S(1)}, f32[1,128,256]{2,1,0:T(8,128)S(1)}, u32[]{:S(2)}, u32[]{:S(2)}) %collective-permute-start.15) | collective-permute-done | bytes 131104 | tf_op jit(solution)/shard_map/ppermute | solution.py:20
  184.9 0.4 fusion.89
  185.3 1.9 collective-permute-start.17
  187.2 2.4 %collective-permute-start.18 = (f32[1,128,256]{2,1,0:T(8,128)S(1)}, f32[1,128,256]{2,1,0:T(8,128)S(1)}, u32[]{:S(2)}, u32[]{:S(2)}) collective-permute-start(f32[1,128,256]{2,1,0:T(8,128)S(1)} %get-tuple-element.21), channel_id=1, source_target_pairs={{0,1},{1,2},{2,3},{3,4},{4,5},{5,6},{6,7},{8,9},{9,10},{10,11},{11... | collective-permute-start | bytes 393224 | tf_op jit(solution)/shard_map/ppermute | solution.py:20
  189.6 1.3 collective-permute-start.13
  190.9 1.5 collective-permute-start.16
  192.5 1.9 collective-permute-done.18
  194.4 0.4 fusion.99
  194.8 1.3 collective-permute-start.19
  196.1 4.2 %collective-permute-done.13 = f32[2,128,256]{2,1,0:T(8,128)S(1)} collective-permute-done((f32[2,128,256]{2,1,0:T(8,128)S(1)}, f32[2,128,256]{2,1,0:T(8,128)S(1)}, u32[]{:S(2)}, u32[]{:S(2)}) %collective-permute-start.13) | collective-permute-done | bytes 262176 | tf_op jit(solution)/shard_map/ppermute | solution.py:32
  200.3 16.5 %collective-permute-done.16 = f32[2,128,256]{2,1,0:T(8,128)S(1)} collective-permute-done((f32[2,128,256]{2,1,0:T(8,128)S(1)}, f32[2,128,256]{2,1,0:T(8,128)S(1)}, u32[]{:S(2)}, u32[]{:S(2)}) %collective-permute-start.16) | collective-permute-done | bytes 262176 | tf_op jit(solution)/shard_map/ppermute | solution.py:32
  216.8 0.5 fusion.66
  217.3 1.9 broadcast_in_dim.2
  219.2 3.8 %reshape.50 = f32[1,4,256,512]{3,2,1,0:T(8,128)} reshape(f32[2,2,128,2,512]{4,3,2,1,0:T(2,128)} %broadcast_in_dim.2) | data formatting | bytes 4194304 | tf_op jit(solution)/shard_map/reshape | solution.py:76
  223.0 3.4 %add.304 = f32[1,4,256,512]{3,2,1,0:T(8,128)} add(f32[1,4,256,512]{3,2,1,0:T(8,128)S(1)} %copy-done.7, f32[1,4,256,512]{3,2,1,0:T(8,128)} %reshape.50) | non-fusion elementwise | flops 524288 | bytes 6291456 | tf_op jit(solution)/shard_map/add | solution.py:104
  (25 shorter events, 0.1 us)
Async XLA Ops:
  0.0 49.7 %copy-start.9 = (f32[4,256,512]{2,1,0:T(8,128)S(1)}, f32[4,256,512]{2,1,0:T(8,128)}, u32[]{:S(2)}) copy-start(f32[4,256,512]{2,1,0:T(8,128)} %param.3) | copy-start | bytes 6291460
  0.0 49.7 %collective-permute-start = (f32[1,4,256,512]{3,2,1,0:T(8,128)}, f32[1,4,256,512]{3,2,1,0:T(8,128)}, u32[]{:S(2)}, u32[]{:S(2)}) collective-permute-start(f32[1,4,256,512]{3,2,1,0:T(8,128)} %param.4), channel_id=1, source_target_pairs={{0,8},{8,16},{16,24},{1,9},{9,17},{17,25},{2,10},{10,18},{18,26},{... | collective-permute-start | bytes 6291464 | tf_op jit(solution)/shard_map/ppermute | solution.py:32
  4.5 52.0 %collective-permute-start.1 = (f32[2,256,512]{2,1,0:T(8,128)}, f32[2,256,512]{2,1,0:T(8,128)S(1)}, u32[]{:S(2)}, u32[]{:S(2)}) collective-permute-start(f32[2,256,512]{2,1,0:T(8,128)} %get-tuple-element.17), channel_id=1, source_target_pairs={{1,0},{2,1},{3,2},{4,3},{5,4},{6,5},{7,6},{9,8},{10,9},{11,10},{12... | collective-permute-start | bytes 3145736 | tf_op jit(solution)/shard_map/ppermute | solution.py:22
  7.2 49.3 %collective-permute-start.3 = (f32[2,256,512]{2,1,0:T(8,128)}, f32[2,256,512]{2,1,0:T(8,128)}, u32[]{:S(2)}, u32[]{:S(2)}) collective-permute-start(f32[2,256,512]{2,1,0:T(8,128)} %get-tuple-element.16), channel_id=1, source_target_pairs={{0,1},{1,2},{2,3},{3,4},{4,5},{5,6},{6,7},{8,9},{9,10},{10,11},{11... | collective-permute-start | bytes 3145736 | tf_op jit(solution)/shard_map/ppermute | solution.py:20
  51.8 11.8 %copy-start.5 = (f32[4,256,512]{2,1,0:T(8,128)}, f32[4,256,512]{2,1,0:T(8,128)S(1)}, u32[]{:S(2)}) copy-start(f32[4,256,512]{2,1,0:T(8,128)S(1)} %bitcast_select_fusion) | copy-start | bytes 6291460
  51.8 16.5 %copy-start = (f32[4,256,512]{2,1,0:T(8,128)S(1)}, f32[4,256,512]{2,1,0:T(8,128)}, u32[]{:S(2)}) copy-start(f32[4,256,512]{2,1,0:T(8,128)} %param.5) | copy-start | bytes 6291460
  51.9 11.7 %collective-permute-start.2 = (f32[1,256,512]{2,1,0:T(8,128)S(1)}, f32[1,256,512]{2,1,0:T(8,128)S(1)}, u32[]{:S(2)}, u32[]{:S(2)}) collective-permute-start(f32[1,256,512]{2,1,0:T(8,128)S(1)} %get-tuple-element.18), channel_id=1, source_target_pairs={{1,0},{2,1},{3,2},{4,3},{5,4},{6,5},{7,6},{9,8},{10,9},{11,10},{12... | collective-permute-start | bytes 1572872 | tf_op jit(solution)/shard_map/ppermute | solution.py:22
  54.1 14.2 %collective-permute-start.4 = (f32[1,256,512]{2,1,0:T(8,128)S(1)}, f32[1,256,512]{2,1,0:T(8,128)S(1)}, u32[]{:S(2)}, u32[]{:S(2)}) collective-permute-start(f32[1,256,512]{2,1,0:T(8,128)S(1)} %get-tuple-element.19), channel_id=1, source_target_pairs={{0,1},{1,2},{2,3},{3,4},{4,5},{5,6},{6,7},{8,9},{9,10},{10,11},{11... | collective-permute-start | bytes 1572872 | tf_op jit(solution)/shard_map/ppermute | solution.py:20
  78.0 39.1 %copy-start.1 = (f32[4,256,512]{2,1,0:T(8,128)}, f32[4,256,512]{2,1,0:T(8,128)S(1)}, u32[]{:S(2)}) copy-start(f32[4,256,512]{2,1,0:T(8,128)S(1)} %get-tuple-element.6) | copy-start | bytes 6291460
  78.0 39.1 %copy-start.2 = (f32[4,256,512]{2,1,0:T(8,128)}, f32[4,256,512]{2,1,0:T(8,128)S(1)}, u32[]{:S(2)}) copy-start(f32[4,256,512]{2,1,0:T(8,128)S(1)} %get-tuple-element.7) | copy-start | bytes 6291460
  78.0 39.1 %copy-start.3 = (f32[4,256,512]{2,1,0:T(8,128)}, f32[4,256,512]{2,1,0:T(8,128)S(1)}, u32[]{:S(2)}) copy-start(f32[4,256,512]{2,1,0:T(8,128)S(1)} %get-tuple-element.8) | copy-start | bytes 6291460
  78.0 15.8 %copy-start.4 = (f32[4,256,512]{2,1,0:T(8,128)S(1)}, f32[4,256,512]{2,1,0:T(8,128)}, u32[]{:S(2)}) copy-start(f32[4,256,512]{2,1,0:T(8,128)} %get-tuple-element.9) | copy-start | bytes 6291460
  80.3 12.5 %collective-permute-start.5 = (f32[1,256,512]{2,1,0:T(8,128)S(1)}, f32[1,256,512]{2,1,0:T(8,128)S(1)}, u32[]{:S(2)}, u32[]{:S(2)}) collective-permute-start(f32[1,256,512]{2,1,0:T(8,128)S(1)} %get-tuple-element.14), channel_id=1, source_target_pairs={{1,0},{2,1},{3,2},{4,3},{5,4},{6,5},{7,6},{9,8},{10,9},{11,10},{12... | collective-permute-start | bytes 1572872 | tf_op jit(solution)/shard_map/ppermute | solution.py:22
  82.4 11.4 %collective-permute-start.6 = (f32[1,256,512]{2,1,0:T(8,128)S(1)}, f32[1,256,512]{2,1,0:T(8,128)S(1)}, u32[]{:S(2)}, u32[]{:S(2)}) collective-permute-start(f32[1,256,512]{2,1,0:T(8,128)S(1)} %get-tuple-element.15), channel_id=1, source_target_pairs={{0,1},{1,2},{2,3},{3,4},{4,5},{5,6},{6,7},{8,9},{9,10},{10,11},{11... | collective-permute-start | bytes 1572872 | tf_op jit(solution)/shard_map/ppermute | solution.py:20
  102.0 13.0 %collective-permute-start.7 = (f32[1,256,512]{2,1,0:T(8,128)S(1)}, f32[1,256,512]{2,1,0:T(8,128)S(1)}, u32[]{:S(2)}, u32[]{:S(2)}) collective-permute-start(f32[1,256,512]{2,1,0:T(8,128)S(1)} %get-tuple-element.12), channel_id=1, source_target_pairs={{1,0},{2,1},{3,2},{4,3},{5,4},{6,5},{7,6},{9,8},{10,9},{11,10},{12... | collective-permute-start | bytes 1572872 | tf_op jit(solution)/shard_map/ppermute | solution.py:22
  105.7 11.4 %collective-permute-start.8 = (f32[1,256,512]{2,1,0:T(8,128)S(1)}, f32[1,256,512]{2,1,0:T(8,128)S(1)}, u32[]{:S(2)}, u32[]{:S(2)}) collective-permute-start(f32[1,256,512]{2,1,0:T(8,128)S(1)} %get-tuple-element.13), channel_id=1, source_target_pairs={{0,1},{1,2},{2,3},{3,4},{4,5},{5,6},{6,7},{8,9},{9,10},{10,11},{11... | collective-permute-start | bytes 1572872 | tf_op jit(solution)/shard_map/ppermute | solution.py:20
  122.0 1.3 copy-start.6
  124.3 22.7 %collective-permute-start.10 = (f32[1,256,512]{2,1,0:T(8,128)}, f32[1,256,512]{2,1,0:T(8,128)}, u32[]{:S(2)}, u32[]{:S(2)}) collective-permute-start(f32[1,256,512]{2,1,0:T(8,128)} %get-tuple-element.11), channel_id=1, source_target_pairs={{0,1},{1,2},{2,3},{3,4},{4,5},{5,6},{6,7},{8,9},{9,10},{10,11},{11... | collective-permute-start | bytes 1572872 | tf_op jit(solution)/shard_map/ppermute | solution.py:20
  127.2 19.8 %collective-permute-start.9 = (f32[1,256,512]{2,1,0:T(8,128)}, f32[1,256,512]{2,1,0:T(8,128)}, u32[]{:S(2)}, u32[]{:S(2)}) collective-permute-start(f32[1,256,512]{2,1,0:T(8,128)} %get-tuple-element.10), channel_id=1, source_target_pairs={{1,0},{2,1},{3,2},{4,3},{5,4},{6,5},{7,6},{9,8},{10,9},{11,10},{12... | collective-permute-start | bytes 1572872 | tf_op jit(solution)/shard_map/ppermute | solution.py:22
  162.1 8.8 %copy-start.8 = (f32[4,128,512]{2,1,0:T(8,128)S(1)}, f32[4,128,512]{2,1,0:T(8,128)}, u32[]{:S(2)}) copy-start(f32[4,128,512]{2,1,0:T(8,128)} %reduce_sum.19) | copy-start | bytes 3145732
  166.3 5.5 %collective-permute-start.11 = (f32[1,128,256]{2,1,0:T(8,128)S(1)}, f32[1,128,256]{2,1,0:T(8,128)S(1)}, u32[]{:S(2)}, u32[]{:S(2)}) collective-permute-start(f32[1,128,256]{2,1,0:T(8,128)S(1)} %get-tuple-element.24), channel_id=1, source_target_pairs={{1,0},{2,1},{3,2},{4,3},{5,4},{6,5},{7,6},{9,8},{10,9},{11,10},{12... | collective-permute-start | bytes 393224 | tf_op jit(solution)/shard_map/ppermute | solution.py:22
  168.2 7.2 %collective-permute-start.12 = (f32[1,128,256]{2,1,0:T(8,128)S(1)}, f32[1,128,256]{2,1,0:T(8,128)S(1)}, u32[]{:S(2)}, u32[]{:S(2)}) collective-permute-start(f32[1,128,256]{2,1,0:T(8,128)S(1)} %get-tuple-element.25), channel_id=1, source_target_pairs={{0,1},{1,2},{2,3},{3,4},{4,5},{5,6},{6,7},{8,9},{9,10},{10,11},{11... | collective-permute-start | bytes 393224 | tf_op jit(solution)/shard_map/ppermute | solution.py:20
  175.8 4.4 %collective-permute-start.14 = (f32[1,128,256]{2,1,0:T(8,128)S(1)}, f32[1,128,256]{2,1,0:T(8,128)S(1)}, u32[]{:S(2)}, u32[]{:S(2)}) collective-permute-start(f32[1,128,256]{2,1,0:T(8,128)S(1)} %get-tuple-element.22), channel_id=1, source_target_pairs={{1,0},{2,1},{3,2},{4,3},{5,4},{6,5},{7,6},{9,8},{10,9},{11,10},{12... | collective-permute-start | bytes 393224 | tf_op jit(solution)/shard_map/ppermute | solution.py:22
  177.7 7.2 %collective-permute-start.15 = (f32[1,128,256]{2,1,0:T(8,128)S(1)}, f32[1,128,256]{2,1,0:T(8,128)S(1)}, u32[]{:S(2)}, u32[]{:S(2)}) collective-permute-start(f32[1,128,256]{2,1,0:T(8,128)S(1)} %get-tuple-element.23), channel_id=1, source_target_pairs={{0,1},{1,2},{2,3},{3,4},{4,5},{5,6},{6,7},{8,9},{9,10},{10,11},{11... | collective-permute-start | bytes 393224 | tf_op jit(solution)/shard_map/ppermute | solution.py:20
  185.3 7.2 %collective-permute-start.17 = (f32[1,128,256]{2,1,0:T(8,128)S(1)}, f32[1,128,256]{2,1,0:T(8,128)S(1)}, u32[]{:S(2)}, u32[]{:S(2)}) collective-permute-start(f32[1,128,256]{2,1,0:T(8,128)S(1)} %get-tuple-element.20), channel_id=1, source_target_pairs={{1,0},{2,1},{3,2},{4,3},{5,4},{6,5},{7,6},{9,8},{10,9},{11,10},{12... | collective-permute-start | bytes 393224 | tf_op jit(solution)/shard_map/ppermute | solution.py:22
  187.2 7.2 %collective-permute-start.18 = (f32[1,128,256]{2,1,0:T(8,128)S(1)}, f32[1,128,256]{2,1,0:T(8,128)S(1)}, u32[]{:S(2)}, u32[]{:S(2)}) collective-permute-start(f32[1,128,256]{2,1,0:T(8,128)S(1)} %get-tuple-element.21), channel_id=1, source_target_pairs={{0,1},{1,2},{2,3},{3,4},{4,5},{5,6},{6,7},{8,9},{9,10},{10,11},{11... | collective-permute-start | bytes 393224 | tf_op jit(solution)/shard_map/ppermute | solution.py:20
  189.6 10.6 %collective-permute-start.13 = (f32[2,128,256]{2,1,0:T(8,128)S(1)}, f32[2,128,256]{2,1,0:T(8,128)S(1)}, u32[]{:S(2)}, u32[]{:S(2)}) collective-permute-start(f32[2,128,256]{2,1,0:T(8,128)S(1)} %fusion.79), channel_id=1, source_target_pairs={{0,8},{8,16},{16,24},{1,9},{9,17},{17,25},{2,10},{10,18},{18,26},{... | collective-permute-start | bytes 786440 | tf_op jit(solution)/shard_map/ppermute | solution.py:32
  190.9 25.8 %collective-permute-start.16 = (f32[2,128,256]{2,1,0:T(8,128)S(1)}, f32[2,128,256]{2,1,0:T(8,128)S(1)}, u32[]{:S(2)}, u32[]{:S(2)}) collective-permute-start(f32[2,128,256]{2,1,0:T(8,128)S(1)} %fusion.89), channel_id=1, source_target_pairs={{0,16},{8,24},{1,17},{9,25},{2,18},{10,26},{3,19},{11,27},{4,20},{... | collective-permute-start | bytes 786440 | tf_op jit(solution)/shard_map/ppermute | solution.py:32
  194.8 22.0 %collective-permute-start.19 = (f32[2,128,256]{2,1,0:T(8,128)S(1)}, f32[2,128,256]{2,1,0:T(8,128)S(1)}, u32[]{:S(2)}, u32[]{:S(2)}) collective-permute-start(f32[2,128,256]{2,1,0:T(8,128)S(1)} %fusion.99), channel_id=1, source_target_pairs={{0,24},{1,25},{2,26},{3,27},{4,28},{5,29},{6,30},{7,31}} | collective-permute-start | bytes 786440 | tf_op jit(solution)/shard_map/ppermute | solution.py:32
  219.2 3.8 %copy-start.7 = (f32[1,4,256,512]{3,2,1,0:T(8,128)S(1)}, f32[1,4,256,512]{3,2,1,0:T(8,128)}, u32[]{:S(2)}) copy-start(f32[1,4,256,512]{3,2,1,0:T(8,128)} %param.4) | copy-start | bytes 6291460
where the time goes:
time: 227 us; the launch traced here: 226 us
  waiting for transfers between devices  102 us (45%)
  other arithmetic  54.6 us (24%)
  starting transfers between devices  44.9 us (20%)
  local copies, waits for them, and re-layouts  21.8 us (10%)
  matrix products  2.78 us (1%)
    ppermute x4, waiting for transfers between devices, shifted(): return lax.ppermute(x, axis, pairs)  61.2 us
    add x6, other arithmetic, advance(): return center + 0.5 * courant * flux  23.8 us
    ppermute x8, waiting for transfers between devices, extended(): lax.ppermute(head, axis, [((i + 1) % count, i) for i in range(ends)])  22.5 us
    ppermute x8, starting transfers between devices, extended(): lax.ppermute(head, axis, [((i + 1) % count, i) for i in range(ends)])  20.3 us
    ppermute x8, starting transfers between devices, extended(): lax.ppermute(tail, axis, [(i, (i + 1) % count) for i in range(ends)])  19.1 us
    ppermute x8, waiting for transfers between devices, extended(): lax.ppermute(tail, axis, [(i, (i + 1) % count) for i in range(ends)])  18.1 us
    sub x1, other arithmetic, local(): residual = state - iterate[0]  12.6 us
    reduce_sum x2, other arithmetic, restrict(): values.reshape(depth_z // 2, 2, depth_y // 2, 2, depth_x).sum(axis=(1, 3))  8.77 us
  transfers between devices with their start and end apart: 20, of which 13 were waited for; matrix products, arithmetic and copies ran while one was open for 10% of the time, Pallas kernels for 0%

commit v1 on v0

v1 whole, which is shorter than its diff:
```python
import functools

import jax
import jax.numpy as jnp
from jax import lax
from jax.experimental import pallas as pl
from jax.experimental.pallas import tpu as pltpu
from jax.sharding import PartitionSpec as P

STEPS = 4
courant = 0.15
GAIN = 0.5 * courant
MARGIN = 16
F32 = jnp.float32
VMEM = pltpu.VMEM


def params(limit):
    return pltpu.CompilerParams(vmem_limit_bytes=limit)


def whole(count):
    return [pl.BlockSpec(memory_space=VMEM)] * count


def shape(*dims):
    return jax.ShapeDtypeStruct(dims, F32)


def split_dot(x, selection):
    high = x.astype(jnp.bfloat16)
    rest = x - high.astype(F32)
    middle = rest.astype(jnp.bfloat16)
    low = (rest - middle.astype(F32)).astype(jnp.bfloat16)
    dot = functools.partial(jnp.dot, preferred_element_type=F32)
    return dot(high, selection) + dot(middle, selection) + dot(low, selection)


def pairing(width):
    fine = lax.broadcasted_iota(jnp.int32, (width, width // 2), 0)
    coarse = lax.broadcasted_iota(jnp.int32, (width, width // 2), 1)
    return jnp.where((fine == 2 * coarse) | (fine == 2 * coarse + 1), 1.0, 0.0).astype(jnp.bfloat16)


def spreading(width):
    coarse = lax.broadcasted_iota(jnp.int32, (width // 2, width), 0)
    fine = lax.broadcasted_iota(jnp.int32, (width // 2, width), 1)
    return jnp.where((fine == 2 * coarse) | (fine == 2 * coarse + 1), 1.0, 0.0).astype(jnp.bfloat16)


def block_mean(first, second, rows_scr, select):
    rows = first.shape[0]
    lanes = split_dot(first + second, select)
    parts = []
    for j in range(lanes.shape[1] // 128):
        rows_scr[j, 0:rows, :] = lanes[:, 128 * j : 128 * j + 128]
        even = rows_scr[j, pl.ds(0, rows // 2, 2), :]
        odd = rows_scr[j, pl.ds(1, rows // 2, 2), :]
        parts.append(0.125 * (even + odd))
    return jnp.concatenate(parts, axis=1)


def tile_masks(lanes):
    sub = lax.broadcasted_iota(jnp.int32, (8, lanes), 0)
    lane = lax.broadcasted_iota(jnp.int32, (8, lanes), 1)
    return sub, lane


def weights_plane(load, store, rows, lanes, dot_low=True):
    sub, lane = tile_masks(lanes)
    tiles = rows // 8
    zero = jnp.zeros((8, lanes), F32)
    for i in range(tiles):
        c = load(0, i)
        down = load(0, i - 1) if i > 0 else zero
        up = load(0, i + 1) if i + 1 < tiles else zero
        cym = jnp.where(sub == 0, pltpu.roll(down, 1, 0), pltpu.roll(c, 1, 0))
        cyp = jnp.where(sub == 7, pltpu.roll(up, 7, 0), pltpu.roll(c, 7, 0))
        cxm = jnp.where(lane == 0, 0.0, pltpu.roll(c, 1, 1))
        cxp = jnp.where(lane == lanes - 1, 0.0, pltpu.roll(c, lanes - 1, 1))
        czm = load(-1, i)
        czp = load(1, i)
        gain = jnp.where(c > 0.0, GAIN, 0.0)
        store(0, i, 1.0 - GAIN * (6.0 * c + (cxm + cxp) + (cym + cyp) + (czm + czp)))
        wxm = gain * (c + cxm)
        wxp = gain * (c + cxp)
        wym = gain * (c + cym)
        wyp = gain * (c + cyp)
        store(1, i, jnp.where(lane == 0, 0.0, wxm))
        store(2, i, jnp.where(lane == lanes - 1, 0.0, wxp))
        store(3, i, jnp.where(sub == 0, 0.0, wym) if i == 0 else wym)
        store(4, i, jnp.where(sub == 7, 0.0, wyp) if i + 1 == tiles else wyp)
        store(5, i, gain * (c + czm))
        store(6, i, gain * (c + czp))


def step_plane(weight, load, store, rows, lanes):
    sub, _ = tile_masks(lanes)
    tiles = rows // 8
    center = load(0, 0)
    below = center
    for i in range(tiles):
        above = load(0, i + 1) if i + 1 < tiles else center
        ym = jnp.where(sub == 0, pltpu.roll(below, 1, 0), pltpu.roll(center, 1, 0))
        yp = jnp.where(sub == 7, pltpu.roll(above, 7, 0), pltpu.roll(center, 7, 0))
        xm = pltpu.roll(center, 1, 1)
        xp = pltpu.roll(center, lanes - 1, 1)
        out = weight(0, i) * center
        out = out + (weight(1, i) * xm + weight(2, i) * xp)
        out = out + (weight(3, i) * ym + weight(4, i) * yp)
        out = out + (weight(5, i) * load(-1, i) + weight(6, i) * load(1, i))
        store(i, out)
        below, center = center, above


def tile(i):
    return slice(8 * i, 8 * i + 8)


def fine_kernel(planes, flag_ref, c_ref, partner_ref, other_ref, first_ref, second_ref, own_ref, to_partner_ref, to_other_ref,
                coarse_ref, c_scr, w_scr, a_scr, b_scr, cc_scr, rows_scr, keep_scr):
    half, upper, last = flag_ref[0], flag_ref[1], flag_ref[2]
    rows, lanes = c_ref.shape[1:]
    own_rows = rows - MARGIN
    depth = 3 * planes
    select = pairing(lanes)
    at_partner = upper * (2 * planes)
    at_other = (1 - upper) * (2 * planes)
    c_scr[planes : 2 * planes] = c_ref[...]
    c_scr[pl.ds(at_partner, planes)] = partner_ref[...]
    c_scr[pl.ds(at_other, planes)] = other_ref[...]

    def weigh(z, _):
        below, above = jnp.maximum(z - 1, 0), jnp.minimum(z + 1, depth - 1)

        def load(dz, i):
            at = z if dz == 0 else (below if dz < 0 else above)
            return c_scr[at, tile(i), :]

        def store(k, i, w):
            w_scr[k, z, tile(i), :] = w

        weights_plane(load, store, rows, lanes)
        return 0

    lax.fori_loop(0, depth, weigh, 0)

    coarse_planes = depth // 2
    for q in range(coarse_planes):
        cc_scr[q] = block_mean(c_scr[2 * q], c_scr[2 * q + 1], rows_scr, select)
    coarse_rows, coarse_lanes = rows // 2, lanes // 2
    reach = planes // 2
    for q in range(reach):
        at = reach + q

        def load(dz, i):
            return cc_scr[at + dz, tile(i), :]

        def store(k, i, w):
            coarse_ref[k, q, tile(i), :] = w

        weights_plane(load, store, coarse_rows, coarse_lanes)

    for field, source in enumerate((first_ref, second_ref)):
        zeros = jnp.zeros((planes, rows, lanes), F32)
        a_scr[0:planes] = zeros
        a_scr[2 * planes :] = zeros
        b_scr[0 : planes - 1] = zeros[1:]
        b_scr[2 * planes + 1 :] = zeros[1:]
        edge = pl.multiple_of(own_rows * (1 - half), 8)
        a_scr[planes : 2 * planes, pl.ds(edge, MARGIN), :] = jnp.zeros((planes, MARGIN, lanes), F32)
        a_scr[planes : 2 * planes, pl.ds(pl.multiple_of(MARGIN * half, 8), own_rows), :] = source[...]
        kept = []
        for q in range(reach):
            kept.append(block_mean(a_scr[planes + 2 * q], a_scr[planes + 2 * q + 1], rows_scr, select))
        for number in range(STEPS):
            v_in, v_out = (a_scr, b_scr) if number % 2 == 0 else (b_scr, a_scr)

            def advance(z, _):
                below, above = jnp.maximum(z - 1, 0), jnp.minimum(z + 1, depth - 1)

                def load(dz, i):
                    at = z if dz == 0 else (below if dz < 0 else above)
                    return v_in[at, tile(i), :]

                def weight(k, i):
                    return w_scr[k, z, tile(i), :]

                def store(i, v):
                    v_out[z, tile(i), :] = v

                step_plane(weight, load, store, rows, lanes)
                return 0

            lax.fori_loop(planes - 1 - number, 2 * planes + 1 + number, advance, 0)
        result = a_scr if STEPS % 2 == 0 else b_scr
        means = [block_mean(result[2 * q], result[2 * q + 1], rows_scr, select) for q in range(coarse_planes)]

        scale = 1.0 if field == 1 else jnp.where(last == 1, 0.0, 1.0).astype(F32)
        zero = jnp.zeros((8, coarse_lanes), F32)
        for q in range(reach):
            keep_scr[q] = kept[q] * scale
        for q in range(reach):
            def load(dz, i):
                at = q + dz
                if at < 0 or at >= reach:
                    return zero
                return keep_scr[at, tile(i), :]

            def weight(k, i):
                return coarse_ref[k, q, tile(i), :]

            def store(i, v):
                own_ref[field, q, tile(i), :] = means[reach + q][8 * i : 8 * i + 8] - v

            step_plane(weight, load, store, coarse_rows, coarse_lanes)
        low_c, high_c = cc_scr[reach - 1], cc_scr[2 * reach]
        low_w = jnp.where(low_c > 0.0, GAIN * (low_c + cc_scr[reach]), 0.0)
        high_w = jnp.where(high_c > 0.0, GAIN * (high_c + cc_scr[2 * reach - 1]), 0.0)
        low = means[:reach]
        high = means[2 * reach :]
        low[-1] = low[-1] - low_w * keep_scr[0]
        high[0] = high[0] - high_w * keep_scr[reach - 1]

        @pl.when(upper == 1)
        def _():
            for q in range(reach):
                to_partner_ref[field, q] = high[q]
                to_other_ref[field, q] = low[q]

        @pl.when(upper == 0)
        def _():
            for q in range(reach):
                to_partner_ref[field, q] = low[q]
                to_other_ref[field, q] = high[q]


def edges(flag_ref, val, to_partner_ref, to_other_ref):
    upper = flag_ref[1]

    @pl.when(upper == 1)
    def _():
        to_partner_ref[0] = val[-1]
        to_other_ref[0] = val[0]

    @pl.when(upper == 0)
    def _():
        to_partner_ref[0] = val[0]
        to_other_ref[0] = val[-1]


def sum_kernel(flag_ref, own_ref, partner_ref, other_ref, val_ref, extra_ref, to_partner_ref, to_other_ref):
    val = own_ref[0] + partner_ref[0] + other_ref[0]
    val_ref[...] = val
    extra_ref[...] = own_ref[1] + partner_ref[1] + other_ref[1]
    edges(flag_ref, val, to_partner_ref, to_other_ref)


def chain_kernel(slot, flag_ref, weight_ref, val_ref, partner_ref, other_ref, extra_ref, next_ref, to_partner_ref, to_other_ref,
                 wide):
    upper = flag_ref[1]
    add = flag_ref[slot].astype(F32)
    planes, rows, lanes = val_ref.shape
    wide[1 : planes + 1] = val_ref[...]
    wide[upper * (planes + 1)] = partner_ref[0]
    wide[(1 - upper) * (planes + 1)] = other_ref[0]
    for q in range(planes):
        def load(dz, i):
            return wide[1 + q + dz, tile(i), :]

        def weight(k, i):
            return weight_ref[k, q, tile(i), :]

        def store(i, v):
            next_ref[q, tile(i), :] = v + add * extra_ref[q, tile(i), :]

        step_plane(weight, load, store, rows, lanes)
    edges(flag_ref, next_ref[...], to_partner_ref, to_other_ref)


def final_kernel(parts, overlap, iterate_ref, *refs):
    pieces, out_ref, rows_scr, fine_scr = refs[: 2 * parts], refs[2 * parts], refs[2 * parts + 1], refs[2 * parts + 2]
    planes, rows, lanes = iterate_ref.shape
    select, spread = pairing(lanes), spreading(lanes)
    own = rows // 4
    for q in range(planes // 2):
        low = sum(ref[q] for ref in pieces[1:parts]) + pieces[0][q]
        high = sum(ref[q] for ref in pieces[parts + 1 :]) + pieces[parts][q]
        both = low[own - overlap :] + high[: 2 * overlap]
        error = jnp.concatenate([low[: own - overlap], both, high[2 * overlap :]], axis=0)
        error = error - block_mean(iterate_ref[2 * q], iterate_ref[2 * q + 1], rows_scr, select)
        wide = split_dot(error, spread)
        for j in range(lanes // 128):
            column = slice(128 * j, 128 * j + 128)
            fine_scr[j, pl.ds(0, rows // 2, 2), :] = wide[:, column]
            fine_scr[j, pl.ds(1, rows // 2, 2), :] = wide[:, column]
            for part in range(2):
                out_ref[2 * q + part, :, column] = iterate_ref[2 * q + part, :, column] + fine_scr[j]


def swap_pairs(count, first):
    pairs = []
    for i in range(first, count - 1, 2):
        pairs += [(i, i + 1), (i + 1, i)]
    return pairs


def local(initial, iterate, diffusivity):
    layers, slabs = lax.axis_size("tm"), lax.axis_size("space")
    t, s = lax.axis_index("tm"), lax.axis_index("space")
    planes, all_rows, lanes = initial.shape
    assert layers % 2 == 0 and slabs % 2 == 0 and planes == STEPS
    half, group, last_group = t % 2, t // 2, layers // 2 - 1
    last = group == last_group
    own_rows = all_rows // 2
    rows = own_rows + MARGIN
    coarse_rows = rows // 2
    reach = planes // 2
    coarse_lanes = lanes // 2
    upper = 1 - s % 2

    def partner_swap(x):
        return lax.ppermute(x, "space", swap_pairs(slabs, 0))

    def other_swap(x):
        return lax.ppermute(x, "space", swap_pairs(slabs, 1))

    c = lax.dynamic_slice_in_dim(diffusivity, half * (all_rows - rows), rows, axis=1)
    c_other = other_swap(c)
    c_partner = partner_swap(c)
    to_row_partner = lax.dynamic_slice_in_dim(iterate[0], (1 - half) * own_rows, own_rows, axis=1)
    row_pairs = swap_pairs(layers, 0)
    row_pairs.remove((layers - 1, layers - 2))
    received = lax.ppermute(to_row_partner, "tm", row_pairs)
    kept = lax.dynamic_slice_in_dim(iterate[0], half * own_rows, own_rows, axis=1)
    start = lax.dynamic_slice_in_dim(initial, half * own_rows, own_rows, axis=1)
    first = jnp.where(last, start, jnp.where(half == 0, kept, received))
    second = jnp.where(last == (half == 0), kept, received)

    flags = [half, upper, last.astype(jnp.int32)]
    for number in range(1, layers):
        flags.append(jnp.where(last, number == layers - 1, number == 1).astype(jnp.int32))
    flags = jnp.stack([f.astype(jnp.int32) for f in flags])
    smem = pl.BlockSpec(memory_space=pltpu.SMEM)

    fields = shape(2, reach, coarse_rows, coarse_lanes)
    own, to_partner, to_other, weights = pl.pallas_call(
        functools.partial(fine_kernel, planes),
        out_shape=(fields, fields, fields, shape(7, reach, coarse_rows, coarse_lanes)),
        in_specs=[smem] + whole(5),
        out_specs=tuple(whole(4)),
        scratch_shapes=[
            VMEM((3 * planes, rows, lanes), F32),
            VMEM((7, 3 * planes, rows, lanes), F32),
            VMEM((3 * planes, rows, lanes), F32),
            VMEM((3 * planes, rows, lanes), F32),
            VMEM((3 * reach, coarse_rows, coarse_lanes), F32),
            VMEM((coarse_lanes // 128, rows, 128), F32),
            VMEM((reach, coarse_rows, coarse_lanes), F32),
        ],
        compiler_params=params(60 * 1024 * 1024),
        name="fine",
    )(flags, c, c_partner, c_other, first, second)

    from_other = other_swap(to_other)
    from_partner = partner_swap(to_partner)
    plane = shape(1, coarse_rows, coarse_lanes)
    block = shape(reach, coarse_rows, coarse_lanes)
    val, extra, to_partner, to_other = pl.pallas_call(
        sum_kernel,
        out_shape=(block, block, plane, plane),
        in_specs=[smem] + whole(3),
        out_specs=tuple(whole(4)),
        name="gather",
    )(flags, own, from_partner, from_other)

    low, high = [], []

    def deliver(val, number):
        for side, into in ((0, low), (1, high)):
            pairs = [(2 * last_group + side, number)]
            for p in range(last_group):
                if 2 * p + 1 + number < layers:
                    pairs.append((2 * p + side, 2 * p + 1 + number))
            into.append(lax.ppermute(val, "tm", pairs))

    deliver(val, 0)
    for number in range(1, layers):
        from_other = other_swap(to_other)
        from_partner = partner_swap(to_partner)
        val, to_partner, to_other = pl.pallas_call(
            functools.partial(chain_kernel, 2 + number),
            out_shape=(block, plane, plane),
            in_specs=[smem] + whole(5),
            out_specs=tuple(whole(3)),
            scratch_shapes=[VMEM((reach + 2, coarse_rows, coarse_lanes), F32)],
            name=f"chain{number}",
        )(flags, weights, val, from_partner, from_other, extra)
        deliver(val, number)

    corrected = pl.pallas_call(
        functools.partial(final_kernel, layers, MARGIN // 2),
        out_shape=shape(planes, all_rows, lanes),
        in_specs=whole(1 + 2 * layers),
        out_specs=pl.BlockSpec(memory_space=VMEM),
        scratch_shapes=[VMEM((coarse_lanes // 128, all_rows, 128), F32), VMEM((lanes // 128, all_rows, 128), F32)],
        compiler_params=params(40 * 1024 * 1024),
        name="final",
    )(iterate[0], *low, *high)
    return corrected[None]


def solution(mesh):
    placed = (P("space", None, None), P("tm", "space", None, None), P("space", None, None))
    return jax.shard_map(
        local, mesh=mesh, in_specs=placed, out_specs=P("tm", "space", None, None), check_vma=False
    )
```

time: 227 us -> 134 us (0.59)
  waiting for transfers between devices: 102 us -> 46.2 us
  other arithmetic: 54.6 us -> 3.58 us
  Pallas kernels: 0 us -> 43.3 us
  local copies, waits for them, and re-layouts: 21.8 us -> 7.31 us
  starting transfers between devices: 44.9 us -> 31.8 us
  matrix products: 2.78 us -> 0 us
    ppermute x20 -> x19, waiting for transfers between devices: 102 us -> 46.2 us  [the longest x1 21.5 us: local(): received = lax.ppermute(to_row_partner, 'tm', row_pairs)]
    pallas_call x0 -> x6, Pallas kernels: none -> 43.3 us  [the longest x1 31.4 us: local(): pl.pallas_call(functools.partial(fine_kernel, planes), out_shape=(fields,...]
    add x7 -> x0, other arithmetic: 27.2 us -> none  [the longest x6 23.8 us: advance(): return center + 0.5 * courant * flux]
    ppermute x20 -> x19, starting transfers between devices: 44.9 us -> 31.8 us  [the longest x5 15.5 us: other_swap(): return lax.ppermute(x, 'space', swap_pairs(slabs, 1))]
    sub x1 -> x0, other arithmetic: 12.6 us -> none  [local(): residual = state - iterate[0]]
    reshape x3 -> x0, local copies, waits for them, and re-layouts: 12.1 us -> none  [the longest x2 8.3 us: restrict(): values.reshape(depth_z // 2, 2, depth_y // 2, 2, depth_x).sum(axis=(1, 3))]
    reduce_sum x2 -> x0, other arithmetic: 8.77 us -> none  [restrict(): values.reshape(depth_z // 2, 2, depth_y // 2, 2, depth_x).sum(axis=(1, 3))]
    slice x9 -> x0, local copies, waits for them, and re-layouts: 6.54 us -> none  [the longest x7 3.48 us: extended(): head = lax.slice_in_dim(cells, 0, width, axis=dim)]
  transfers between devices with their start and end apart: 20 -> 19, of which waited for: 13 -> 7; matrix products, arithmetic and copies ran while one was open for 10% -> 3% of each run, Pallas kernels for 0% -> 3%
where the time goes in v1:
time: 134 us; the launch traced here: 132 us
  waiting for transfers between devices  46.2 us (34%)
  Pallas kernels  43.3 us (32%)
  starting transfers between devices  31.8 us (24%)
  local copies, waits for them, and re-layouts  7.31 us (5%)
  other arithmetic  3.58 us (3%)
    pallas_call x1, Pallas kernels, local(): pl.pallas_call(functools.partial(fine_kernel, planes), out_shape=(fields,...  31.4 us
    ppermute x1, waiting for transfers between devices, local(): received = lax.ppermute(to_row_partner, 'tm', row_pairs)  21.5 us
    ppermute x5, waiting for transfers between devices, other_swap(): return lax.ppermute(x, 'space', swap_pairs(slabs, 1))  16.5 us
    ppermute x5, starting transfers between devices, other_swap(): return lax.ppermute(x, 'space', swap_pairs(slabs, 1))  15.5 us
    ppermute x8, starting transfers between devices, deliver(): into.append(lax.ppermute(val, 'tm', pairs))  14.2 us
    ppermute x8, waiting for transfers between devices, deliver(): into.append(lax.ppermute(val, 'tm', pairs))  8.25 us
    pallas_call x3, Pallas kernels, local(): pl.pallas_call(functools.partial(chain_kernel, 2 + number), out_shape=(bl...  6.74 us
    unnamed x22, local copies, waits for them, and re-layouts  4.18 us
  transfers between devices with their start and end apart: 19, of which 7 were waited for; matrix products, arithmetic and copies ran while one was open for 3% of the time, Pallas kernels for 3%

profile of v1, /device:TPU:28, one launch (start us, length us, event | category | flops | bytes accessed | tf_op | source)
XLA Modules:
  0.0 132.5 jit_solution(12916816964126161103)
XLA Ops:
  0.0 0.0 copy-start
  0.0 2.4 %dynamic-slice_bitcast_fusion = f32[4,128,512]{2,1,0:T(8,128)} fusion(f32[1,4,256,512]{3,2,1,0:T(8,128)} %param.4, s32[]{:T(128)S(6)} %select_n.59), kind=kLoop, calls=%fused_computation.3 | loop fusion | bytes 2097156 | tf_op jit(solution)/shard_map/dynamic_slice | solution.py:331
  2.4 1.3 collective-permute-start.2
  3.7 0.0 copy-done
  3.7 0.1 constant_dynamic-slice_fusion.c_ref
  3.8 0.0 copy-start.2
  3.8 2.8 %collective-permute-start.1 = (f32[4,144,512]{2,1,0:T(8,128)S(1)}, f32[4,144,512]{2,1,0:T(8,128)}, u32[]{:S(2)}, u32[]{:S(2)}) collective-permute-start(f32[4,144,512]{2,1,0:T(8,128)S(1)} %constant_dynamic-slice_fusion.c_ref), channel_id=1, source_target_pairs={{1,2},{2,1},{3,4},{4,3},{5,6},{6,5},{9,10},{10,9},{11,12},{12,11},... | collective-permute-start | bytes 3538952 | tf_op jit(solution)/shard_map/ppermute | solution.py:326
  6.6 0.8 collective-permute-start
  7.4 0.6 stack.29.flag_ref
  8.1 21.5 %collective-permute-done.2 = f32[4,128,512]{2,1,0:T(8,128)} collective-permute-done((f32[4,128,512]{2,1,0:T(8,128)}, f32[4,128,512]{2,1,0:T(8,128)}, u32[]{:S(2)}, u32[]{:S(2)}) %collective-permute-start.2) | collective-permute-done | bytes 1048608 | tf_op jit(solution)/shard_map/ppermute | solution.py:334
  29.5 3.6 %bitcast_select_fusion = (f32[4,128,512]{2,1,0:T(8,128)}, f32[4,128,512]{2,1,0:T(8,128)}) fusion(f32[4,128,512]{2,1,0:T(8,128)} %collective-permute-done.2, f32[1,4,256,512]{3,2,1,0:T(8,128)} %param.4, s32[]{:T(128)S(6)} %select_n.57, pred[]{:T(512)S(6)} %eq.15, pred[]{:T(512)S(6)} %eq.14, f32[4,256,512]{2,1,0:T(8,128)} %param.3, pred[]{:T(512)S(6)} %eq.13), kind=kLoop, calls=%fused_computation | loop fusion | flops 786432 | bytes 5242887 | tf_op jit(solution)/shard_map/jit(_where)/select_n | solution.py:338
  33.1 0.0 copy-done.2
  33.1 1.0 collective-permute-done.1.other_ref
  34.1 0.0 collective-permute-done.partner_ref
  34.1 31.4 %fine.1 = (f32[2,2,72,256]{3,2,1,0:T(8,128)}, f32[2,2,72,256]{3,2,1,0:T(8,128)}, f32[2,2,72,256]{3,2,1,0:T(8,128)}, f32[7,2,72,256]{3,2,1,0:T(8,128)}) custom-call(s32[6]{0:T(128)} %stack.29.flag_ref, f32[4,144,512]{2,1,0:T(8,128)} %copy-done.2, f32[4,144,512]{2,1,0:T(8,128)} %collective-permute-done.partner_ref, ...), custom_call_target="tpu_custom_call" | custom-call | tf_op jit(solution)/shard_map/fine/pallas_call | solution.py:347
  65.5 0.0 collective-permute-start.3
  65.5 3.6 %collective-permute-start.4 = (f32[2,2,72,256]{3,2,1,0:T(8,128)}, f32[2,2,72,256]{3,2,1,0:T(8,128)S(1)}, u32[]{:S(2)}, u32[]{:S(2)}) collective-permute-start(f32[2,2,72,256]{3,2,1,0:T(8,128)} %get-tuple-element.22), channel_id=1, source_target_pairs={{1,2},{2,1},{3,4},{4,3},{5,6},{6,5},{9,10},{10,9},{11,12},{12,11},... | collective-permute-start | bytes 884744 | tf_op jit(solution)/shard_map/ppermute | solution.py:326
  69.2 0.0 collective-permute-done.3.partner_ref
  69.2 0.0 copy-start.3
  69.2 8.4 %collective-permute-done.4.other_ref = f32[2,2,72,256]{3,2,1,0:T(8,128)S(1)} collective-permute-done((f32[2,2,72,256]{3,2,1,0:T(8,128)}, f32[2,2,72,256]{3,2,1,0:T(8,128)S(1)}, u32[]{:S(2)}, u32[]{:S(2)}) %collective-permute-start.4) | collective-permute-done | bytes 294944 | tf_op jit(solution)/shard_map/ppermute | solution.py:326
  77.6 0.0 copy-done.3
  77.6 0.7 copy-done.4
  78.4 2.0 %gather.1 = (f32[2,72,256]{2,1,0:T(8,128)}, f32[2,72,256]{2,1,0:T(8,128)}, f32[1,72,256]{2,1,0:T(8,128)}, f32[1,72,256]{2,1,0:T(8,128)}) custom-call(s32[6]{0:T(128)} %stack.29.flag_ref, f32[2,2,72,256]{3,2,1,0:T(8,128)} %get-tuple-element.20.own_ref, f32[2,2,72,256]{3,2,1,0:T(8,128)} %copy-done.3, f32[2,2,72,256]{3,2,1,0:T(8,128)} %copy-done.4), custom_call_target="tpu_custom_call" | custom-call | tf_op jit(solution)/shard_map/gather/pallas_call | solution.py:369
  80.3 0.0 collective-permute-start.6
  80.3 3.0 %collective-permute-start.7 = (f32[1,72,256]{2,1,0:T(8,128)}, f32[1,72,256]{2,1,0:T(8,128)S(1)}, u32[]{:S(2)}, u32[]{:S(2)}) collective-permute-start(f32[1,72,256]{2,1,0:T(8,128)} %get-tuple-element.26), channel_id=1, source_target_pairs={{1,2},{2,1},{3,4},{4,3},{5,6},{6,5},{9,10},{10,9},{11,12},{12,11},... | collective-permute-start | bytes 221192 | tf_op jit(solution)/shard_map/ppermute | solution.py:326
  83.3 0.0 collective-permute-done.6.partner_ref
  83.3 0.0 copy-start.9
  83.3 3.8 %collective-permute-done.7.other_ref = f32[1,72,256]{2,1,0:T(8,128)S(1)} collective-permute-done((f32[1,72,256]{2,1,0:T(8,128)}, f32[1,72,256]{2,1,0:T(8,128)S(1)}, u32[]{:S(2)}, u32[]{:S(2)}) %collective-permute-start.7) | collective-permute-done | bytes 73760 | tf_op jit(solution)/shard_map/ppermute | solution.py:326
  87.1 0.0 copy-done.9
  87.1 0.6 copy-done.10
  87.7 2.2 %chain1.1 = (f32[2,72,256]{2,1,0:T(8,128)}, f32[1,72,256]{2,1,0:T(8,128)}, f32[1,72,256]{2,1,0:T(8,128)}) custom-call(s32[6]{0:T(128)} %stack.29.flag_ref, f32[7,2,72,256]{3,2,1,0:T(8,128)} %get-tuple-element.24.weight_ref, f32[2,72,256]{2,1,0:T(8,128)} %get-tuple-element.23.val_ref, f32[1,72,256]{2,1,0:T(8,128)} %copy-done.9, f32[1,72,256]{2,1,0:T(8,128)} %copy-done.10, ...), custom_call_target="tpu_custom_call" | custom-call | tf_op jit(solution)/shard_map/chain1/pallas_call | solution.py:391
  90.0 0.0 collective-permute-start.9
  90.0 3.0 %collective-permute-start.10 = (f32[1,72,256]{2,1,0:T(8,128)}, f32[1,72,256]{2,1,0:T(8,128)S(1)}, u32[]{:S(2)}, u32[]{:S(2)}) collective-permute-start(f32[1,72,256]{2,1,0:T(8,128)} %get-tuple-element.30), channel_id=1, source_target_pairs={{1,2},{2,1},{3,4},{4,3},{5,6},{6,5},{9,10},{10,9},{11,12},{12,11},... | collective-permute-start | bytes 221192 | tf_op jit(solution)/shard_map/ppermute | solution.py:326
  93.0 4.0 %collective-permute-start.15 = (f32[2,72,256]{2,1,0:T(8,128)}, f32[2,72,256]{2,1,0:T(8,128)S(1)}, u32[]{:S(2)}, u32[]{:S(2)}) collective-permute-start(f32[2,72,256]{2,1,0:T(8,128)} %get-tuple-element.23.val_ref), channel_id=1, source_target_pairs={{24,0},{8,8},{25,1},{9,9},{26,2},{10,10},{27,3},{11,11},{28,4},{12... | collective-permute-start | bytes 442376 | tf_op jit(solution)/shard_map/ppermute | solution.py:385
  97.0 0.7 collective-permute-start.5
  97.7 1.3 collective-permute-start.16
  99.0 0.0 collective-permute-done.9.partner_ref
  99.0 0.0 copy-start.5
  99.0 0.0 collective-permute-done.10.other_ref
  99.0 0.6 copy-done.5
  99.6 0.6 copy-done.7
  100.2 2.3 %chain2.1 = (f32[2,72,256]{2,1,0:T(8,128)}, f32[1,72,256]{2,1,0:T(8,128)}, f32[1,72,256]{2,1,0:T(8,128)}) custom-call(s32[6]{0:T(128)} %stack.29.flag_ref, f32[7,2,72,256]{3,2,1,0:T(8,128)} %get-tuple-element.24.weight_ref, f32[2,72,256]{2,1,0:T(8,128)} %get-tuple-element.28.val_ref, f32[1,72,256]{2,1,0:T(8,128)} %copy-done.5, f32[1,72,256]{2,1,0:T(8,128)} %copy-done.7, ...), custom_call_target="tpu_custom_call" | custom-call | tf_op jit(solution)/shard_map/chain2/pallas_call | solution.py:391
  102.5 0.0 collective-permute-start.12
  102.5 3.1 %collective-permute-start.13 = (f32[1,72,256]{2,1,0:T(8,128)}, f32[1,72,256]{2,1,0:T(8,128)S(1)}, u32[]{:S(2)}, u32[]{:S(2)}) collective-permute-start(f32[1,72,256]{2,1,0:T(8,128)} %get-tuple-element.33), channel_id=1, source_target_pairs={{1,2},{2,1},{3,4},{4,3},{5,6},{6,5},{9,10},{10,9},{11,12},{12,11},... | collective-permute-start | bytes 221192 | tf_op jit(solution)/shard_map/ppermute | solution.py:326
  105.6 0.0 collective-permute-done.12.partner_ref
  105.6 0.0 copy-start.6
  105.6 0.7 collective-permute-start.8
  106.3 3.3 %collective-permute-done.13.other_ref = f32[1,72,256]{2,1,0:T(8,128)S(1)} collective-permute-done((f32[1,72,256]{2,1,0:T(8,128)}, f32[1,72,256]{2,1,0:T(8,128)S(1)}, u32[]{:S(2)}, u32[]{:S(2)}) %collective-permute-start.13) | collective-permute-done | bytes 73760 | tf_op jit(solution)/shard_map/ppermute | solution.py:326
  109.6 3.4 %collective-permute-start.17 = (f32[2,72,256]{2,1,0:T(8,128)}, f32[2,72,256]{2,1,0:T(8,128)S(1)}, u32[]{:S(2)}, u32[]{:S(2)}) collective-permute-start(f32[2,72,256]{2,1,0:T(8,128)} %get-tuple-element.31.val_ref), channel_id=1, source_target_pairs={{24,16},{8,24},{25,17},{9,25},{26,18},{10,26},{27,19},{11,27},{28,... | collective-permute-start | bytes 442376 | tf_op jit(solution)/shard_map/ppermute | solution.py:385
  113.0 0.0 copy-done.6
  113.1 2.3 %chain3.1 = (f32[2,72,256]{2,1,0:T(8,128)}, f32[1,72,256]{2,1,0:T(8,128)}, f32[1,72,256]{2,1,0:T(8,128)}) custom-call(s32[6]{0:T(128)} %stack.29.flag_ref, f32[7,2,72,256]{3,2,1,0:T(8,128)} %get-tuple-element.24.weight_ref, f32[2,72,256]{2,1,0:T(8,128)} %get-tuple-element.31.val_ref, f32[1,72,256]{2,1,0:T(8,128)} %copy-done.6, f32[1,72,256]{2,1,0:T(8,128)} %copy-done.8, ...), custom_call_target="tpu_custom_call" | custom-call | tf_op jit(solution)/shard_map/chain3/pallas_call | solution.py:391
  115.3 0.0 collective-permute-done.15.refs_4_
  115.3 1.3 collective-permute-start.11
  116.6 0.0 collective-permute-done.5.refs_0_
  116.6 1.6 %collective-permute-start.18 = (f32[2,72,256]{2,1,0:T(8,128)}, f32[2,72,256]{2,1,0:T(8,128)S(1)}, u32[]{:S(2)}, u32[]{:S(2)}) collective-permute-start(f32[2,72,256]{2,1,0:T(8,128)} %get-tuple-element.34), channel_id=1, source_target_pairs={{24,24},{25,25},{26,26},{27,27},{28,28},{29,29},{30,30},{31,31}} | collective-permute-start | bytes 442376 | tf_op jit(solution)/shard_map/ppermute | solution.py:385
  118.2 0.0 collective-permute-done.16.refs_5_
  118.2 1.3 collective-permute-start.14
  119.5 0.0 collective-permute-done.8.refs_1_
  119.5 0.0 collective-permute-done.17.refs_6_
  119.5 5.2 %collective-permute-done.11.refs_2_ = f32[2,72,256]{2,1,0:T(8,128)S(1)} collective-permute-done((f32[2,72,256]{2,1,0:T(8,128)}, f32[2,72,256]{2,1,0:T(8,128)S(1)}, u32[]{:S(2)}, u32[]{:S(2)}) %collective-permute-start.11) | collective-permute-done | bytes 147488 | tf_op jit(solution)/shard_map/ppermute | solution.py:385
  124.7 0.0 collective-permute-done.18.refs_7_
  124.7 3.1 %collective-permute-done.14.refs_3_ = f32[2,72,256]{2,1,0:T(8,128)S(1)} collective-permute-done((f32[2,72,256]{2,1,0:T(8,128)}, f32[2,72,256]{2,1,0:T(8,128)S(1)}, u32[]{:S(2)}, u32[]{:S(2)}) %collective-permute-start.14) | collective-permute-done | bytes 147488 | tf_op jit(solution)/shard_map/ppermute | solution.py:385
  127.7 1.6 %copy-done.1 = f32[1,4,256,512]{3,2,1,0:T(8,128)S(1)} copy-done((f32[1,4,256,512]{3,2,1,0:T(8,128)S(1)}, f32[1,4,256,512]{3,2,1,0:T(8,128)}, u32[]{:S(2)}) %copy-start.1) | copy-done | bytes 2097176
  129.3 3.2 %final.1 = f32[4,256,512]{2,1,0:T(8,128)} custom-call(f32[4,256,512]{2,1,0:T(8,128)S(1)} %bitcast.13, f32[2,72,256]{2,1,0:T(8,128)S(1)} %collective-permute-done.5.refs_0_, f32[2,72,256]{2,1,0:T(8,128)S(1)} %collective-permute-done.8.refs_1_, f32[2,72,256]{2,1,0:T(8,128)S(1)} %collective-permute-done.11.refs_2_, ...), custom_call_target="tpu_custom_call" | custom-call | tf_op jit(solution)/shard_map/final/pallas_call | solution.py:401
  (6 shorter events, 0.0 us)
Async XLA Ops:
  0.0 3.7 %copy-start = (f32[4,256,512]{2,1,0:T(8,128)S(1)}, f32[4,256,512]{2,1,0:T(8,128)}, u32[]{:S(2)}) copy-start(f32[4,256,512]{2,1,0:T(8,128)} %param.5) | copy-start | bytes 6291460
  2.4 27.1 %collective-permute-start.2 = (f32[4,128,512]{2,1,0:T(8,128)}, f32[4,128,512]{2,1,0:T(8,128)}, u32[]{:S(2)}, u32[]{:S(2)}) collective-permute-start(f32[4,128,512]{2,1,0:T(8,128)} %dynamic-slice_bitcast_fusion), channel_id=1, source_target_pairs={{0,8},{8,0},{16,24},{1,9},{9,1},{17,25},{2,10},{10,2},{18,26},{3,1... | collective-permute-start | bytes 3145736 | tf_op jit(solution)/shard_map/ppermute | solution.py:334
  3.8 29.3 %copy-start.2 = (f32[4,144,512]{2,1,0:T(8,128)}, f32[4,144,512]{2,1,0:T(8,128)S(1)}, u32[]{:S(2)}) copy-start(f32[4,144,512]{2,1,0:T(8,128)S(1)} %constant_dynamic-slice_fusion.c_ref) | copy-start | bytes 3538948
  3.8 30.3 %collective-permute-start.1 = (f32[4,144,512]{2,1,0:T(8,128)S(1)}, f32[4,144,512]{2,1,0:T(8,128)}, u32[]{:S(2)}, u32[]{:S(2)}) collective-permute-start(f32[4,144,512]{2,1,0:T(8,128)S(1)} %constant_dynamic-slice_fusion.c_ref), channel_id=1, source_target_pairs={{1,2},{2,1},{3,4},{4,3},{5,6},{6,5},{9,10},{10,9},{11,12},{12,11},... | collective-permute-start | bytes 3538952 | tf_op jit(solution)/shard_map/ppermute | solution.py:326
  6.6 27.5 %collective-permute-start = (f32[4,144,512]{2,1,0:T(8,128)S(1)}, f32[4,144,512]{2,1,0:T(8,128)}, u32[]{:S(2)}, u32[]{:S(2)}) collective-permute-start(f32[4,144,512]{2,1,0:T(8,128)S(1)} %constant_dynamic-slice_fusion.c_ref), channel_id=1, source_target_pairs={{0,1},{1,0},{2,3},{3,2},{4,5},{5,4},{6,7},{7,6},{8,9},{9,8},{10,11... | collective-permute-start | bytes 3538952 | tf_op jit(solution)/shard_map/ppermute | solution.py:323
  65.5 3.7 %collective-permute-start.3 = (f32[2,2,72,256]{3,2,1,0:T(8,128)}, f32[2,2,72,256]{3,2,1,0:T(8,128)S(1)}, u32[]{:S(2)}, u32[]{:S(2)}) collective-permute-start(f32[2,2,72,256]{3,2,1,0:T(8,128)} %get-tuple-element.21), channel_id=1, source_target_pairs={{0,1},{1,0},{2,3},{3,2},{4,5},{5,4},{6,7},{7,6},{8,9},{9,8},{10,11... | collective-permute-start | bytes 884744 | tf_op jit(solution)/shard_map/ppermute | solution.py:323
  65.5 12.1 %collective-permute-start.4 = (f32[2,2,72,256]{3,2,1,0:T(8,128)}, f32[2,2,72,256]{3,2,1,0:T(8,128)S(1)}, u32[]{:S(2)}, u32[]{:S(2)}) collective-permute-start(f32[2,2,72,256]{3,2,1,0:T(8,128)} %get-tuple-element.22), channel_id=1, source_target_pairs={{1,2},{2,1},{3,4},{4,3},{5,6},{6,5},{9,10},{10,9},{11,12},{12,11},... | collective-permute-start | bytes 884744 | tf_op jit(solution)/shard_map/ppermute | solution.py:326
  69.2 8.4 %copy-start.3 = (f32[2,2,72,256]{3,2,1,0:T(8,128)}, f32[2,2,72,256]{3,2,1,0:T(8,128)S(1)}, u32[]{:S(2)}) copy-start(f32[2,2,72,256]{3,2,1,0:T(8,128)S(1)} %collective-permute-done.3.partner_ref) | copy-start | bytes 884740
  77.6 0.7 copy-start.4
  80.3 3.0 %collective-permute-start.6 = (f32[1,72,256]{2,1,0:T(8,128)}, f32[1,72,256]{2,1,0:T(8,128)S(1)}, u32[]{:S(2)}, u32[]{:S(2)}) collective-permute-start(f32[1,72,256]{2,1,0:T(8,128)} %get-tuple-element.25), channel_id=1, source_target_pairs={{0,1},{1,0},{2,3},{3,2},{4,5},{5,4},{6,7},{7,6},{8,9},{9,8},{10,11... | collective-permute-start | bytes 221192 | tf_op jit(solution)/shard_map/ppermute | solution.py:323
  80.3 6.8 %collective-permute-start.7 = (f32[1,72,256]{2,1,0:T(8,128)}, f32[1,72,256]{2,1,0:T(8,128)S(1)}, u32[]{:S(2)}, u32[]{:S(2)}) collective-permute-start(f32[1,72,256]{2,1,0:T(8,128)} %get-tuple-element.26), channel_id=1, source_target_pairs={{1,2},{2,1},{3,4},{4,3},{5,6},{6,5},{9,10},{10,9},{11,12},{12,11},... | collective-permute-start | bytes 221192 | tf_op jit(solution)/shard_map/ppermute | solution.py:326
  83.3 3.8 %copy-start.9 = (f32[1,72,256]{2,1,0:T(8,128)}, f32[1,72,256]{2,1,0:T(8,128)S(1)}, u32[]{:S(2)}) copy-start(f32[1,72,256]{2,1,0:T(8,128)S(1)} %collective-permute-done.6.partner_ref) | copy-start | bytes 221188
  87.1 0.6 copy-start.10
  90.0 9.0 %collective-permute-start.9 = (f32[1,72,256]{2,1,0:T(8,128)}, f32[1,72,256]{2,1,0:T(8,128)S(1)}, u32[]{:S(2)}, u32[]{:S(2)}) collective-permute-start(f32[1,72,256]{2,1,0:T(8,128)} %get-tuple-element.29), channel_id=1, source_target_pairs={{0,1},{1,0},{2,3},{3,2},{4,5},{5,4},{6,7},{7,6},{8,9},{9,8},{10,11... | collective-permute-start | bytes 221192 | tf_op jit(solution)/shard_map/ppermute | solution.py:323
  90.0 9.0 %collective-permute-start.10 = (f32[1,72,256]{2,1,0:T(8,128)}, f32[1,72,256]{2,1,0:T(8,128)S(1)}, u32[]{:S(2)}, u32[]{:S(2)}) collective-permute-start(f32[1,72,256]{2,1,0:T(8,128)} %get-tuple-element.30), channel_id=1, source_target_pairs={{1,2},{2,1},{3,4},{4,3},{5,6},{6,5},{9,10},{10,9},{11,12},{12,11},... | collective-permute-start | bytes 221192 | tf_op jit(solution)/shard_map/ppermute | solution.py:326
  93.0 22.3 %collective-permute-start.15 = (f32[2,72,256]{2,1,0:T(8,128)}, f32[2,72,256]{2,1,0:T(8,128)S(1)}, u32[]{:S(2)}, u32[]{:S(2)}) collective-permute-start(f32[2,72,256]{2,1,0:T(8,128)} %get-tuple-element.23.val_ref), channel_id=1, source_target_pairs={{24,0},{8,8},{25,1},{9,9},{26,2},{10,10},{27,3},{11,11},{28,4},{12... | collective-permute-start | bytes 442376 | tf_op jit(solution)/shard_map/ppermute | solution.py:385
  97.0 19.6 %collective-permute-start.5 = (f32[2,72,256]{2,1,0:T(8,128)}, f32[2,72,256]{2,1,0:T(8,128)S(1)}, u32[]{:S(2)}, u32[]{:S(2)}) collective-permute-start(f32[2,72,256]{2,1,0:T(8,128)} %get-tuple-element.23.val_ref), channel_id=1, source_target_pairs={{16,0},{0,8},{17,1},{1,9},{18,2},{2,10},{19,3},{3,11},{20,4},{4,12... | collective-permute-start | bytes 442376 | tf_op jit(solution)/shard_map/ppermute | solution.py:385
  97.7 20.5 %collective-permute-start.16 = (f32[2,72,256]{2,1,0:T(8,128)}, f32[2,72,256]{2,1,0:T(8,128)S(1)}, u32[]{:S(2)}, u32[]{:S(2)}) collective-permute-start(f32[2,72,256]{2,1,0:T(8,128)} %get-tuple-element.28.val_ref), channel_id=1, source_target_pairs={{24,8},{8,16},{25,9},{9,17},{26,10},{10,18},{27,11},{11,19},{28,12... | collective-permute-start | bytes 442376 | tf_op jit(solution)/shard_map/ppermute | solution.py:385
  99.0 0.6 copy-start.5
  99.6 0.6 copy-start.7
  102.5 3.1 %collective-permute-start.12 = (f32[1,72,256]{2,1,0:T(8,128)}, f32[1,72,256]{2,1,0:T(8,128)S(1)}, u32[]{:S(2)}, u32[]{:S(2)}) collective-permute-start(f32[1,72,256]{2,1,0:T(8,128)} %get-tuple-element.32), channel_id=1, source_target_pairs={{0,1},{1,0},{2,3},{3,2},{4,5},{5,4},{6,7},{7,6},{8,9},{9,8},{10,11... | collective-permute-start | bytes 221192 | tf_op jit(solution)/shard_map/ppermute | solution.py:323
  102.5 7.1 %collective-permute-start.13 = (f32[1,72,256]{2,1,0:T(8,128)}, f32[1,72,256]{2,1,0:T(8,128)S(1)}, u32[]{:S(2)}, u32[]{:S(2)}) collective-permute-start(f32[1,72,256]{2,1,0:T(8,128)} %get-tuple-element.33), channel_id=1, source_target_pairs={{1,2},{2,1},{3,4},{4,3},{5,6},{6,5},{9,10},{10,9},{11,12},{12,11},... | collective-permute-start | bytes 221192 | tf_op jit(solution)/shard_map/ppermute | solution.py:326
  105.6 7.4 %copy-start.6 = (f32[1,72,256]{2,1,0:T(8,128)}, f32[1,72,256]{2,1,0:T(8,128)S(1)}, u32[]{:S(2)}) copy-start(f32[1,72,256]{2,1,0:T(8,128)S(1)} %collective-permute-done.12.partner_ref) | copy-start | bytes 221188
  105.6 13.8 %collective-permute-start.8 = (f32[2,72,256]{2,1,0:T(8,128)}, f32[2,72,256]{2,1,0:T(8,128)S(1)}, u32[]{:S(2)}, u32[]{:S(2)}) collective-permute-start(f32[2,72,256]{2,1,0:T(8,128)} %get-tuple-element.28.val_ref), channel_id=1, source_target_pairs={{16,8},{0,16},{17,9},{1,17},{18,10},{2,18},{19,11},{3,19},{20,12},... | collective-permute-start | bytes 442376 | tf_op jit(solution)/shard_map/ppermute | solution.py:385
  109.6 3.5 %copy-start.8 = (f32[1,72,256]{2,1,0:T(8,128)}, f32[1,72,256]{2,1,0:T(8,128)S(1)}, u32[]{:S(2)}) copy-start(f32[1,72,256]{2,1,0:T(8,128)S(1)} %collective-permute-done.13.other_ref) | copy-start | bytes 221188
  109.6 9.9 %collective-permute-start.17 = (f32[2,72,256]{2,1,0:T(8,128)}, f32[2,72,256]{2,1,0:T(8,128)S(1)}, u32[]{:S(2)}, u32[]{:S(2)}) collective-permute-start(f32[2,72,256]{2,1,0:T(8,128)} %get-tuple-element.31.val_ref), channel_id=1, source_target_pairs={{24,16},{8,24},{25,17},{9,25},{26,18},{10,26},{27,19},{11,27},{28,... | collective-permute-start | bytes 442376 | tf_op jit(solution)/shard_map/ppermute | solution.py:385
  115.3 9.4 %collective-permute-start.11 = (f32[2,72,256]{2,1,0:T(8,128)}, f32[2,72,256]{2,1,0:T(8,128)S(1)}, u32[]{:S(2)}, u32[]{:S(2)}) collective-permute-start(f32[2,72,256]{2,1,0:T(8,128)} %get-tuple-element.31.val_ref), channel_id=1, source_target_pairs={{16,16},{0,24},{17,17},{1,25},{18,18},{2,26},{19,19},{3,27},{20,20... | collective-permute-start | bytes 442376 | tf_op jit(solution)/shard_map/ppermute | solution.py:385
  116.6 8.1 %collective-permute-start.18 = (f32[2,72,256]{2,1,0:T(8,128)}, f32[2,72,256]{2,1,0:T(8,128)S(1)}, u32[]{:S(2)}, u32[]{:S(2)}) collective-permute-start(f32[2,72,256]{2,1,0:T(8,128)} %get-tuple-element.34), channel_id=1, source_target_pairs={{24,24},{25,25},{26,26},{27,27},{28,28},{29,29},{30,30},{31,31}} | collective-permute-start | bytes 442376 | tf_op jit(solution)/shard_map/ppermute | solution.py:385
  118.2 9.5 %collective-permute-start.14 = (f32[2,72,256]{2,1,0:T(8,128)}, f32[2,72,256]{2,1,0:T(8,128)S(1)}, u32[]{:S(2)}, u32[]{:S(2)}) collective-permute-start(f32[2,72,256]{2,1,0:T(8,128)} %get-tuple-element.34), channel_id=1, source_target_pairs={{16,24},{17,25},{18,26},{19,27},{20,28},{21,29},{22,30},{23,31}} | collective-permute-start | bytes 442376 | tf_op jit(solution)/shard_map/ppermute | solution.py:385
  127.7 1.6 %copy-start.1 = (f32[1,4,256,512]{3,2,1,0:T(8,128)S(1)}, f32[1,4,256,512]{3,2,1,0:T(8,128)}, u32[]{:S(2)}) copy-start(f32[1,4,256,512]{3,2,1,0:T(8,128)} %param.4) | copy-start | bytes 6291460

commit v2 on v1

v2 whole, which is shorter than its diff:
```python
import functools

import jax
import jax.numpy as jnp
from jax import lax
from jax.experimental import pallas as pl
from jax.experimental.pallas import tpu as pltpu
from jax.sharding import PartitionSpec as P

STEPS = 4
courant = 0.15
GAIN = 0.5 * courant
MARGIN = 16
F32 = jnp.float32
VMEM = pltpu.VMEM
MIB = 1024 * 1024
VMEM_LIMITS = {"inner": 44 * MIB, "outer": 48 * MIB, "small": 10 * MIB, "final": 16 * MIB}


def params(limit):
    return pltpu.CompilerParams(vmem_limit_bytes=limit)


def whole(count):
    return [pl.BlockSpec(memory_space=VMEM)] * count


def shape(*dims):
    return jax.ShapeDtypeStruct(dims, F32)


def split_dot(x, selection):
    high = x.astype(jnp.bfloat16)
    rest = x - high.astype(F32)
    middle = rest.astype(jnp.bfloat16)
    low = (rest - middle.astype(F32)).astype(jnp.bfloat16)
    dot = functools.partial(jnp.dot, preferred_element_type=F32)
    return dot(high, selection) + dot(middle, selection) + dot(low, selection)


def pairing(width):
    fine = lax.broadcasted_iota(jnp.int32, (width, width // 2), 0)
    coarse = lax.broadcasted_iota(jnp.int32, (width, width // 2), 1)
    return jnp.where((fine == 2 * coarse) | (fine == 2 * coarse + 1), 1.0, 0.0).astype(jnp.bfloat16)


def spreading(width):
    coarse = lax.broadcasted_iota(jnp.int32, (width // 2, width), 0)
    fine = lax.broadcasted_iota(jnp.int32, (width // 2, width), 1)
    return jnp.where((fine == 2 * coarse) | (fine == 2 * coarse + 1), 1.0, 0.0).astype(jnp.bfloat16)


def block_mean(first, second, rows_scr, select):
    rows = first.shape[0]
    lanes = split_dot(first + second, select)
    parts = []
    for j in range(lanes.shape[1] // 128):
        rows_scr[j, 0:rows, :] = lanes[:, 128 * j : 128 * j + 128]
        even = rows_scr[j, pl.ds(0, rows // 2, 2), :]
        odd = rows_scr[j, pl.ds(1, rows // 2, 2), :]
        parts.append(0.125 * (even + odd))
    return jnp.concatenate(parts, axis=1)


def tile_masks(lanes):
    sub = lax.broadcasted_iota(jnp.int32, (8, lanes), 0)
    lane = lax.broadcasted_iota(jnp.int32, (8, lanes), 1)
    return sub, lane


def weights_plane(load, store, rows, lanes, dot_low=True):
    sub, lane = tile_masks(lanes)
    tiles = rows // 8
    zero = jnp.zeros((8, lanes), F32)
    for i in range(tiles):
        c = load(0, i)
        down = load(0, i - 1) if i > 0 else zero
        up = load(0, i + 1) if i + 1 < tiles else zero
        cym = jnp.where(sub == 0, pltpu.roll(down, 1, 0), pltpu.roll(c, 1, 0))
        cyp = jnp.where(sub == 7, pltpu.roll(up, 7, 0), pltpu.roll(c, 7, 0))
        cxm = jnp.where(lane == 0, 0.0, pltpu.roll(c, 1, 1))
        cxp = jnp.where(lane == lanes - 1, 0.0, pltpu.roll(c, lanes - 1, 1))
        czm = load(-1, i)
        czp = load(1, i)
        gain = jnp.where(c > 0.0, GAIN, 0.0)
        store(0, i, 1.0 - GAIN * (6.0 * c + (cxm + cxp) + (cym + cyp) + (czm + czp)))
        wxm = gain * (c + cxm)
        wxp = gain * (c + cxp)
        wym = gain * (c + cym)
        wyp = gain * (c + cyp)
        store(1, i, jnp.where(lane == 0, 0.0, wxm))
        store(2, i, jnp.where(lane == lanes - 1, 0.0, wxp))
        store(3, i, jnp.where(sub == 0, 0.0, wym) if i == 0 else wym)
        store(4, i, jnp.where(sub == 7, 0.0, wyp) if i + 1 == tiles else wyp)
        store(5, i, gain * (c + czm))
        store(6, i, gain * (c + czp))


def step_plane(weight, load, store, rows, lanes, fields=1):
    sub, _ = tile_masks(lanes)
    tiles = rows // 8
    center = [load(f, 0, 0) for f in range(fields)]
    below = list(center)
    for i in range(tiles):
        w = [weight(k, i) for k in range(7)]
        for f in range(fields):
            mid = center[f]
            above = load(f, 0, i + 1) if i + 1 < tiles else mid
            ym = jnp.where(sub == 0, pltpu.roll(below[f], 1, 0), pltpu.roll(mid, 1, 0))
            yp = jnp.where(sub == 7, pltpu.roll(above, 7, 0), pltpu.roll(mid, 7, 0))
            xm = pltpu.roll(mid, 1, 1)
            xp = pltpu.roll(mid, lanes - 1, 1)
            out = w[0] * mid
            out = out + (w[1] * xm + w[2] * xp)
            out = out + (w[3] * ym + w[4] * yp)
            out = out + (w[5] * load(f, -1, i) + w[6] * load(f, 1, i))
            store(f, i, out)
            below[f], center[f] = mid, above


def tile(i):
    return slice(8 * i, 8 * i + 8)


def at_row(value, step):
    return pl.multiple_of(value * step, 8)


def propagate(planes, flag_ref, c_scr, w_scr, a_scr, b_scr, cc_scr, cw_scr, rows_scr, keep_scr):
    last = flag_ref[2]
    depth, rows, lanes = c_scr.shape
    select = pairing(lanes)
    coarse_planes, reach = depth // 2, planes // 2
    coarse_rows, coarse_lanes = rows // 2, lanes // 2
    last_plane = depth - 1

    def weigh(z, _):
        below, above = jnp.maximum(z - 1, 0), jnp.minimum(z + 1, last_plane)

        def load(dz, i):
            at = z if dz == 0 else (below if dz < 0 else above)
            return c_scr[at, tile(i), :]

        def store(k, i, w):
            w_scr[k, z, tile(i), :] = w

        weights_plane(load, store, rows, lanes)
        return 0

    lax.fori_loop(0, depth, weigh, 0)

    def restrict_c(q, _):
        cc_scr[q] = block_mean(c_scr[2 * q], c_scr[2 * q + 1], rows_scr, select)
        return 0

    lax.fori_loop(0, coarse_planes, restrict_c, 0)
    for q in range(reach):
        def load(dz, i):
            return cc_scr[reach + q + dz, tile(i), :]

        def store(k, i, w):
            cw_scr[k, q, tile(i), :] = w

        weights_plane(load, store, coarse_rows, coarse_lanes)

    def keep(n, _):
        field, q = n // reach, n % reach
        keep_scr[n] = block_mean(
            a_scr[field, planes + 2 * q], a_scr[field, planes + 2 * q + 1], rows_scr, select
        )
        return 0

    lax.fori_loop(0, 2 * reach, keep, 0)
    for number in range(STEPS):
        v_in, v_out = (a_scr, b_scr) if number % 2 == 0 else (b_scr, a_scr)

        def advance(z, _):
            below, above = jnp.maximum(z - 1, 0), jnp.minimum(z + 1, last_plane)

            def load(f, dz, i):
                at = z if dz == 0 else (below if dz < 0 else above)
                return v_in[f, at, tile(i), :]

            def weight(k, i):
                return w_scr[k, z, tile(i), :]

            def store(f, i, v):
                v_out[f, z, tile(i), :] = v

            step_plane(weight, load, store, rows, lanes, 2)
            return 0

        lax.fori_loop(planes - 1 - number, 2 * planes + 1 + number, advance, 0)
    result = a_scr if STEPS % 2 == 0 else b_scr

    def restrict_v(n, _):
        field, q = n // coarse_planes, n % coarse_planes
        mean = block_mean(result[field, 2 * q], result[field, 2 * q + 1], rows_scr, select)
        b_scr[field, q, 0:coarse_rows, 0:coarse_lanes] = mean
        return 0

    lax.fori_loop(0, 2 * coarse_planes, restrict_v, 0)

    scale = jnp.where(last == 1, 0.0, 1.0).astype(F32)
    for q in range(reach):
        keep_scr[q] = keep_scr[q] * scale
    zero = jnp.zeros((8, coarse_lanes), F32)
    low_c, high_c = cc_scr[reach - 1], cc_scr[2 * reach]
    low_w = jnp.where(low_c > 0.0, GAIN * (low_c + cc_scr[reach]), 0.0)
    high_w = jnp.where(high_c > 0.0, GAIN * (high_c + cc_scr[2 * reach - 1]), 0.0)
    for q in range(reach):
        def load(f, dz, i):
            at = q + dz
            return zero if at < 0 or at >= reach else keep_scr[f * reach + at, tile(i), :]

        def weight(k, i):
            return cw_scr[k, q, tile(i), :]

        def store(f, i, v):
            b_scr[f, reach + q, tile(i), 0:coarse_lanes] = b_scr[f, reach + q, tile(i), 0:coarse_lanes] - v

        step_plane(weight, load, store, coarse_rows, coarse_lanes, 2)
    planes_of = []
    for f in range(2):
        mean = [b_scr[f, q, 0:coarse_rows, 0:coarse_lanes] for q in range(coarse_planes)]
        mean[reach - 1] = mean[reach - 1] - low_w * keep_scr[f * reach]
        mean[2 * reach] = mean[2 * reach] - high_w * keep_scr[f * reach + reach - 1]
        planes_of.append(mean)
    return planes_of


def place_fields(flag_ref, planes, own_at, count, row_at, first_row, iterate_ref, initial_ref, received_ref, a_scr, b_scr):
    half, last = flag_ref[0], flag_ref[2]
    a_scr[...] = jnp.zeros(a_scr.shape, F32)
    edge = jnp.zeros((2, planes - 1) + b_scr.shape[2:], F32)
    b_scr[:, 0 : planes - 1] = edge
    b_scr[:, 2 * planes + 1 :] = edge
    own = pl.ds(own_at, count)
    source = pl.ds(row_at, count)
    first_kept = (last == 0) & (half == 0)
    second_kept = (last == 1) == (half == 0)

    @pl.when(last == 1)
    def _():
        a_scr[0, planes : 2 * planes, own, :] = initial_ref[:, source, :]

    @pl.when(first_kept)
    def _():
        a_scr[0, planes : 2 * planes, own, :] = iterate_ref[:, source, :]

    @pl.when((last == 0) & (half == 1))
    def _():
        a_scr[0, planes : 2 * planes, own, :] = received_ref[...]

    @pl.when(second_kept)
    def _():
        a_scr[1, planes : 2 * planes, own, :] = iterate_ref[:, source, :]

    @pl.when(jnp.logical_not(second_kept))
    def _():
        a_scr[1, planes : 2 * planes, own, :] = received_ref[...]


def inner_kernel(planes, flag_ref, c_ref, partner_ref, other_ref, iterate_ref, initial_ref, received_ref,
                 own_ref, up_ref, down_ref, weight_ref, c_scr, w_scr, a_scr, b_scr, cc_scr, cw_scr, rows_scr, keep_scr):
    half, upper = flag_ref[0], flag_ref[1]
    rows = c_scr.shape[1]
    count = received_ref.shape[1]
    window = pl.ds(at_row(1 - half, c_ref.shape[1] - rows), rows)
    c_scr[planes : 2 * planes] = c_ref[:, window, :]
    c_scr[pl.ds(upper * (2 * planes), planes)] = partner_ref[:, window, :]
    c_scr[pl.ds((1 - upper) * (2 * planes), planes)] = other_ref[...]
    middle = iterate_ref.shape[1] // 2
    row_at = pl.multiple_of(middle - count + half * count, 8)
    place_fields(flag_ref, planes, MARGIN, count, row_at, None, iterate_ref, initial_ref, received_ref, a_scr, b_scr)
    fields = propagate(planes, flag_ref, c_scr, w_scr, a_scr, b_scr, cc_scr, cw_scr, rows_scr, keep_scr)
    reach = planes // 2
    for f, mean in enumerate(fields):
        for q in range(reach):
            down_ref[f, q] = mean[q]
            own_ref[f, q] = mean[reach + q]
            up_ref[f, q] = mean[2 * reach + q]
    weight_ref[...] = cw_scr[...]


def outer_kernel(planes, flag_ref, c_ref, partner_ref, other_ref, rest_ref, iterate_ref, initial_ref, received_ref,
                 in_own_ref, in_up_ref, in_down_ref, in_weight_ref, own_ref, to_partner_ref, to_other_ref, weight_ref,
                 c_scr, w_scr, a_scr, b_scr, cc_scr, cw_scr, rows_scr, keep_scr):
    half, upper = flag_ref[0], flag_ref[1]
    rows = c_scr.shape[1]
    count = received_ref.shape[1]
    all_rows = c_ref.shape[1]
    inner, rest = other_ref.shape[1], rest_ref.shape[1]
    shared = rows - rest
    window = pl.ds(at_row(half, all_rows - rows), rows)
    c_scr[planes : 2 * planes] = c_ref[:, window, :]
    c_scr[pl.ds(upper * (2 * planes), planes)] = partner_ref[:, window, :]
    far = pl.ds((1 - upper) * (2 * planes), planes)
    c_scr[far, pl.ds(at_row(half, shared), rest), :] = rest_ref[...]
    c_scr[far, pl.ds(at_row(1 - half, rest), shared), :] = other_ref[:, pl.ds(at_row(half, inner - shared), shared), :]
    row_at = at_row(half, iterate_ref.shape[1] - count)
    place_fields(flag_ref, planes, at_row(half, MARGIN), count, row_at, None, iterate_ref, initial_ref, received_ref,
                 a_scr, b_scr)
    fields = propagate(planes, flag_ref, c_scr, w_scr, a_scr, b_scr, cc_scr, cw_scr, rows_scr, keep_scr)
    reach = planes // 2
    outer_at = pl.ds(at_row(half, (all_rows - rows) // 2), rows // 2)
    inner_at = pl.ds(at_row(1 - half, (all_rows - inner) // 2), inner // 2)

    def put(ref, f, q, outer, inner_ref):
        ref[f, q] = jnp.zeros(ref.shape[2:], F32)
        ref[f, q, outer_at, :] = outer
        ref[f, q, inner_at, :] = ref[f, q, inner_at, :] + inner_ref[f, q]

    for f, mean in enumerate(fields):
        for q in range(reach):
            put(own_ref, f, q, mean[reach + q], in_own_ref)

    @pl.when(upper == 1)
    def _():
        for f, mean in enumerate(fields):
            for q in range(reach):
                put(to_partner_ref, f, q, mean[2 * reach + q], in_up_ref)
                put(to_other_ref, f, q, mean[q], in_down_ref)

    @pl.when(upper == 0)
    def _():
        for f, mean in enumerate(fields):
            for q in range(reach):
                put(to_partner_ref, f, q, mean[q], in_down_ref)
                put(to_other_ref, f, q, mean[2 * reach + q], in_up_ref)

    kept = inner // 2 - 8
    from_outer = all_rows // 2 - kept
    for k in range(7):
        for q in range(reach):
            weight_ref[k, q, pl.ds(at_row(1 - half, from_outer), kept), :] = in_weight_ref[k, q, pl.ds(at_row(1 - half, 8), kept), :]
            weight_ref[k, q, pl.ds(at_row(half, kept), from_outer), :] = cw_scr[k, q, pl.ds(at_row(half, 8), from_outer), :]


def edges(flag_ref, val, to_partner_ref, to_other_ref):
    upper = flag_ref[1]

    @pl.when(upper == 1)
    def _():
        to_partner_ref[0] = val[-1]
        to_other_ref[0] = val[0]

    @pl.when(upper == 0)
    def _():
        to_partner_ref[0] = val[0]
        to_other_ref[0] = val[-1]


def sum_kernel(flag_ref, own_ref, partner_ref, other_ref, val_ref, extra_ref, to_partner_ref, to_other_ref):
    val = own_ref[0] + partner_ref[0] + other_ref[0]
    val_ref[...] = val
    extra_ref[...] = own_ref[1] + partner_ref[1] + other_ref[1]
    edges(flag_ref, val, to_partner_ref, to_other_ref)


def chain_kernel(add_slot, send_slots, more, flag_ref, weight_ref, partner_ref, other_ref, extra_ref, *refs):
    earlier = refs[: more + 1]
    val_ref = earlier[-1]
    next_ref, to_partner_ref, to_other_ref = refs[more + 1 : more + 4]
    sends, wide = refs[more + 4 : -1], refs[-1]
    upper = flag_ref[1]
    add = flag_ref[add_slot].astype(F32)
    planes, rows, lanes = val_ref.shape
    wide[1 : planes + 1] = val_ref[...]
    wide[upper * (planes + 1)] = partner_ref[0]
    wide[(1 - upper) * (planes + 1)] = other_ref[0]
    for q in range(planes):
        def load(f, dz, i):
            return wide[1 + q + dz, tile(i), :]

        def weight(k, i):
            return weight_ref[k, q, tile(i), :]

        def store(f, i, v):
            next_ref[q, tile(i), :] = v + add * extra_ref[q, tile(i), :]

        step_plane(weight, load, store, rows, lanes)
    edges(flag_ref, next_ref[...], to_partner_ref, to_other_ref)
    for slot, ref in zip(send_slots, sends):
        which = flag_ref[slot]

        @pl.when(which < 0)
        def _():
            ref[...] = jnp.zeros(ref.shape, F32)

        for m, source in enumerate([*earlier, next_ref]):
            @pl.when(which == m)
            def _():
                ref[...] = source[...]


def final_kernel(slots, flag_ref, iterate_ref, *refs):
    count = len(slots)
    pieces, out_ref, rows_scr, fine_scr, error_scr = refs[:count], *refs[count:]
    planes, rows, lanes = iterate_ref.shape
    select, spread = pairing(lanes), spreading(lanes)
    piece_rows = pieces[0].shape[1]
    for q in range(planes // 2):
        error_scr[...] = -block_mean(iterate_ref[2 * q], iterate_ref[2 * q + 1], rows_scr, select)
        for slot, ref in zip(slots, pieces):
            at = pl.ds(at_row(flag_ref[slot], rows // 2 - piece_rows), piece_rows)
            error_scr[at, :] = error_scr[at, :] + ref[q]
        wide = split_dot(error_scr[...], spread)
        for j in range(lanes // 128):
            column = slice(128 * j, 128 * j + 128)
            fine_scr[j, pl.ds(0, rows // 2, 2), :] = wide[:, column]
            fine_scr[j, pl.ds(1, rows // 2, 2), :] = wide[:, column]
            for part in range(2):
                out_ref[2 * q + part, :, column] = iterate_ref[2 * q + part, :, column] + fine_scr[j]


def swap_pairs(count, first):
    pairs = []
    for i in range(first, count - 1, 2):
        pairs += [(i, i + 1), (i + 1, i)]
    return pairs


def roles(layers):
    last_group = layers // 2 - 1
    rows = []
    for t in range(layers):
        half, last = t % 2, int(t // 2 == last_group)
        adds = [int(number == (layers - 1 if last else 1)) for number in range(1, layers)]
        sends = []
        for shift in range(layers):
            k = (t + shift) % layers
            m = k if last else k - 1 - (t - half)
            sends.append(m if m >= 0 else -1)
        halves = [(t - shift) % layers % 2 for shift in range(layers)]
        rows.append([half, last, *adds, *sends, *halves])
    return rows


def local(initial, iterate, diffusivity):
    layers, slabs = lax.axis_size("tm"), lax.axis_size("space")
    t, s = lax.axis_index("tm"), lax.axis_index("space")
    planes, all_rows, lanes = initial.shape
    assert layers % 2 == 0 and slabs % 2 == 0 and planes == STEPS
    half = t % 2
    own_rows = all_rows // 2
    rows = own_rows + MARGIN
    inner_own = (3 * own_rows // 8) // 16 * 16
    outer_own = own_rows - inner_own
    inner_rows, outer_rows = inner_own + 2 * MARGIN, outer_own + MARGIN
    coarse_rows, coarse_lanes = rows // 2, lanes // 2
    reach = planes // 2
    upper = 1 - s % 2
    field = iterate[0]

    def partner_swap(x):
        return lax.ppermute(x, "space", swap_pairs(slabs, 0))

    def other_swap(x):
        return lax.ppermute(x, "space", swap_pairs(slabs, 1))

    def rows_of(x, start, count):
        return lax.dynamic_slice_in_dim(x, start, count, axis=1)

    base = half * (all_rows - rows)
    other_inner = other_swap(rows_of(diffusivity, base + (1 - half) * (rows - inner_rows), inner_rows))
    c = rows_of(diffusivity, base, rows)
    c_partner = partner_swap(c)
    row_pairs = swap_pairs(layers, 0)
    row_pairs.remove((layers - 1, layers - 2))
    got_inner = lax.ppermute(rows_of(field, own_rows - half * inner_own, inner_own), "tm", row_pairs)
    other_rest = other_swap(rows_of(diffusivity, base + half * inner_rows, rows - inner_rows))
    got_outer = lax.ppermute(rows_of(field, (1 - half) * (all_rows - outer_own), outer_own), "tm", row_pairs)

    table = roles(layers)
    mine = jnp.asarray(table, jnp.int32)[t]
    flags = jnp.concatenate([mine[:1], jnp.reshape(upper, (1,)).astype(jnp.int32), mine[1:]])
    add_at, send_at, half_at = 3, 2 + layers, 2 + 2 * layers
    smem = pl.BlockSpec(memory_space=pltpu.SMEM)

    def propagation(kernel, own, window, ins, out_rows, name):
        fields = shape(2, reach, out_rows, coarse_lanes)
        return pl.pallas_call(
            functools.partial(kernel, planes),
            out_shape=(fields, fields, fields, shape(7, reach, out_rows, coarse_lanes)),
            in_specs=[smem] + whole(len(ins)),
            out_specs=tuple(whole(4)),
            scratch_shapes=[
                VMEM((3 * planes, window, lanes), F32),
                VMEM((7, 3 * planes, window, lanes), F32),
                VMEM((2, 3 * planes, window, lanes), F32),
                VMEM((2, 3 * planes, window, lanes), F32),
                VMEM((3 * reach, window // 2, coarse_lanes), F32),
                VMEM((7, reach, window // 2, coarse_lanes), F32),
                VMEM((coarse_lanes // 128, window, 128), F32),
                VMEM((2 * reach, window // 2, coarse_lanes), F32),
            ],
            compiler_params=params(VMEM_LIMITS[name]),
            name=name,
        )(flags, *ins)

    inner = propagation(
        inner_kernel, inner_own, inner_rows, (c, c_partner, other_inner, field, initial, got_inner), inner_rows // 2, "inner"
    )
    own, to_partner, to_other, weights = propagation(
        outer_kernel, outer_own, outer_rows,
        (c, c_partner, other_inner, other_rest, field, initial, got_outer, *inner), coarse_rows, "outer",
    )

    from_other = other_swap(to_other)
    from_partner = partner_swap(to_partner)
    plane = shape(1, coarse_rows, coarse_lanes)
    block = shape(reach, coarse_rows, coarse_lanes)
    val, extra, to_partner, to_other = pl.pallas_call(
        sum_kernel,
        out_shape=(block, block, plane, plane),
        in_specs=[smem] + whole(3),
        out_specs=tuple(whole(4)),
        compiler_params=params(VMEM_LIMITS["small"]),
        name="gather",
    )(flags, own, from_partner, from_other)

    ready = [max(row[1 + layers + shift] for row in table) for shift in range(layers)]
    arrived = [None] * layers
    values = [val]
    for number in range(1, layers):
        from_other = other_swap(to_other)
        from_partner = partner_swap(to_partner)
        shifts = [shift for shift in range(layers) if max(ready[shift], 1) == number]
        earlier = values if shifts else values[-1:]
        val, to_partner, to_other, *sends = pl.pallas_call(
            functools.partial(chain_kernel, add_at + number - 1, [send_at + shift for shift in shifts], len(earlier) - 1),
            out_shape=(block, plane, plane, *[block] * len(shifts)),
            in_specs=[smem] + whole(4 + len(earlier)),
            out_specs=tuple(whole(3 + len(shifts))),
            scratch_shapes=[VMEM((reach + 2, coarse_rows, coarse_lanes), F32)],
            compiler_params=params(VMEM_LIMITS["small"]),
            name=f"chain{number}",
        )(flags, weights, from_partner, from_other, extra, *earlier)
        values.append(val)
        for shift, send in zip(shifts, sends):
            pairs = [
                (source, (source + shift) % layers)
                for source in range(layers)
                if table[source][1 + layers + shift] >= 0
            ]
            arrived[shift] = lax.ppermute(send, "tm", pairs) if shift else send

    corrected = pl.pallas_call(
        functools.partial(final_kernel, [half_at + shift for shift in range(layers)]),
        out_shape=shape(planes, all_rows, lanes),
        in_specs=[smem] + whole(1 + layers),
        out_specs=pl.BlockSpec(memory_space=VMEM),
        scratch_shapes=[
            VMEM((coarse_lanes // 128, all_rows, 128), F32),
            VMEM((lanes // 128, all_rows, 128), F32),
            VMEM((all_rows // 2, coarse_lanes), F32),
        ],
        compiler_params=params(VMEM_LIMITS["final"]),
        name="final",
    )(flags, field, *arrived)
    return corrected[None]


def solution(mesh):
    placed = (P("space", None, None), P("tm", "space", None, None), P("space", None, None))
    return jax.shard_map(
        local, mesh=mesh, in_specs=placed, out_specs=P("tm", "space", None, None), check_vma=False
    )
```

time: 134 us -> 135 us (level)
  Pallas kernels: 43.3 us -> 54.7 us
  starting transfers between devices: 31.8 us -> 25.4 us
  local copies, waits for them, and re-layouts: 7.31 us -> 11.1 us
  waiting for transfers between devices: 46.2 us -> 42.7 us
  other arithmetic: 3.58 us -> 0.11 us
    pallas_call x5 -> x6, Pallas kernels: 41.4 us -> 54.1 us  [the longest x2 47.2 us: propagation(): pl.pallas_call(functools.partial(kernel, planes), out_shape=(fields, fiel...]
    ppermute x9 -> x5, starting transfers between devices: 15.5 us -> 7.48 us  [the longest x3 4.92 us: local(): arrived[shift] = lax.ppermute(send, 'tm', pairs) if shift else send]
    ppermute x9 -> x5, waiting for transfers between devices: 29.7 us -> 25.7 us  [the longest x1 18.2 us: local(): lax.ppermute(rows_of(field, own_rows - half * inner_own, inner_own), 'tm'...]
    dynamic_slice x2 -> x6, local copies, waits for them, and re-layouts: 2.51 us -> 6.25 us  [the longest x5 5.56 us: rows_of(): return lax.dynamic_slice_in_dim(x, start, count, axis=1)]
    select_n x1 -> x0, other arithmetic: 3.58 us -> none  [local(): second = jnp.where(last == (half == 0), kept, received)]
    ppermute x5 -> x6, starting transfers between devices: 15.5 us -> 17.6 us  [other_swap(): return lax.ppermute(x, 'space', swap_pairs(slabs, 1))]
    pallas_call x1, Pallas kernels: 1.97 us -> 0.59 us  [local(): pl.pallas_call(sum_kernel, out_shape=(block, block, plane, plane), in_spe...]
    unnamed x22 -> x8, local copies, waits for them, and re-layouts: 4.18 us -> 4.78 us
  transfers between devices with their start and end apart: 19 -> 16, of which waited for: 7 -> 7; matrix products, arithmetic and copies ran while one was open for 3% -> 5% of each run, Pallas kernels for 3% -> 17%
where the time goes in v2:
time: 135 us; the launch traced here: 134 us
  Pallas kernels  54.7 us (41%)
  waiting for transfers between devices  42.7 us (32%)
  starting transfers between devices  25.4 us (19%)
  local copies, waits for them, and re-layouts  11.1 us (8%)
    pallas_call x2, Pallas kernels, propagation(): pl.pallas_call(functools.partial(kernel, planes), out_shape=(fields, fiel...  47.2 us
    ppermute x1, waiting for transfers between devices, local(): lax.ppermute(rows_of(field, own_rows - half * inner_own, inner_own), 'tm'...  18.2 us
    ppermute x6, starting transfers between devices, other_swap(): return lax.ppermute(x, 'space', swap_pairs(slabs, 1))  17.6 us
    ppermute x6, waiting for transfers between devices, other_swap(): return lax.ppermute(x, 'space', swap_pairs(slabs, 1))  17 us
    ppermute x3, waiting for transfers between devices, local(): arrived[shift] = lax.ppermute(send, 'tm', pairs) if shift else send  7.42 us
    dynamic_slice x5, local copies, waits for them, and re-layouts, rows_of(): return lax.dynamic_slice_in_dim(x, start, count, axis=1)  5.56 us
    ppermute x3, starting transfers between devices, local(): arrived[shift] = lax.ppermute(send, 'tm', pairs) if shift else send  4.92 us
    unnamed x8, local copies, waits for them, and re-layouts  4.78 us
  transfers between devices with their start and end apart: 16, of which 7 were waited for; matrix products, arithmetic and copies ran while one was open for 5% of the time, Pallas kernels for 17%

profile of v2, /device:TPU:28, one launch (start us, length us, event | category | flops | bytes accessed | tf_op | source)
XLA Modules:
  0.0 134.2 jit_solution(16860165876126995464)
XLA Ops:
  0.0 0.0 copy-start
  0.0 1.6 %copy-done = f32[4,256,512]{2,1,0:T(8,128)S(1)} copy-done((f32[4,256,512]{2,1,0:T(8,128)S(1)}, f32[4,256,512]{2,1,0:T(8,128)}, u32[]{:S(2)}) %copy-start) | copy-done | bytes 2097176
  1.6 0.1 constant_dynamic-slice_fusion.2.c_ref
  1.7 0.1 collective-permute-start
  1.8 0.9 constant_dynamic-slice_fusion.1
  2.7 3.4 %collective-permute-start.1 = (f32[4,80,512]{2,1,0:T(8,128)}, f32[4,80,512]{2,1,0:T(8,128)}, u32[]{:S(2)}, u32[]{:S(2)}) collective-permute-start(f32[4,80,512]{2,1,0:T(8,128)} %constant_dynamic-slice_fusion.1), channel_id=1, source_target_pairs={{1,2},{2,1},{3,4},{4,3},{5,6},{6,5},{9,10},{10,9},{11,12},{12,11},... | collective-permute-start | bytes 1966088 | tf_op jit(solution)/shard_map/ppermute | solution.py:460
  6.1 2.0 %dynamic-slice_bitcast_fusion = f32[4,80,512]{2,1,0:T(8,128)} fusion(f32[1,4,256,512]{3,2,1,0:T(8,128)} %param.5, s32[]{:T(128)S(6)} %select_n.35), kind=kLoop, calls=%fused_computation | loop fusion | bytes 1310724 | tf_op jit(solution)/shard_map/dynamic_slice | solution.py:463
  8.1 1.3 collective-permute-start.3
  9.4 0.8 constant_dynamic-slice_fusion
  10.2 3.0 %collective-permute-start.2 = (f32[4,64,512]{2,1,0:T(8,128)}, f32[4,64,512]{2,1,0:T(8,128)}, u32[]{:S(2)}, u32[]{:S(2)}) collective-permute-start(f32[4,64,512]{2,1,0:T(8,128)} %constant_dynamic-slice_fusion), channel_id=1, source_target_pairs={{1,2},{2,1},{3,4},{4,3},{5,6},{6,5},{9,10},{10,9},{11,12},{12,11},... | collective-permute-start | bytes 1572872 | tf_op jit(solution)/shard_map/ppermute | solution.py:460
  13.2 1.8 %dynamic-slice_bitcast_fusion.1 = f32[4,48,512]{2,1,0:T(8,128)} fusion(f32[1,4,256,512]{3,2,1,0:T(8,128)} %param.5, s32[]{:T(128)S(6)} %select_n.36), kind=kLoop, calls=%fused_computation.1 | loop fusion | bytes 786436 | tf_op jit(solution)/shard_map/dynamic_slice | solution.py:463
  15.0 1.3 collective-permute-start.4
  16.3 0.7 constant_dynamic-slice_fusion.3
  17.0 0.1 slice_bitcast_fusion
  17.1 0.1 pad_add_fusion.flag_ref
  17.2 18.2 %collective-permute-done.4.received_ref = f32[4,48,512]{2,1,0:T(8,128)} collective-permute-done((f32[4,48,512]{2,1,0:T(8,128)}, f32[4,48,512]{2,1,0:T(8,128)}, u32[]{:S(2)}, u32[]{:S(2)}) %collective-permute-start.4) | collective-permute-done | bytes 393248 | tf_op jit(solution)/shard_map/ppermute | solution.py:471
  35.4 0.0 collective-permute-done.1.other_ref
  35.4 0.0 collective-permute-done.partner_ref
  35.4 0.0 copy-start.1
  35.4 1.6 %copy-done.1 = f32[1,4,256,512]{3,2,1,0:T(8,128)S(1)} copy-done((f32[1,4,256,512]{3,2,1,0:T(8,128)S(1)}, f32[1,4,256,512]{3,2,1,0:T(8,128)}, u32[]{:S(2)}) %copy-start.1) | copy-done | bytes 2097176
  37.0 0.0 copy-start.3
  37.0 1.6 %copy-done.3 = f32[4,256,512]{2,1,0:T(8,128)S(1)} copy-done((f32[4,256,512]{2,1,0:T(8,128)S(1)}, f32[4,256,512]{2,1,0:T(8,128)}, u32[]{:S(2)}) %copy-start.3) | copy-done | bytes 2097176
  38.6 21.5 %inner.1 = (f32[2,2,40,256]{3,2,1,0:T(8,128)S(1)}, f32[2,2,40,256]{3,2,1,0:T(8,128)S(1)}, f32[2,2,40,256]{3,2,1,0:T(8,128)S(1)}, f32[7,2,40,256]{3,2,1,0:T(8,128)S(1)}) custom-call(s32[14]{0:T(128)S(1)} %pad_add_fusion.flag_ref, f32[4,144,512]{2,1,0:T(8,128)S(1)} %constant_dynamic-slice_fusion.2.c_ref, f32[4,144,512]{2,1,0:T(8,128)} %collective-permute-done.partner_ref, ...), custom_call_target="tpu_custom_call" | custom-call | tf_op jit(solution)/shard_map/inner/pallas_call | solution.py:483
  60.1 0.0 collective-permute-done.2.rest_ref
  60.2 0.0 collective-permute-done.3.received_ref
  60.2 25.7 %outer.1 = (f32[2,2,72,256]{3,2,1,0:T(8,128)S(1)}, f32[2,2,72,256]{3,2,1,0:T(8,128)S(1)}, f32[2,2,72,256]{3,2,1,0:T(8,128)S(1)}, f32[7,2,72,256]{3,2,1,0:T(8,128)S(1)}) custom-call(s32[14]{0:T(128)S(1)} %pad_add_fusion.flag_ref, f32[4,144,512]{2,1,0:T(8,128)S(1)} %constant_dynamic-slice_fusion.2.c_ref, f32[4,144,512]{2,1,0:T(8,128)} %collective-permute-done.partner_ref, ...), custom_call_target="tpu_custom_call" | custom-call | tf_op jit(solution)/shard_map/outer/pallas_call | solution.py:483
  85.9 0.1 collective-permute-start.5
  86.0 3.4 %collective-permute-start.6 = (f32[2,2,72,256]{3,2,1,0:T(8,128)S(1)}, f32[2,2,72,256]{3,2,1,0:T(8,128)S(1)}, u32[]{:S(2)}, u32[]{:S(2)}) collective-permute-start(f32[2,2,72,256]{3,2,1,0:T(8,128)S(1)} %get-tuple-element.34), channel_id=1, source_target_pairs={{1,2},{2,1},{3,4},{4,3},{5,6},{6,5},{9,10},{10,9},{11,12},{12,11},... | collective-permute-start | bytes 884744 | tf_op jit(solution)/shard_map/ppermute | solution.py:460
  89.4 0.0 collective-permute-done.5.partner_ref
  89.4 7.8 %collective-permute-done.6.other_ref = f32[2,2,72,256]{3,2,1,0:T(8,128)S(1)} collective-permute-done((f32[2,2,72,256]{3,2,1,0:T(8,128)S(1)}, f32[2,2,72,256]{3,2,1,0:T(8,128)S(1)}, u32[]{:S(2)}, u32[]{:S(2)}) %collective-permute-start.6) | collective-permute-done | bytes 294944 | tf_op jit(solution)/shard_map/ppermute | solution.py:460
  97.2 0.6 gather.1
  97.8 0.1 collective-permute-start.7
  97.9 2.6 %collective-permute-start.8 = (f32[1,72,256]{2,1,0:T(8,128)S(1)}, f32[1,72,256]{2,1,0:T(8,128)S(1)}, u32[]{:S(2)}, u32[]{:S(2)}) collective-permute-start(f32[1,72,256]{2,1,0:T(8,128)S(1)} %get-tuple-element.36), channel_id=1, source_target_pairs={{1,2},{2,1},{3,4},{4,3},{5,6},{6,5},{9,10},{10,9},{11,12},{12,11},... | collective-permute-start | bytes 221192 | tf_op jit(solution)/shard_map/ppermute | solution.py:460
  100.5 0.0 collective-permute-done.7.partner_ref
  100.5 4.0 %collective-permute-done.8.other_ref = f32[1,72,256]{2,1,0:T(8,128)S(1)} collective-permute-done((f32[1,72,256]{2,1,0:T(8,128)S(1)}, f32[1,72,256]{2,1,0:T(8,128)S(1)}, u32[]{:S(2)}, u32[]{:S(2)}) %collective-permute-start.8) | collective-permute-done | bytes 73760 | tf_op jit(solution)/shard_map/ppermute | solution.py:460
  104.5 0.0 copy-start.2
  104.5 0.7 chain1.1
  105.2 0.1 collective-permute-start.9
  105.3 2.6 %collective-permute-start.10 = (f32[1,72,256]{2,1,0:T(8,128)S(1)}, f32[1,72,256]{2,1,0:T(8,128)S(1)}, u32[]{:S(2)}, u32[]{:S(2)}) collective-permute-start(f32[1,72,256]{2,1,0:T(8,128)S(1)} %get-tuple-element.40), channel_id=1, source_target_pairs={{1,2},{2,1},{3,4},{4,3},{5,6},{6,5},{9,10},{10,9},{11,12},{12,11},... | collective-permute-start | bytes 221192 | tf_op jit(solution)/shard_map/ppermute | solution.py:460
  107.9 0.0 collective-permute-done.9.partner_ref
  107.9 4.0 %collective-permute-done.10.other_ref = f32[1,72,256]{2,1,0:T(8,128)S(1)} collective-permute-done((f32[1,72,256]{2,1,0:T(8,128)S(1)}, f32[1,72,256]{2,1,0:T(8,128)S(1)}, u32[]{:S(2)}, u32[]{:S(2)}) %collective-permute-start.10) | collective-permute-done | bytes 73760 | tf_op jit(solution)/shard_map/ppermute | solution.py:460
  111.8 0.8 chain2.1
  112.6 0.1 collective-permute-start.11
  112.7 2.6 %collective-permute-start.12 = (f32[1,72,256]{2,1,0:T(8,128)S(1)}, f32[1,72,256]{2,1,0:T(8,128)S(1)}, u32[]{:S(2)}, u32[]{:S(2)}) collective-permute-start(f32[1,72,256]{2,1,0:T(8,128)S(1)} %get-tuple-element.43), channel_id=1, source_target_pairs={{1,2},{2,1},{3,4},{4,3},{5,6},{6,5},{9,10},{10,9},{11,12},{12,11},... | collective-permute-start | bytes 221192 | tf_op jit(solution)/shard_map/ppermute | solution.py:460
  115.3 0.4 collective-permute-start.14
  115.7 2.4 %collective-permute-start.15 = (f32[2,72,256]{2,1,0:T(8,128)S(1)}, f32[2,72,256]{2,1,0:T(8,128)S(1)}, u32[]{:S(2)}, u32[]{:S(2)}) collective-permute-start(f32[2,72,256]{2,1,0:T(8,128)S(1)} %get-tuple-element.48), channel_id=1, source_target_pairs={{0,24},{16,8},{24,16},{1,25},{17,9},{25,17},{2,26},{18,10},{26,18}... | collective-permute-start | bytes 442376 | tf_op jit(solution)/shard_map/ppermute | solution.py:547
  118.1 0.0 collective-permute-done.11.partner_ref
  118.1 1.2 collective-permute-done.12.other_ref
  119.3 1.5 %chain3.1 = (f32[2,72,256]{2,1,0:T(8,128)}, f32[1,72,256]{2,1,0:T(8,128)}, f32[1,72,256]{2,1,0:T(8,128)}, f32[2,72,256]{2,1,0:T(8,128)S(1)}, f32[2,72,256]{2,1,0:T(8,128)S(1)}) custom-call(s32[14]{0:T(128)S(1)} %pad_add_fusion.flag_ref, f32[7,2,72,256]{3,2,1,0:T(8,128)S(1)} %get-tuple-element.31.weight_ref, ...), custom_call_target="tpu_custom_call" | custom-call | tf_op jit(solution)/shard_map/chain3/pallas_call | solution.py:531
  120.8 2.2 %collective-permute-start.13 = (f32[2,72,256]{2,1,0:T(8,128)S(1)}, f32[2,72,256]{2,1,0:T(8,128)S(1)}, u32[]{:S(2)}, u32[]{:S(2)}) collective-permute-start(f32[2,72,256]{2,1,0:T(8,128)S(1)} %get-tuple-element.46), channel_id=1, source_target_pairs={{0,8},{8,16},{16,24},{24,0},{1,9},{9,17},{17,25},{25,1},{2,10},{10... | collective-permute-start | bytes 442376 | tf_op jit(solution)/shard_map/ppermute | solution.py:547
  122.9 4.4 %collective-permute-done.14.refs_2_ = f32[2,72,256]{2,1,0:T(8,128)S(1)} collective-permute-done((f32[2,72,256]{2,1,0:T(8,128)S(1)}, f32[2,72,256]{2,1,0:T(8,128)S(1)}, u32[]{:S(2)}, u32[]{:S(2)}) %collective-permute-start.14) | collective-permute-done | bytes 147488 | tf_op jit(solution)/shard_map/ppermute | solution.py:547
  127.3 0.0 collective-permute-done.15.refs_3_
  127.3 3.0 %collective-permute-done.13.refs_1_ = f32[2,72,256]{2,1,0:T(8,128)S(1)} collective-permute-done((f32[2,72,256]{2,1,0:T(8,128)S(1)}, f32[2,72,256]{2,1,0:T(8,128)S(1)}, u32[]{:S(2)}, u32[]{:S(2)}) %collective-permute-start.13) | collective-permute-done | bytes 147488 | tf_op jit(solution)/shard_map/ppermute | solution.py:547
  130.3 0.0 copy-done.2
  130.3 3.9 %final.1 = f32[4,256,512]{2,1,0:T(8,128)} custom-call(s32[14]{0:T(128)S(1)} %pad_add_fusion.flag_ref, f32[4,256,512]{2,1,0:T(8,128)S(1)} %bitcast.13, f32[2,72,256]{2,1,0:T(8,128)S(1)} %get-tuple-element.45.refs_0_, f32[2,72,256]{2,1,0:T(8,128)S(1)} %collective-permute-done.13.refs_1_, f32[2,72,256]{2,1,0:T(8,128)S(1)} %collective-permute-done.14.refs_2_, ...), custom_call_target="tpu_custom_call" | custom-call | tf_op jit(solution)/shard_map/final/pallas_call | solution.py:549
Async XLA Ops:
  0.0 1.6 %copy-start = (f32[4,256,512]{2,1,0:T(8,128)S(1)}, f32[4,256,512]{2,1,0:T(8,128)}, u32[]{:S(2)}) copy-start(f32[4,256,512]{2,1,0:T(8,128)} %param.6) | copy-start | bytes 6291460
  1.7 33.8 %collective-permute-start = (f32[4,144,512]{2,1,0:T(8,128)S(1)}, f32[4,144,512]{2,1,0:T(8,128)}, u32[]{:S(2)}, u32[]{:S(2)}) collective-permute-start(f32[4,144,512]{2,1,0:T(8,128)S(1)} %constant_dynamic-slice_fusion.2.c_ref), channel_id=1, source_target_pairs={{0,1},{1,0},{2,3},{3,2},{4,5},{5,4},{6,7},{7,6},{8,9},{9,8},{10,11... | collective-permute-start | bytes 3538952 | tf_op jit(solution)/shard_map/ppermute | solution.py:457
  2.7 32.8 %collective-permute-start.1 = (f32[4,80,512]{2,1,0:T(8,128)}, f32[4,80,512]{2,1,0:T(8,128)}, u32[]{:S(2)}, u32[]{:S(2)}) collective-permute-start(f32[4,80,512]{2,1,0:T(8,128)} %constant_dynamic-slice_fusion.1), channel_id=1, source_target_pairs={{1,2},{2,1},{3,4},{4,3},{5,6},{6,5},{9,10},{10,9},{11,12},{12,11},... | collective-permute-start | bytes 1966088 | tf_op jit(solution)/shard_map/ppermute | solution.py:460
  8.1 52.1 %collective-permute-start.3 = (f32[4,80,512]{2,1,0:T(8,128)}, f32[4,80,512]{2,1,0:T(8,128)}, u32[]{:S(2)}, u32[]{:S(2)}) collective-permute-start(f32[4,80,512]{2,1,0:T(8,128)} %dynamic-slice_bitcast_fusion), channel_id=1, source_target_pairs={{0,8},{8,0},{16,24},{1,9},{9,1},{17,25},{2,10},{10,2},{18,26},{3,1... | collective-permute-start | bytes 1966088 | tf_op jit(solution)/shard_map/ppermute | solution.py:473
  10.2 49.9 %collective-permute-start.2 = (f32[4,64,512]{2,1,0:T(8,128)}, f32[4,64,512]{2,1,0:T(8,128)}, u32[]{:S(2)}, u32[]{:S(2)}) collective-permute-start(f32[4,64,512]{2,1,0:T(8,128)} %constant_dynamic-slice_fusion), channel_id=1, source_target_pairs={{1,2},{2,1},{3,4},{4,3},{5,6},{6,5},{9,10},{10,9},{11,12},{12,11},... | collective-permute-start | bytes 1572872 | tf_op jit(solution)/shard_map/ppermute | solution.py:460
  15.0 20.4 %collective-permute-start.4 = (f32[4,48,512]{2,1,0:T(8,128)}, f32[4,48,512]{2,1,0:T(8,128)}, u32[]{:S(2)}, u32[]{:S(2)}) collective-permute-start(f32[4,48,512]{2,1,0:T(8,128)} %dynamic-slice_bitcast_fusion.1), channel_id=1, source_target_pairs={{0,8},{8,0},{16,24},{1,9},{9,1},{17,25},{2,10},{10,2},{18,26},{3,1... | collective-permute-start | bytes 1179656 | tf_op jit(solution)/shard_map/ppermute | solution.py:471
  35.4 1.6 %copy-start.1 = (f32[1,4,256,512]{3,2,1,0:T(8,128)S(1)}, f32[1,4,256,512]{3,2,1,0:T(8,128)}, u32[]{:S(2)}) copy-start(f32[1,4,256,512]{3,2,1,0:T(8,128)} %param.5) | copy-start | bytes 6291460
  37.0 1.6 %copy-start.3 = (f32[4,256,512]{2,1,0:T(8,128)S(1)}, f32[4,256,512]{2,1,0:T(8,128)}, u32[]{:S(2)}) copy-start(f32[4,256,512]{2,1,0:T(8,128)} %initial_ref.3) | copy-start | bytes 6291460
  85.9 3.5 %collective-permute-start.5 = (f32[2,2,72,256]{3,2,1,0:T(8,128)S(1)}, f32[2,2,72,256]{3,2,1,0:T(8,128)S(1)}, u32[]{:S(2)}, u32[]{:S(2)}) collective-permute-start(f32[2,2,72,256]{3,2,1,0:T(8,128)S(1)} %get-tuple-element.33), channel_id=1, source_target_pairs={{0,1},{1,0},{2,3},{3,2},{4,5},{5,4},{6,7},{7,6},{8,9},{9,8},{10,11... | collective-permute-start | bytes 884744 | tf_op jit(solution)/shard_map/ppermute | solution.py:457
  86.0 11.2 %collective-permute-start.6 = (f32[2,2,72,256]{3,2,1,0:T(8,128)S(1)}, f32[2,2,72,256]{3,2,1,0:T(8,128)S(1)}, u32[]{:S(2)}, u32[]{:S(2)}) collective-permute-start(f32[2,2,72,256]{3,2,1,0:T(8,128)S(1)} %get-tuple-element.34), channel_id=1, source_target_pairs={{1,2},{2,1},{3,4},{4,3},{5,6},{6,5},{9,10},{10,9},{11,12},{12,11},... | collective-permute-start | bytes 884744 | tf_op jit(solution)/shard_map/ppermute | solution.py:460
  97.8 2.7 %collective-permute-start.7 = (f32[1,72,256]{2,1,0:T(8,128)S(1)}, f32[1,72,256]{2,1,0:T(8,128)S(1)}, u32[]{:S(2)}, u32[]{:S(2)}) collective-permute-start(f32[1,72,256]{2,1,0:T(8,128)S(1)} %get-tuple-element.35), channel_id=1, source_target_pairs={{0,1},{1,0},{2,3},{3,2},{4,5},{5,4},{6,7},{7,6},{8,9},{9,8},{10,11... | collective-permute-start | bytes 221192 | tf_op jit(solution)/shard_map/ppermute | solution.py:457
  97.9 6.6 %collective-permute-start.8 = (f32[1,72,256]{2,1,0:T(8,128)S(1)}, f32[1,72,256]{2,1,0:T(8,128)S(1)}, u32[]{:S(2)}, u32[]{:S(2)}) collective-permute-start(f32[1,72,256]{2,1,0:T(8,128)S(1)} %get-tuple-element.36), channel_id=1, source_target_pairs={{1,2},{2,1},{3,4},{4,3},{5,6},{6,5},{9,10},{10,9},{11,12},{12,11},... | collective-permute-start | bytes 221192 | tf_op jit(solution)/shard_map/ppermute | solution.py:460
  104.5 25.9 %copy-start.2 = (f32[1,4,256,512]{3,2,1,0:T(8,128)S(1)}, f32[1,4,256,512]{3,2,1,0:T(8,128)}, u32[]{:S(2)}) copy-start(f32[1,4,256,512]{3,2,1,0:T(8,128)} %param.5) | copy-start | bytes 6291460
  105.2 2.7 %collective-permute-start.9 = (f32[1,72,256]{2,1,0:T(8,128)S(1)}, f32[1,72,256]{2,1,0:T(8,128)S(1)}, u32[]{:S(2)}, u32[]{:S(2)}) collective-permute-start(f32[1,72,256]{2,1,0:T(8,128)S(1)} %get-tuple-element.39), channel_id=1, source_target_pairs={{0,1},{1,0},{2,3},{3,2},{4,5},{5,4},{6,7},{7,6},{8,9},{9,8},{10,11... | collective-permute-start | bytes 221192 | tf_op jit(solution)/shard_map/ppermute | solution.py:457
  105.3 6.6 %collective-permute-start.10 = (f32[1,72,256]{2,1,0:T(8,128)S(1)}, f32[1,72,256]{2,1,0:T(8,128)S(1)}, u32[]{:S(2)}, u32[]{:S(2)}) collective-permute-start(f32[1,72,256]{2,1,0:T(8,128)S(1)} %get-tuple-element.40), channel_id=1, source_target_pairs={{1,2},{2,1},{3,4},{4,3},{5,6},{6,5},{9,10},{10,9},{11,12},{12,11},... | collective-permute-start | bytes 221192 | tf_op jit(solution)/shard_map/ppermute | solution.py:460
  112.6 5.4 %collective-permute-start.11 = (f32[1,72,256]{2,1,0:T(8,128)S(1)}, f32[1,72,256]{2,1,0:T(8,128)S(1)}, u32[]{:S(2)}, u32[]{:S(2)}) collective-permute-start(f32[1,72,256]{2,1,0:T(8,128)S(1)} %get-tuple-element.42), channel_id=1, source_target_pairs={{0,1},{1,0},{2,3},{3,2},{4,5},{5,4},{6,7},{7,6},{8,9},{9,8},{10,11... | collective-permute-start | bytes 221192 | tf_op jit(solution)/shard_map/ppermute | solution.py:457
  112.7 6.6 %collective-permute-start.12 = (f32[1,72,256]{2,1,0:T(8,128)S(1)}, f32[1,72,256]{2,1,0:T(8,128)S(1)}, u32[]{:S(2)}, u32[]{:S(2)}) collective-permute-start(f32[1,72,256]{2,1,0:T(8,128)S(1)} %get-tuple-element.43), channel_id=1, source_target_pairs={{1,2},{2,1},{3,4},{4,3},{5,6},{6,5},{9,10},{10,9},{11,12},{12,11},... | collective-permute-start | bytes 221192 | tf_op jit(solution)/shard_map/ppermute | solution.py:460
  115.3 12.0 %collective-permute-start.14 = (f32[2,72,256]{2,1,0:T(8,128)S(1)}, f32[2,72,256]{2,1,0:T(8,128)S(1)}, u32[]{:S(2)}, u32[]{:S(2)}) collective-permute-start(f32[2,72,256]{2,1,0:T(8,128)S(1)} %get-tuple-element.47), channel_id=1, source_target_pairs={{0,16},{8,24},{16,0},{24,8},{1,17},{9,25},{17,1},{25,9},{2,18},{10... | collective-permute-start | bytes 442376 | tf_op jit(solution)/shard_map/ppermute | solution.py:547
  115.7 11.6 %collective-permute-start.15 = (f32[2,72,256]{2,1,0:T(8,128)S(1)}, f32[2,72,256]{2,1,0:T(8,128)S(1)}, u32[]{:S(2)}, u32[]{:S(2)}) collective-permute-start(f32[2,72,256]{2,1,0:T(8,128)S(1)} %get-tuple-element.48), channel_id=1, source_target_pairs={{0,24},{16,8},{24,16},{1,25},{17,9},{25,17},{2,26},{18,10},{26,18}... | collective-permute-start | bytes 442376 | tf_op jit(solution)/shard_map/ppermute | solution.py:547
  120.8 9.6 %collective-permute-start.13 = (f32[2,72,256]{2,1,0:T(8,128)S(1)}, f32[2,72,256]{2,1,0:T(8,128)S(1)}, u32[]{:S(2)}, u32[]{:S(2)}) collective-permute-start(f32[2,72,256]{2,1,0:T(8,128)S(1)} %get-tuple-element.46), channel_id=1, source_target_pairs={{0,8},{8,16},{16,24},{24,0},{1,9},{9,17},{17,25},{25,1},{2,10},{10... | collective-permute-start | bytes 442376 | tf_op jit(solution)/shard_map/ppermute | solution.py:547

commit v3 on v2

v3 whole, which is shorter than its diff:
```python
import functools

import jax
import jax.numpy as jnp
from jax import lax
from jax.experimental import pallas as pl
from jax.experimental.pallas import tpu as pltpu
from jax.sharding import PartitionSpec as P

STEPS = 4
courant = 0.15
GAIN = 0.5 * courant
MARGIN = 16
F32 = jnp.float32
VMEM = pltpu.VMEM
MIB = 1024 * 1024
VMEM_LIMITS = {"fine": 51 * MIB, "small": 10 * MIB, "final": 16 * MIB}


def params(limit):
    return pltpu.CompilerParams(vmem_limit_bytes=limit)


def whole(count):
    return [pl.BlockSpec(memory_space=VMEM)] * count


def shape(*dims):
    return jax.ShapeDtypeStruct(dims, F32)


def split_dot(x, selection):
    high = x.astype(jnp.bfloat16)
    rest = x - high.astype(F32)
    middle = rest.astype(jnp.bfloat16)
    low = (rest - middle.astype(F32)).astype(jnp.bfloat16)
    dot = functools.partial(jnp.dot, preferred_element_type=F32)
    return dot(high, selection) + dot(middle, selection) + dot(low, selection)


def pairing(width):
    fine = lax.broadcasted_iota(jnp.int32, (width, width // 2), 0)
    coarse = lax.broadcasted_iota(jnp.int32, (width, width // 2), 1)
    return jnp.where((fine == 2 * coarse) | (fine == 2 * coarse + 1), 1.0, 0.0).astype(jnp.bfloat16)


def spreading(width):
    coarse = lax.broadcasted_iota(jnp.int32, (width // 2, width), 0)
    fine = lax.broadcasted_iota(jnp.int32, (width // 2, width), 1)
    return jnp.where((fine == 2 * coarse) | (fine == 2 * coarse + 1), 1.0, 0.0).astype(jnp.bfloat16)


def natural_mean(first, second, rows_scr, select):
    rows = first.shape[0]
    lanes = split_dot(first + second, select)
    parts = []
    for j in range(lanes.shape[1] // 128):
        rows_scr[j, 0:rows, :] = lanes[:, 128 * j : 128 * j + 128]
        even = rows_scr[j, pl.ds(0, rows // 2, 2), :]
        odd = rows_scr[j, pl.ds(1, rows // 2, 2), :]
        parts.append(0.125 * (even + odd))
    return jnp.concatenate(parts, axis=1)


def tile(i):
    return slice(8 * i, 8 * i + 8)


def dealt_mean(load, tiles, select):
    sums = [
        (load(0, 2 * i) + load(1, 2 * i)) + (load(0, 2 * i + 1) + load(1, 2 * i + 1)) for i in range(tiles // 2)
    ]
    return 0.125 * split_dot(jnp.concatenate(sums, axis=0), select)


def weights_plane(load, store, rows, lanes):
    sub = lax.broadcasted_iota(jnp.int32, (8, 128), 0)
    lane = lax.broadcasted_iota(jnp.int32, (8, 128), 1)
    tiles, blocks = rows // 8, lanes // 128

    def cut(x):
        return [x[:, 128 * j : 128 * j + 128] for j in range(blocks)]

    c = cut(load(0, 0))
    below = [pltpu.roll(x, 1, 0) for x in cut(load(0, tiles - 1))]
    wrapped = [pltpu.roll(x, 7, 0) for x in c]
    for i in range(tiles):
        above = cut(load(0, i + 1)) if i + 1 < tiles else wrapped
        czm, czp = cut(load(-1, i)), cut(load(1, i))
        right = [pltpu.roll(x, 1, 1) for x in c]
        left = [pltpu.roll(x, 127, 1) for x in c]
        w = [[] for _ in range(7)]
        for j in range(blocks):
            mid = c[j]
            xm = mid + jnp.where(lane == 0, right[j - 1] if j else 0.0, right[j])
            xp = mid + jnp.where(lane == 127, left[j + 1] if j + 1 < blocks else 0.0, left[j])
            ym = mid + (jnp.where(sub == 0, 0.0, below[j]) if i == 0 else below[j])
            yp = mid + (jnp.where(sub == 7, 0.0, above[j]) if i + 1 == tiles else above[j])
            zm, zp = mid + czm[j], mid + czp[j]
            w[0].append(1.0 - ((xm + xp) + (ym + yp) + (zm + zp)))
            w[1].append(xm if j else jnp.where(lane == 0, 0.0, xm))
            w[2].append(xp if j + 1 < blocks else jnp.where(lane == 127, 0.0, xp))
            w[3].append(jnp.where(sub == 0, 0.0, ym) if i == 0 else ym)
            w[4].append(jnp.where(sub == 7, 0.0, yp) if i + 1 == tiles else yp)
            inside = mid > 0.0
            w[5].append(jnp.where(inside, zm, 0.0))
            w[6].append(jnp.where(inside, zp, 0.0))
        for k in range(7):
            store(k, i, jnp.concatenate(w[k], axis=1))
        below, c = c, above


def step_plane(weight, load, store, rows, lanes, fields=1):
    tiles = rows // 8
    below = [pltpu.roll(load(f, 0, tiles - 1), 1, 0) for f in range(fields)]
    center = [load(f, 0, 0) for f in range(fields)]
    wrapped = [pltpu.roll(v, 7, 0) for v in center]
    for i in range(tiles):
        w = [weight(k, i) for k in range(7)]
        for f in range(fields):
            mid = center[f]
            above = load(f, 0, i + 1) if i + 1 < tiles else wrapped[f]
            xm = pltpu.roll(mid, 1, 1)
            xp = pltpu.roll(mid, lanes - 1, 1)
            out = w[0] * mid
            out = out + (w[1] * xm + w[2] * xp)
            out = out + (w[3] * below[f] + w[4] * above)
            out = out + (w[5] * load(f, -1, i) + w[6] * load(f, 1, i))
            store(f, i, out)
            below[f], center[f] = mid, above


def at_row(value, step):
    return pl.multiple_of(value * step, 8)


def slice_kernel(c_hbm, iterate_hbm, c_ref, send_ref, sem):
    half = lax.rem(lax.axis_index("tm"), 2)
    own = send_ref.shape[1]
    window = pl.ds(at_row(half, c_hbm.shape[1] - c_ref.shape[1]), c_ref.shape[1])
    send = pltpu.make_async_copy(iterate_hbm.at[:, pl.ds(at_row(1 - half, own), own), :], send_ref, sem.at[0])
    keep = pltpu.make_async_copy(c_hbm.at[:, window, :], c_ref, sem.at[1])
    send.start()
    keep.start()
    send.wait()
    keep.wait()


def fine_kernel(planes, flag_ref, c_hbm, partner_hbm, other_hbm, iterate_hbm, initial_hbm, received_hbm,
                own_ref, to_partner_ref, to_other_ref, coarse_ref,
                c_raw, v_raw, c_scr, w_scr, a_scr, b_scr, cc_scr, keep_scr, c_sem, v_sem):
    half, upper, last = flag_ref[0], flag_ref[1], flag_ref[2]
    depth, rows, lanes = c_scr.shape
    own_rows = rows - MARGIN
    tiles = rows // 8
    columns = [slice(128 * j, 128 * j + 128) for j in range(lanes // 128)]
    select = pairing(lanes)
    coarse_planes, reach = depth // 2, planes // 2
    coarse_rows, coarse_lanes = rows // 2, lanes // 2
    last_plane = depth - 1

    slabs = ((c_hbm, planes), (partner_hbm, upper * (2 * planes)), (other_hbm, (1 - upper) * (2 * planes)))
    c_copies = [
        pltpu.make_async_copy(ref.at[:, :, column], c_raw.at[pl.ds(at, planes), j], c_sem.at[n, j])
        for n, (ref, at) in enumerate(slabs)
        for j, column in enumerate(columns)
    ]
    for copy in c_copies:
        copy.start()
    into = pl.ds(at_row(half, MARGIN), own_rows)
    source = pl.ds(at_row(half, own_rows), own_rows)

    def fetch(ref, f):
        for j in range(len(columns)):
            pltpu.make_async_copy(ref[j], v_raw.at[f, :, j, into, :], v_sem.at[f, j]).start()

    def halves(ref):
        return [ref.at[:, source, column] for column in columns]

    received = [received_hbm.at[:, :, column] for column in columns]

    first_kept = (last == 0) & (half == 0)
    first_got = (last == 0) & (half == 1)
    second_kept = (last == 1) == (half == 0)
    for f, choices in enumerate(
        (
            ((last == 1, halves(initial_hbm)), (first_kept, halves(iterate_hbm)), (first_got, received)),
            ((second_kept, halves(iterate_hbm)), (jnp.logical_not(second_kept), received)),
        )
    ):
        for condition, ref in choices:
            @pl.when(condition)
            def _():
                fetch(ref, f)

    outside = pl.ds(at_row(1 - half, own_rows), MARGIN)
    v_raw[:, :, :, outside, :] = jnp.zeros(v_raw.shape[:3] + (MARGIN, 128), F32)
    idle = jnp.zeros((2, planes) + a_scr.shape[2:], F32)
    a_scr[:, 0:planes] = idle
    a_scr[:, 2 * planes :] = idle
    b_scr[:, 0 : planes - 1] = idle[:, 1:]
    b_scr[:, 2 * planes + 1 :] = idle[:, 1:]
    for copy in c_copies:
        copy.wait()

    def deal_c(z, _):
        for j, column in enumerate(columns):
            for i in range(tiles):
                c_scr[z, tile(i), column] = GAIN * c_raw[z, j, pl.ds(i, 8, tiles), :]
        return 0

    lax.fori_loop(0, depth, deal_c, 0)

    def weigh(z, _):
        below, above = jnp.maximum(z - 1, 0), jnp.minimum(z + 1, last_plane)

        def load(dz, i):
            at = z if dz == 0 else (below if dz < 0 else above)
            return c_scr[at, tile(i), :]

        def store(k, i, w):
            w_scr[k, z, tile(i), :] = w

        weights_plane(load, store, rows, lanes)
        return 0

    lax.fori_loop(0, depth, weigh, 0)

    def restrict_c(q, _):
        cc_scr[q] = dealt_mean(lambda dz, i: c_scr[2 * q + dz, tile(i), :], tiles, select)
        return 0

    lax.fori_loop(reach - 1, 2 * reach + 1, restrict_c, 0)
    for q in range(reach):
        def load(dz, i):
            return cc_scr[reach + q + dz, tile(i), :]

        def store(k, i, w):
            coarse_ref[k, q, tile(i), :] = w

        weights_plane(load, store, coarse_rows, coarse_lanes)

    for f in range(2):
        for j in range(len(columns)):
            pltpu.make_async_copy(received[j], v_raw.at[f, :, j, into, :], v_sem.at[f, j]).wait()

    def deal_v(z, _):
        for f in range(2):
            for j, column in enumerate(columns):
                for i in range(tiles):
                    a_scr[f, planes + z, tile(i), column] = v_raw[f, z, j, pl.ds(i, 8, tiles), :]
        return 0

    lax.fori_loop(0, planes, deal_v, 0)

    def keep(n, _):
        f, q = n // reach, n % reach
        keep_scr[n] = dealt_mean(lambda dz, i: a_scr[f, planes + 2 * q + dz, tile(i), :], tiles, select)
        return 0

    lax.fori_loop(0, 2 * reach, keep, 0)
    for number in range(STEPS):
        v_in, v_out = (a_scr, b_scr) if number % 2 == 0 else (b_scr, a_scr)

        def advance(z, _):
            below, above = jnp.maximum(z - 1, 0), jnp.minimum(z + 1, last_plane)

            def load(f, dz, i):
                at = z if dz == 0 else (below if dz < 0 else above)
                return v_in[f, at, tile(i), :]

            def weight(k, i):
                return w_scr[k, z, tile(i), :]

            def store(f, i, v):
                v_out[f, z, tile(i), :] = v

            step_plane(weight, load, store, rows, lanes, 2)
            return 0

        lax.fori_loop(planes - 1 - number, 2 * planes + 1 + number, advance, 0)
    result = a_scr if STEPS % 2 == 0 else b_scr

    scale = jnp.where(last == 1, 0.0, 1.0).astype(F32)
    for q in range(reach):
        keep_scr[q] = keep_scr[q] * scale
    zero = jnp.zeros((8, coarse_lanes), F32)
    for q in range(reach):
        def load(f, dz, i):
            at = q + dz
            return zero if at < 0 or at >= reach else keep_scr[f * reach + at, tile(i), :]

        def weight(k, i):
            return coarse_ref[k, q, tile(i), :]

        def store(f, i, v):
            own_ref[f, q, tile(i), :] = v

        step_plane(weight, load, store, coarse_rows, coarse_lanes, 2)

    def mean_of(f, q):
        return dealt_mean(lambda dz, i: result[f, 2 * q + dz, tile(i), :], tiles, select)

    low_c, high_c = cc_scr[reach - 1], cc_scr[2 * reach]
    low_w = jnp.where(low_c > 0.0, low_c + cc_scr[reach], 0.0)
    high_w = jnp.where(high_c > 0.0, high_c + cc_scr[2 * reach - 1], 0.0)
    for f in range(2):
        for q in range(reach):
            own_ref[f, q] = mean_of(f, reach + q) - own_ref[f, q]
        for q in range(reach):
            low, high = mean_of(f, q), mean_of(f, 2 * reach + q)
            if q == reach - 1:
                low = low - low_w * keep_scr[f * reach]
            if q == 0:
                high = high - high_w * keep_scr[f * reach + reach - 1]

            @pl.when(upper == 1)
            def _():
                to_partner_ref[f, q] = high
                to_other_ref[f, q] = low

            @pl.when(upper == 0)
            def _():
                to_partner_ref[f, q] = low
                to_other_ref[f, q] = high


def edges(flag_ref, val, to_partner_ref, to_other_ref):
    upper = flag_ref[1]

    @pl.when(upper == 1)
    def _():
        to_partner_ref[0] = val[-1]
        to_other_ref[0] = val[0]

    @pl.when(upper == 0)
    def _():
        to_partner_ref[0] = val[0]
        to_other_ref[0] = val[-1]


def sum_kernel(flag_ref, own_ref, partner_ref, other_ref, val_ref, extra_ref, to_partner_ref, to_other_ref):
    val = own_ref[0] + partner_ref[0] + other_ref[0]
    val_ref[...] = val
    extra_ref[...] = own_ref[1] + partner_ref[1] + other_ref[1]
    edges(flag_ref, val, to_partner_ref, to_other_ref)


def chain_kernel(add_slot, send_slots, more, flag_ref, weight_ref, partner_ref, other_ref, extra_ref, *refs):
    earlier = refs[: more + 1]
    val_ref = earlier[-1]
    next_ref, to_partner_ref, to_other_ref = refs[more + 1 : more + 4]
    sends, wide = refs[more + 4 : -1], refs[-1]
    upper = flag_ref[1]
    add = flag_ref[add_slot].astype(F32)
    planes, rows, lanes = val_ref.shape
    wide[1 : planes + 1] = val_ref[...]
    wide[upper * (planes + 1)] = partner_ref[0]
    wide[(1 - upper) * (planes + 1)] = other_ref[0]
    for q in range(planes):
        def load(f, dz, i):
            return wide[1 + q + dz, tile(i), :]

        def weight(k, i):
            return weight_ref[k, q, tile(i), :]

        def store(f, i, v):
            next_ref[q, tile(i), :] = v + add * extra_ref[q, tile(i), :]

        step_plane(weight, load, store, rows, lanes)
    edges(flag_ref, next_ref[...], to_partner_ref, to_other_ref)
    for slot, ref in zip(send_slots, sends):
        which = flag_ref[slot]

        @pl.when(which < 0)
        def _():
            ref[...] = jnp.zeros(ref.shape, F32)

        for m, source in enumerate([*earlier, next_ref]):
            @pl.when(which == m)
            def _():
                ref[...] = source[...]


def final_kernel(slots, flag_ref, iterate_ref, *refs):
    count = len(slots)
    pieces, out_ref, rows_scr, fine_scr, sum_scr, error_scr = refs[:count], *refs[count:]
    planes, rows, lanes = iterate_ref.shape
    select, spread = pairing(lanes), spreading(lanes)
    piece_rows = pieces[0].shape[1]
    tiles = piece_rows // 8
    sum_scr[...] = jnp.zeros(sum_scr.shape, F32)
    for slot, ref in zip(slots, pieces):
        side = flag_ref[slot]
        sum_scr[side] = sum_scr[side] + ref[...]
    for q in range(planes // 2):
        for j in range(lanes // 256):
            column = slice(128 * j, 128 * j + 128)
            error_scr[j] = jnp.zeros(error_scr.shape[1:], F32)
            for side in range(2):
                base = side * (rows // 2 - piece_rows)
                for i in range(tiles):
                    at = pl.ds(base + i, 8, tiles)
                    error_scr[j, at, :] = error_scr[j, at, :] + sum_scr[side, q, tile(i), column]
        error = jnp.concatenate([error_scr[j] for j in range(lanes // 256)], axis=1)
        error = error - natural_mean(iterate_ref[2 * q], iterate_ref[2 * q + 1], rows_scr, select)
        wide = split_dot(error, spread)
        for j in range(lanes // 128):
            column = slice(128 * j, 128 * j + 128)
            fine_scr[j, pl.ds(0, rows // 2, 2), :] = wide[:, column]
            fine_scr[j, pl.ds(1, rows // 2, 2), :] = wide[:, column]
            for part in range(2):
                out_ref[2 * q + part, :, column] = iterate_ref[2 * q + part, :, column] + fine_scr[j]


def swap_pairs(count, first):
    pairs = []
    for i in range(first, count - 1, 2):
        pairs += [(i, i + 1), (i + 1, i)]
    return pairs


def roles(layers):
    last_group = layers // 2 - 1
    rows = []
    for t in range(layers):
        half, last = t % 2, int(t // 2 == last_group)
        adds = [int(number == (layers - 1 if last else 1)) for number in range(1, layers)]
        sends = []
        for shift in range(layers):
            k = (t + shift) % layers
            m = k if last else k - 1 - (t - half)
            sends.append(m if m >= 0 else -1)
        halves = [(t - shift) % layers % 2 for shift in range(layers)]
        rows.append([half, last, *adds, *sends, *halves])
    return rows


def local(initial, iterate, diffusivity):
    layers, slabs = lax.axis_size("tm"), lax.axis_size("space")
    t, s = lax.axis_index("tm"), lax.axis_index("space")
    planes, all_rows, lanes = initial.shape
    assert layers % 2 == 0 and slabs % 2 == 0 and planes == STEPS
    half = t % 2
    own_rows = all_rows // 2
    rows = own_rows + MARGIN
    coarse_rows, coarse_lanes = rows // 2, lanes // 2
    last_plane = depth - 1

    slabs = ((c_hbm, planes), (partner_hbm, upper * (2 * planes)), (other_hbm, (1 - upper) * (2 * planes)))
    c_copies = [
        pltpu.make_async_copy(ref.at[:, :, column], c_raw.at[pl.ds(at, planes), j], c_sem.at[n, j])
        for n, (ref, at) in enumerate(slabs)
        for j, column in enumerate(columns)
    ]
    for copy in c_copies:
        copy.start()
    into = pl.ds(at_row(half, MARGIN), own_rows)
    source = pl.ds(at_row(half, own_rows), own_rows)

    def fetch(ref, f):
        for j in range(len(columns)):
            pltpu.make_async_copy(ref[j], v_raw.at[f, :, j, into, :], v_sem.at[f, j]).start()

    def halves(ref):
        return [ref.at[:, source, column] for column in columns]

    received = [received_hbm.at[:, :, column] for column in columns]

    first_kept = (last == 0) & (half == 0)
    first_got = (last == 0) & (half == 1)
    second_kept = (last == 1) == (half == 0)
    for f, choices in enumerate(
        (
            ((last == 1, halves(initial_hbm)), (first_kept, halves(iterate_hbm)), (first_got, received)),
            ((second_kept, halves(iterate_hbm)), (jnp.logical_not(second_kept), received)),
        )
    ):
        for condition, ref in choices:
            @pl.when(condition)
            def _():
                fetch(ref, f)

    outside = pl.ds(at_row(1 - half, own_rows), MARGIN)
    v_raw[:, :, :, outside, :] = jnp.zeros(v_raw.shape[:3] + (MARGIN, 128), F32)
    idle = jnp.zeros((2, planes) + a_scr.shape[2:], F32)
    a_scr[:, 0:planes] = idle
    a_scr[:, 2 * planes :] = idle
    b_scr[:, 0 : planes - 1] = idle[:, 1:]
    b_scr[:, 2 * planes + 1 :] = idle[:, 1:]
    for copy in c_copies:
        copy.wait()

    def deal_c(z, _):
        for j, column in enumerate(columns):
            for i in range(tiles):
                c_scr[z, tile(i), column] = GAIN * c_raw[z, j, pl.ds(i, 8, tiles), :]
        return 0

    lax.fori_loop(0, depth, deal_c, 0)

    def weigh(z, _):
        below, above = jnp.maximum(z - 1, 0), jnp.minimum(z + 1, last_plane)

        def load(dz, i):
            at = z if dz == 0 else (below if dz < 0 else above)
            return c_scr[at, tile(i), :]

        def store(k, i, w):
            w_scr[k, z, tile(i), :] = w

        weights_plane(load, store, rows, lanes)
        return 0

    lax.fori_loop(0, depth, weigh, 0)

    def restrict_c(q, _):
        cc_scr[q] = dealt_mean(lambda dz, i: c_scr[2 * q + dz, tile(i), :], tiles, select)
        return 0

    lax.fori_loop(reach - 1, 2 * reach + 1, restrict_c, 0)
    for q in range(reach):
        def load(dz, i):
            return cc_scr[reach + q + dz, tile(i), :]

        def store(k, i, w):
            coarse_ref[k, q, tile(i), :] = w

        weights_plane(load, store, coarse_rows, coarse_lanes)

    for f in range(2):
        for j in range(len(columns)):
            pltpu.make_async_copy(received[j], v_raw.at[f, :, j, into, :], v_sem.at[f, j]).wait()

    def deal_v(z, _):
        for f in range(2):
            for j, column in enumerate(columns):
                for i in range(tiles):
                    a_scr[f, planes + z, tile(i), column] = v_raw[f, z, j, pl.ds(i, 8, tiles), :]
        return 0

    lax.fori_loop(0, planes, deal_v, 0)

    def keep(n, _):
        f, q = n // reach, n % reach
        keep_scr[n] = dealt_mean(lambda dz, i: a_scr[f, planes + 2 * q + dz, tile(i), :], tiles, select)
        return 0

    lax.fori_loop(0, 2 * reach, keep, 0)
    for number in range(STEPS):
        v_in, v_out = (a_scr, b_scr) if number % 2 == 0 else (b_scr, a_scr)

        def advance(z, _):
            below, above = jnp.maximum(z - 1, 0), jnp.minimum(z + 1, last_plane)

            def load(f, dz, i):
                at = z if dz == 0 else (below if dz < 0 else above)
                return v_in[f, at, tile(i), :]

            def weight(k, i):
                return w_scr[k, z, tile(i), :]

            def store(f, i, v):
                v_out[f, z, tile(i), :] = v

            step_plane(weight, load, store, rows, lanes, 2)
            return 0

        lax.fori_loop(planes - 1 - number, 2 * planes + 1 + number, advance, 0)
    result = a_scr if STEPS % 2 == 0 else b_scr

    scale = jnp.where(last == 1, 0.0, 1.0).astype(F32)
    for q in range(reach):
        keep_scr[q] = keep_scr[q] * scale
    zero = jnp.zeros((8, coarse_lanes), F32)
    for q in range(reach):
        def load(f, dz, i):
            at = q + dz
            return zero if at < 0 or at >= reach else keep_scr[f * reach + at, tile(i), :]

        def weight(k, i):
            return coarse_ref[k, q, tile(i), :]

        def store(f, i, v):
            own_ref[f, q, tile(i), :] = v

        step_plane(weight, load, store, coarse_rows, coarse_lanes, 2)

    def mean_of(f, q):
        return dealt_mean(lambda dz, i: result[f, 2 * q + dz, tile(i), :], tiles, select)

    low_c, high_c = cc_scr[reach - 1], cc_scr[2 * reach]
    low_w = jnp.where(low_c > 0.0, low_c + cc_scr[reach], 0.0)
    high_w = jnp.where(high_c > 0.0, high_c + cc_scr[2 * reach - 1], 0.0)
    for f in range(2):
        for q in range(reach):
            own_ref[f, q] = mean_of(f, reach + q) - own_ref[f, q]
        for q in range(reach):
            low, high = mean_of(f, q), mean_of(f, 2 * reach + q)
            if q == reach - 1:
                low = low - low_w * keep_scr[f * reach]
            if q == 0:
                high = high - high_w * keep_scr[f * reach + reach - 1]

            @pl.when(upper == 1)
            def _():
                to_partner_ref[f, q] = high
                to_other_ref[f, q] = low

            @pl.when(upper == 0)
            def _():
                to_partner_ref[f, q] = low
                to_other_ref[f, q] = high


def edges(flag_ref, val, to_partner_ref, to_other_ref):
    upper = flag_ref[1]

    @pl.when(upper == 1)
    def _():
        to_partner_ref[0] = val[-1]
        to_other_ref[0] = val[0]

    @pl.when(upper == 0)
    def _():
        to_partner_ref[0] = val[0]
        to_other_ref[0] = val[-1]


def sum_kernel(flag_ref, own_ref, partner_ref, other_ref, val_ref, extra_ref, to_partner_ref, to_other_ref):
    val = own_ref[0] + partner_ref[0] + other_ref[0]
    val_ref[...] = val
    extra_ref[...] = own_ref[1] + partner_ref[1] + other_ref[1]
    edges(flag_ref, val, to_partner_ref, to_other_ref)


def chain_kernel(add_slot, send_slots, more, flag_ref, weight_ref, partner_ref, other_ref, extra_ref, *refs):
    earlier = refs[: more + 1]
    val_ref = earlier[-1]
    next_ref, to_partner_ref, to_other_ref = refs[more + 1 : more + 4]
    sends, wide = refs[more + 4 : -1], refs[-1]
    upper = flag_ref[1]
    add = flag_ref[add_slot].astype(F32)
    planes, rows, lanes = val_ref.shape
    wide[1 : planes + 1] = val_ref[...]
    wide[upper * (planes + 1)] = partner_ref[0]
    wide[(1 - upper) * (planes + 1)] = other_ref[0]
    for q in range(planes):
        def load(f, dz, i):
            return wide[1 + q + dz, tile(i), :]

        def weight(k, i):
            return weight_ref[k, q, tile(i), :]

        def store(f, i, v):
            next_ref[q, tile(i), :] = v + add * extra_ref[q, tile(i), :]

        step_plane(weight, load, store, rows, lanes)
    edges(flag_ref, next_ref[...], to_partner_ref, to_other_ref)
    for slot, ref in zip(send_slots, sends):
        which = flag_ref[slot]

        @pl.when(which < 0)
        def _():
            ref[...] = jnp.zeros(ref.shape, F32)

        for m, source in enumerate([*earlier, next_ref]):
            @pl.when(which == m)
            def _():
                ref[...] = source[...]


def final_kernel(slots, flag_ref, iterate_ref, *refs):
    count = len(slots)
    pieces, out_ref, rows_scr, fine_scr, sum_scr, error_scr = refs[:count], *refs[count:]
    planes, rows, lanes = iterate_ref.shape
    select, spread = pairing(lanes), spreading(lanes)
    piece_rows = pieces[0].shape[1]
    tiles = piece_rows // 8
    sum_scr[...] = jnp.zeros(sum_scr.shape, F32)
    for slot, ref in zip(slots, pieces):
        side = flag_ref[slot]
        sum_scr[side] = sum_scr[side] + ref[...]
    for q in range(planes // 2):
        for j in range(lanes // 256):
            column = slice(128 * j, 128 * j + 128)
            error_scr[j] = jnp.zeros(error_scr.shape[1:], F32)
            for side in range(2):
                base = side * (rows // 2 - piece_rows)
                for i in range(tiles):
                    at = pl.ds(base + i, 8, tiles)
                    error_scr[j, at, :] = error_scr[j, at, :] + sum_scr[side, q, tile(i), column]
        error = jnp.concatenate([error_scr[j] for j in range(lanes // 256)], axis=1)
        error = error - natural_mean(iterate_ref[2 * q], iterate_ref[2 * q + 1], rows_scr, select)
        wide = split_dot(error, spread)
        for j in range(lanes // 128):
            column = slice(128 * j, 128 * j + 128)
            fine_scr[j, pl.ds(0, rows // 2, 2), :] = wide[:, column]
            fine_scr[j, pl.ds(1, rows // 2, 2), :] = wide[:, column]
            for part in range(2):
                out_ref[2 * q + part, :, column] = iterate_ref[2 * q + part, :, column] + fine_scr[j]


def swap_pairs(count, first):
    pairs = []
    for i in range(first, count - 1, 2):
        pairs += [(i, i + 1), (i + 1, i)]
    return pairs


def roles(layers):
    last_group = layers // 2 - 1
    rows = []
    for t in range(layers):
        half, last = t % 2, int(t // 2 == last_group)
        adds = [int(number == (layers - 1 if last else 1)) for number in range(1, layers)]
        sends = []
        for shift in range(layers):
            k = (t + shift) % layers
            m = k if last else k - 1 - (t - half)
            sends.append(m if m >= 0 else -1)
        halves = [(t - shift) % layers % 2 for shift in range(layers)]
        rows.append([half, last, *adds, *sends, *halves])
    return rows


def local(initial, iterate, diffusivity):
    layers, slabs = lax.axis_size("tm"), lax.axis_size("space")
    t, s = lax.axis_index("tm"), lax.axis_index("space")
    planes, all_rows, lanes = initial.shape
    assert layers % 2 == 0 and slabs % 2 == 0 and planes == STEPS
    half = t % 2
    own_rows = all_rows // 2
    rows = own_rows + MARGIN
    inner_own = (3 * own_rows // 8) // 16 * 16
    outer_own = own_rows - inner_own
    inner_rows, outer_rows = inner_own + 2 * MARGIN, outer_own + MARGIN
    coarse_rows, coarse_lanes = rows // 2, lanes // 2
    reach = planes // 2
    upper = 1 - s % 2
    field = iterate[0]

    def partner_swap(x):
        return lax.ppermute(x, "space", swap_pairs(slabs, 0))

    def other_swap(x):
        return lax.ppermute(x, "space", swap_pairs(slabs, 1))

    anywhere = pl.BlockSpec(memory_space=pl.ANY)
    in_hbm = pl.BlockSpec(memory_space=pltpu.HBM)
    c, to_row_partner = pl.pallas_call(
        slice_kernel,
        out_shape=(shape(planes, rows, lanes), shape(planes, own_rows, lanes)),
        in_specs=[in_hbm] * 2,
        out_specs=tuple(whole(2)),
        scratch_shapes=[pltpu.SemaphoreType.DMA((2,))],
        compiler_params=params(VMEM_LIMITS["small"]),
        name="slices",
    )(diffusivity, field)
    row_pairs = swap_pairs(layers, 0)
    row_pairs.remove((layers - 1, layers - 2))
    received = lax.ppermute(to_row_partner, "tm", row_pairs)
    c_other = other_swap(c)
    c_partner = partner_swap(c)

    table = roles(layers)
    mine = jnp.asarray(table, jnp.int32)[t]
    flags = jnp.concatenate([mine[:1], jnp.reshape(upper, (1,)).astype(jnp.int32), mine[1:]])
    add_at, send_at, half_at = 3, 2 + layers, 2 + 2 * layers
    smem = pl.BlockSpec(memory_space=pltpu.SMEM)

    fields = shape(2, reach, coarse_rows, coarse_lanes)
    blocks = lanes // 128
    own, to_partner, to_other, weights = pl.pallas_call(
        functools.partial(fine_kernel, planes),
        out_shape=(fields, fields, fields, shape(7, reach, coarse_rows, coarse_lanes)),
        in_specs=[smem] + [anywhere] * 3 + [in_hbm] * 2 + [anywhere],
        out_specs=tuple(whole(4)),
        scratch_shapes=[
            VMEM((3 * planes, blocks, rows, 128), F32),
            VMEM((2, planes, blocks, rows, 128), F32),
            VMEM((3 * planes, rows, lanes), F32),
            VMEM((7, 3 * planes, rows, lanes), F32),
            VMEM((2, 3 * planes, rows, lanes), F32),
            VMEM((2, 3 * planes, rows, lanes), F32),
            VMEM((3 * reach, coarse_rows, coarse_lanes), F32),
            VMEM((2 * reach, coarse_rows, coarse_lanes), F32),
            pltpu.SemaphoreType.DMA((3, blocks)),
            pltpu.SemaphoreType.DMA((2, blocks)),
        ],
        compiler_params=params(VMEM_LIMITS["fine"]),
        name="fine",
    )(flags, c, c_partner, c_other, field, initial, received)

    from_other = other_swap(to_other)
    from_partner = partner_swap(to_partner)
    plane = shape(1, coarse_rows, coarse_lanes)
    block = shape(reach, coarse_rows, coarse_lanes)
    val, extra, to_partner, to_other = pl.pallas_call(
        sum_kernel,
        out_shape=(block, block, plane, plane),
        in_specs=[smem] + whole(3),
        out_specs=tuple(whole(4)),
        compiler_params=params(VMEM_LIMITS["small"]),
        name="gather",
    )(flags, own, from_partner, from_other)

    ready = [max(row[1 + layers + shift] for row in table) for shift in range(layers)]
    arrived = [None] * layers
    values = [val]
    for number in range(1, layers):
        from_other = other_swap(to_other)
        from_partner = partner_swap(to_partner)
        shifts = [shift for shift in range(layers) if max(ready[shift], 1) == number]
        earlier = values if shifts else values[-1:]
        val, to_partner, to_other, *sends = pl.pallas_call(
            functools.partial(chain_kernel, add_at + number - 1, [send_at + shift for shift in shifts], len(earlier) - 1),
            out_shape=(block, plane, plane, *[block] * len(shifts)),
            in_specs=[smem] + whole(4 + len(earlier)),
            out_specs=tuple(whole(3 + len(shifts))),
            scratch_shapes=[VMEM((reach + 2, coarse_rows, coarse_lanes), F32)],
            compiler_params=params(VMEM_LIMITS["small"]),
            name=f"chain{number}",
        )(flags, weights, from_partner, from_other, extra, *earlier)
        values.append(val)
        for shift, send in zip(shifts, sends):
            pairs = [
                (source, (source + shift) % layers)
                for source in range(layers)
                if table[source][1 + layers + shift] >= 0
            ]
            arrived[shift] = lax.ppermute(send, "tm", pairs) if shift else send

    corrected = pl.pallas_call(
        functools.partial(final_kernel, [half_at + shift for shift in range(layers)]),
        out_shape=shape(planes, all_rows, lanes),
        in_specs=[smem] + whole(1 + layers),
        out_specs=pl.BlockSpec(memory_space=VMEM),
        scratch_shapes=[
            VMEM((coarse_lanes // 128, all_rows, 128), F32),
            VMEM((lanes // 128, all_rows, 128), F32),
            VMEM((2, reach, coarse_rows, coarse_lanes), F32),
            VMEM((coarse_lanes // 128, all_rows // 2, 128), F32),
        ],
        compiler_params=params(VMEM_LIMITS["final"]),
        name="final",
    )(flags, field, *arrived)
    return corrected[None]


def solution(mesh):
    placed = (P("space", None, None), P("tm", "space", None, None), P("space", None, None))
    return jax.shard_map(
        local, mesh=mesh, in_specs=placed, out_specs=P("tm", "space", None, None), check_vma=False
    )
```

time: 135 us -> 110 us (0.81)
  Pallas kernels: 54.7 us -> 32.5 us
  local copies, waits for them, and re-layouts: 11.1 us -> 3.96 us
  waiting for transfers between devices: 42.7 us -> 49.6 us
  starting transfers between devices: 25.4 us -> 22 us
    pallas_call x2, Pallas kernels: 47.2 us -> 25.2 us  [the longest x1 25 us: local(): pl.pallas_call(functools.partial(fine_kernel, planes), out_shape=(fields,...]
    ppermute x2 -> x1, waiting for transfers between devices: 18.2 us -> 24.8 us  [local(): received = lax.ppermute(to_row_partner, 'tm', row_pairs)]
    dynamic_slice x5 -> x0, local copies, waits for them, and re-layouts: 5.56 us -> none  [rows_of(): return lax.dynamic_slice_in_dim(x, start, count, axis=1)]
    ppermute x6 -> x5, starting transfers between devices: 17.6 us -> 14.5 us  [other_swap(): return lax.ppermute(x, 'space', swap_pairs(slabs, 1))]
    unnamed x8, local copies, waits for them, and re-layouts: 4.78 us -> 3.19 us
    ppermute x6 -> x5, waiting for transfers between devices: 17 us -> 16.9 us  [other_swap(): return lax.ppermute(x, 'space', swap_pairs(slabs, 1))]
  transfers between devices with their start and end apart: 16 -> 14, of which waited for: 7 -> 7; matrix products, arithmetic and copies ran while one was open for 5% -> 1% of each run, Pallas kernels for 17% -> 1%
where the time goes in v3:
time: 110 us; the launch traced here: 108 us
  waiting for transfers between devices  49.6 us (45%)
  Pallas kernels  32.5 us (30%)
  starting transfers between devices  22 us (20%)
  local copies, waits for them, and re-layouts  3.96 us (4%)
    pallas_call x1, Pallas kernels, local(): pl.pallas_call(functools.partial(fine_kernel, planes), out_shape=(fields,...  25 us
    ppermute x1, waiting for transfers between devices, local(): received = lax.ppermute(to_row_partner, 'tm', row_pairs)  24.8 us
    ppermute x5, waiting for transfers between devices, other_swap(): return lax.ppermute(x, 'space', swap_pairs(slabs, 1))  16.9 us
    ppermute x5, starting transfers between devices, other_swap(): return lax.ppermute(x, 'space', swap_pairs(slabs, 1))  14.5 us
    ppermute x3, waiting for transfers between devices, local(): arrived[shift] = lax.ppermute(send, 'tm', pairs) if shift else send  7.82 us
    ppermute x3, starting transfers between devices, local(): arrived[shift] = lax.ppermute(send, 'tm', pairs) if shift else send  5.14 us
    pallas_call x1, Pallas kernels, local(): pl.pallas_call(functools.partial(final_kernel, [half_at + shift for shift...  3.75 us
    unnamed x8, local copies, waits for them, and re-layouts  3.19 us
  transfers between devices with their start and end apart: 14, of which 7 were waited for; matrix products, arithmetic and copies ran while one was open for 1% of the time, Pallas kernels for 1%

profile of v3, /device:TPU:28, one launch (start us, length us, event | category | flops | bytes accessed | tf_op | source)
XLA Modules:
  0.0 108.4 jit_solution(8931506102990655904)
XLA Ops:
  0.0 0.0 copy-start
  0.0 1.6 %copy-done = f32[1,4,256,512]{3,2,1,0:T(8,128)S(1)} copy-done((f32[1,4,256,512]{3,2,1,0:T(8,128)S(1)}, f32[1,4,256,512]{3,2,1,0:T(8,128)}, u32[]{:S(2)}) %copy-start) | copy-done | bytes 2097176
  1.6 0.0 copy-start.2
  1.6 1.6 %copy-done.2 = f32[4,256,512]{2,1,0:T(8,128)S(1)} copy-done((f32[4,256,512]{2,1,0:T(8,128)S(1)}, f32[4,256,512]{2,1,0:T(8,128)}, u32[]{:S(2)}) %copy-start.2) | copy-done | bytes 2097176
  3.2 0.2 slices.1
  3.4 0.0 copy-start.3
  3.4 2.8 %collective-permute-start.1 = (f32[4,144,512]{2,1,0:T(8,128)S(1)}, f32[4,144,512]{2,1,0:T(8,128)}, u32[]{:S(2)}, u32[]{:S(2)}) collective-permute-start(f32[4,144,512]{2,1,0:T(8,128)S(1)} %get-tuple-element.25.c_hbm), channel_id=1, source_target_pairs={{1,2},{2,1},{3,4},{4,3},{5,6},{6,5},{9,10},{10,9},{11,12},{12,11},... | collective-permute-start | bytes 3538952 | tf_op jit(solution)/shard_map/ppermute | solution.py:747
  6.2 0.8 collective-permute-start
  7.0 1.3 %collective-permute-start.2 = (f32[4,128,512]{2,1,0:T(8,128)S(1)}, f32[4,128,512]{2,1,0:T(8,128)S(1)}, u32[]{:S(2)}, u32[]{:S(2)}) collective-permute-start(f32[4,128,512]{2,1,0:T(8,128)S(1)} %get-tuple-element.26), channel_id=1, source_target_pairs={{0,8},{8,0},{16,24},{1,9},{9,1},{17,25},{2,10},{10,2},{18,26},{3,1... | collective-permute-start | bytes 3145736 | tf_op jit(solution)/shard_map/ppermute | solution.py:762
  8.3 0.7 constant_dynamic-slice_fusion
  9.0 0.1 slice_bitcast_fusion
  9.1 0.1 pad_add_fusion.flag_ref
  9.2 24.8 %collective-permute-done.2.received_hbm = f32[4,128,512]{2,1,0:T(8,128)S(1)} collective-permute-done((f32[4,128,512]{2,1,0:T(8,128)S(1)}, f32[4,128,512]{2,1,0:T(8,128)S(1)}, u32[]{:S(2)}, u32[]{:S(2)}) %collective-permute-start.2) | collective-permute-done | bytes 1048608 | tf_op jit(solution)/shard_map/ppermute | solution.py:762
  34.0 0.0 collective-permute-done.1.other_hbm
  34.0 0.0 collective-permute-done.partner_hbm
  34.0 0.0 copy-done.3
  34.0 25.0 %fine.1 = (f32[2,2,72,256]{3,2,1,0:T(8,128)S(1)}, f32[2,2,72,256]{3,2,1,0:T(8,128)S(1)}, f32[2,2,72,256]{3,2,1,0:T(8,128)S(1)}, f32[7,2,72,256]{3,2,1,0:T(8,128)S(1)}) custom-call(s32[14]{0:T(128)S(1)} %pad_add_fusion.flag_ref, f32[4,144,512]{2,1,0:T(8,128)} %copy-done.3, f32[4,144,512]{2,1,0:T(8,128)} %collective-permute-done.partner_hbm, ...), custom_call_target="tpu_custom_call" | custom-call | tf_op jit(solution)/shard_map/fine/pallas_call | solution.py:774
  58.9 0.1 collective-permute-start.3
  59.0 3.4 %collective-permute-start.4 = (f32[2,2,72,256]{3,2,1,0:T(8,128)S(1)}, f32[2,2,72,256]{3,2,1,0:T(8,128)S(1)}, u32[]{:S(2)}, u32[]{:S(2)}) collective-permute-start(f32[2,2,72,256]{3,2,1,0:T(8,128)S(1)} %get-tuple-element.30), channel_id=1, source_target_pairs={{1,2},{2,1},{3,4},{4,3},{5,6},{6,5},{9,10},{10,9},{11,12},{12,11},... | collective-permute-start | bytes 884744 | tf_op jit(solution)/shard_map/ppermute | solution.py:747
  62.5 0.0 collective-permute-done.3.partner_ref
  62.5 8.4 %collective-permute-done.4.other_ref = f32[2,2,72,256]{3,2,1,0:T(8,128)S(1)} collective-permute-done((f32[2,2,72,256]{3,2,1,0:T(8,128)S(1)}, f32[2,2,72,256]{3,2,1,0:T(8,128)S(1)}, u32[]{:S(2)}, u32[]{:S(2)}) %collective-permute-start.4) | collective-permute-done | bytes 294944 | tf_op jit(solution)/shard_map/ppermute | solution.py:747
  70.8 0.6 gather.1
  71.4 0.1 collective-permute-start.5
  71.5 2.8 %collective-permute-start.6 = (f32[1,72,256]{2,1,0:T(8,128)S(1)}, f32[1,72,256]{2,1,0:T(8,128)S(1)}, u32[]{:S(2)}, u32[]{:S(2)}) collective-permute-start(f32[1,72,256]{2,1,0:T(8,128)S(1)} %get-tuple-element.32), channel_id=1, source_target_pairs={{1,2},{2,1},{3,4},{4,3},{5,6},{6,5},{9,10},{10,9},{11,12},{12,11},... | collective-permute-start | bytes 221192 | tf_op jit(solution)/shard_map/ppermute | solution.py:747
  74.3 0.0 collective-permute-done.5.partner_ref
  74.3 3.8 %collective-permute-done.6.other_ref = f32[1,72,256]{2,1,0:T(8,128)S(1)} collective-permute-done((f32[1,72,256]{2,1,0:T(8,128)S(1)}, f32[1,72,256]{2,1,0:T(8,128)S(1)}, u32[]{:S(2)}, u32[]{:S(2)}) %collective-permute-start.6) | collective-permute-done | bytes 73760 | tf_op jit(solution)/shard_map/ppermute | solution.py:747
  78.1 0.0 copy-start.1
  78.1 0.7 chain1.1
  78.8 0.1 collective-permute-start.7
  78.9 2.8 %collective-permute-start.8 = (f32[1,72,256]{2,1,0:T(8,128)S(1)}, f32[1,72,256]{2,1,0:T(8,128)S(1)}, u32[]{:S(2)}, u32[]{:S(2)}) collective-permute-start(f32[1,72,256]{2,1,0:T(8,128)S(1)} %get-tuple-element.36), channel_id=1, source_target_pairs={{1,2},{2,1},{3,4},{4,3},{5,6},{6,5},{9,10},{10,9},{11,12},{12,11},... | collective-permute-start | bytes 221192 | tf_op jit(solution)/shard_map/ppermute | solution.py:747
  81.7 0.0 collective-permute-done.7.partner_ref
  81.7 3.8 %collective-permute-done.8.other_ref = f32[1,72,256]{2,1,0:T(8,128)S(1)} collective-permute-done((f32[1,72,256]{2,1,0:T(8,128)S(1)}, f32[1,72,256]{2,1,0:T(8,128)S(1)}, u32[]{:S(2)}, u32[]{:S(2)}) %collective-permute-start.8) | collective-permute-done | bytes 73760 | tf_op jit(solution)/shard_map/ppermute | solution.py:747
  85.5 0.8 chain2.1
  86.3 0.1 collective-permute-start.9
  86.4 2.8 %collective-permute-start.10 = (f32[1,72,256]{2,1,0:T(8,128)S(1)}, f32[1,72,256]{2,1,0:T(8,128)S(1)}, u32[]{:S(2)}, u32[]{:S(2)}) collective-permute-start(f32[1,72,256]{2,1,0:T(8,128)S(1)} %get-tuple-element.39), channel_id=1, source_target_pairs={{1,2},{2,1},{3,4},{4,3},{5,6},{6,5},{9,10},{10,9},{11,12},{12,11},... | collective-permute-start | bytes 221192 | tf_op jit(solution)/shard_map/ppermute | solution.py:747
  89.2 0.4 collective-permute-start.12
  89.6 2.3 %collective-permute-start.13 = (f32[2,72,256]{2,1,0:T(8,128)S(1)}, f32[2,72,256]{2,1,0:T(8,128)S(1)}, u32[]{:S(2)}, u32[]{:S(2)}) collective-permute-start(f32[2,72,256]{2,1,0:T(8,128)S(1)} %get-tuple-element.44), channel_id=1, source_target_pairs={{0,24},{16,8},{24,16},{1,25},{17,9},{25,17},{2,26},{18,10},{26,18}... | collective-permute-start | bytes 442376 | tf_op jit(solution)/shard_map/ppermute | solution.py:832
  91.9 0.0 collective-permute-done.9.partner_ref
  91.9 1.0 collective-permute-done.10.other_ref
  92.9 1.5 %chain3.1 = (f32[2,72,256]{2,1,0:T(8,128)}, f32[1,72,256]{2,1,0:T(8,128)}, f32[1,72,256]{2,1,0:T(8,128)}, f32[2,72,256]{2,1,0:T(8,128)S(1)}, f32[2,72,256]{2,1,0:T(8,128)S(1)}) custom-call(s32[14]{0:T(128)S(1)} %pad_add_fusion.flag_ref, f32[7,2,72,256]{3,2,1,0:T(8,128)S(1)} %get-tuple-element.27.weight_ref, ...), custom_call_target="tpu_custom_call" | custom-call | tf_op jit(solution)/shard_map/chain3/pallas_call | solution.py:816
  94.4 2.4 %collective-permute-start.11 = (f32[2,72,256]{2,1,0:T(8,128)S(1)}, f32[2,72,256]{2,1,0:T(8,128)S(1)}, u32[]{:S(2)}, u32[]{:S(2)}) collective-permute-start(f32[2,72,256]{2,1,0:T(8,128)S(1)} %get-tuple-element.42), channel_id=1, source_target_pairs={{0,8},{8,16},{16,24},{24,0},{1,9},{9,17},{17,25},{25,1},{2,10},{10... | collective-permute-start | bytes 442376 | tf_op jit(solution)/shard_map/ppermute | solution.py:832
  96.8 4.8 %collective-permute-done.12.refs_2_ = f32[2,72,256]{2,1,0:T(8,128)S(1)} collective-permute-done((f32[2,72,256]{2,1,0:T(8,128)S(1)}, f32[2,72,256]{2,1,0:T(8,128)S(1)}, u32[]{:S(2)}, u32[]{:S(2)}) %collective-permute-start.12) | collective-permute-done | bytes 147488 | tf_op jit(solution)/shard_map/ppermute | solution.py:832
  101.6 0.0 collective-permute-done.13.refs_3_
  101.6 3.0 %collective-permute-done.11.refs_1_ = f32[2,72,256]{2,1,0:T(8,128)S(1)} collective-permute-done((f32[2,72,256]{2,1,0:T(8,128)S(1)}, f32[2,72,256]{2,1,0:T(8,128)S(1)}, u32[]{:S(2)}, u32[]{:S(2)}) %collective-permute-start.11) | collective-permute-done | bytes 147488 | tf_op jit(solution)/shard_map/ppermute | solution.py:832
  104.6 0.0 copy-done.1
  104.6 3.7 %final.1 = f32[4,256,512]{2,1,0:T(8,128)} custom-call(s32[14]{0:T(128)S(1)} %pad_add_fusion.flag_ref, f32[4,256,512]{2,1,0:T(8,128)S(1)} %bitcast.9, f32[2,72,256]{2,1,0:T(8,128)S(1)} %get-tuple-element.41.refs_0_, f32[2,72,256]{2,1,0:T(8,128)S(1)} %collective-permute-done.11.refs_1_, f32[2,72,256]{2,1,0:T(8,128)S(1)} %collective-permute-done.12.refs_2_, ...), custom_call_target="tpu_custom_call" | custom-call | tf_op jit(solution)/shard_map/final/pallas_call | solution.py:834
Async XLA Ops:
  0.0 1.6 %copy-start = (f32[1,4,256,512]{3,2,1,0:T(8,128)S(1)}, f32[1,4,256,512]{3,2,1,0:T(8,128)}, u32[]{:S(2)}) copy-start(f32[1,4,256,512]{3,2,1,0:T(8,128)} %param.5) | copy-start | bytes 6291460
  1.6 1.6 %copy-start.2 = (f32[4,256,512]{2,1,0:T(8,128)S(1)}, f32[4,256,512]{2,1,0:T(8,128)}, u32[]{:S(2)}) copy-start(f32[4,256,512]{2,1,0:T(8,128)} %c_hbm.1) | copy-start | bytes 6291460
  3.4 30.6 %copy-start.3 = (f32[4,144,512]{2,1,0:T(8,128)}, f32[4,144,512]{2,1,0:T(8,128)S(1)}, u32[]{:S(2)}) copy-start(f32[4,144,512]{2,1,0:T(8,128)S(1)} %get-tuple-element.25.c_hbm) | copy-start | bytes 3538948
  3.4 30.6 %collective-permute-start.1 = (f32[4,144,512]{2,1,0:T(8,128)S(1)}, f32[4,144,512]{2,1,0:T(8,128)}, u32[]{:S(2)}, u32[]{:S(2)}) collective-permute-start(f32[4,144,512]{2,1,0:T(8,128)S(1)} %get-tuple-element.25.c_hbm), channel_id=1, source_target_pairs={{1,2},{2,1},{3,4},{4,3},{5,6},{6,5},{9,10},{10,9},{11,12},{12,11},... | collective-permute-start | bytes 3538952 | tf_op jit(solution)/shard_map/ppermute | solution.py:747
  6.2 27.8 %collective-permute-start = (f32[4,144,512]{2,1,0:T(8,128)S(1)}, f32[4,144,512]{2,1,0:T(8,128)}, u32[]{:S(2)}, u32[]{:S(2)}) collective-permute-start(f32[4,144,512]{2,1,0:T(8,128)S(1)} %get-tuple-element.25.c_hbm), channel_id=1, source_target_pairs={{0,1},{1,0},{2,3},{3,2},{4,5},{5,4},{6,7},{7,6},{8,9},{9,8},{10,11... | collective-permute-start | bytes 3538952 | tf_op jit(solution)/shard_map/ppermute | solution.py:744
  7.0 27.0 %collective-permute-start.2 = (f32[4,128,512]{2,1,0:T(8,128)S(1)}, f32[4,128,512]{2,1,0:T(8,128)S(1)}, u32[]{:S(2)}, u32[]{:S(2)}) collective-permute-start(f32[4,128,512]{2,1,0:T(8,128)S(1)} %get-tuple-element.26), channel_id=1, source_target_pairs={{0,8},{8,0},{16,24},{1,9},{9,1},{17,25},{2,10},{10,2},{18,26},{3,1... | collective-permute-start | bytes 3145736 | tf_op jit(solution)/shard_map/ppermute | solution.py:762
  58.9 3.5 %collective-permute-start.3 = (f32[2,2,72,256]{3,2,1,0:T(8,128)S(1)}, f32[2,2,72,256]{3,2,1,0:T(8,128)S(1)}, u32[]{:S(2)}, u32[]{:S(2)}) collective-permute-start(f32[2,2,72,256]{3,2,1,0:T(8,128)S(1)} %get-tuple-element.29), channel_id=1, source_target_pairs={{0,1},{1,0},{2,3},{3,2},{4,5},{5,4},{6,7},{7,6},{8,9},{9,8},{10,11... | collective-permute-start | bytes 884744 | tf_op jit(solution)/shard_map/ppermute | solution.py:744
  59.0 11.8 %collective-permute-start.4 = (f32[2,2,72,256]{3,2,1,0:T(8,128)S(1)}, f32[2,2,72,256]{3,2,1,0:T(8,128)S(1)}, u32[]{:S(2)}, u32[]{:S(2)}) collective-permute-start(f32[2,2,72,256]{3,2,1,0:T(8,128)S(1)} %get-tuple-element.30), channel_id=1, source_target_pairs={{1,2},{2,1},{3,4},{4,3},{5,6},{6,5},{9,10},{10,9},{11,12},{12,11},... | collective-permute-start | bytes 884744 | tf_op jit(solution)/shard_map/ppermute | solution.py:747
  71.4 2.9 %collective-permute-start.5 = (f32[1,72,256]{2,1,0:T(8,128)S(1)}, f32[1,72,256]{2,1,0:T(8,128)S(1)}, u32[]{:S(2)}, u32[]{:S(2)}) collective-permute-start(f32[1,72,256]{2,1,0:T(8,128)S(1)} %get-tuple-element.31), channel_id=1, source_target_pairs={{0,1},{1,0},{2,3},{3,2},{4,5},{5,4},{6,7},{7,6},{8,9},{9,8},{10,11... | collective-permute-start | bytes 221192 | tf_op jit(solution)/shard_map/ppermute | solution.py:744
  71.5 6.6 %collective-permute-start.6 = (f32[1,72,256]{2,1,0:T(8,128)S(1)}, f32[1,72,256]{2,1,0:T(8,128)S(1)}, u32[]{:S(2)}, u32[]{:S(2)}) collective-permute-start(f32[1,72,256]{2,1,0:T(8,128)S(1)} %get-tuple-element.32), channel_id=1, source_target_pairs={{1,2},{2,1},{3,4},{4,3},{5,6},{6,5},{9,10},{10,9},{11,12},{12,11},... | collective-permute-start | bytes 221192 | tf_op jit(solution)/shard_map/ppermute | solution.py:747
  78.1 26.6 %copy-start.1 = (f32[1,4,256,512]{3,2,1,0:T(8,128)S(1)}, f32[1,4,256,512]{3,2,1,0:T(8,128)}, u32[]{:S(2)}) copy-start(f32[1,4,256,512]{3,2,1,0:T(8,128)} %param.5) | copy-start | bytes 6291460
  78.8 2.9 %collective-permute-start.7 = (f32[1,72,256]{2,1,0:T(8,128)S(1)}, f32[1,72,256]{2,1,0:T(8,128)S(1)}, u32[]{:S(2)}, u32[]{:S(2)}) collective-permute-start(f32[1,72,256]{2,1,0:T(8,128)S(1)} %get-tuple-element.35), channel_id=1, source_target_pairs={{0,1},{1,0},{2,3},{3,2},{4,5},{5,4},{6,7},{7,6},{8,9},{9,8},{10,11... | collective-permute-start | bytes 221192 | tf_op jit(solution)/shard_map/ppermute | solution.py:744
  78.9 6.6 %collective-permute-start.8 = (f32[1,72,256]{2,1,0:T(8,128)S(1)}, f32[1,72,256]{2,1,0:T(8,128)S(1)}, u32[]{:S(2)}, u32[]{:S(2)}) collective-permute-start(f32[1,72,256]{2,1,0:T(8,128)S(1)} %get-tuple-element.36), channel_id=1, source_target_pairs={{1,2},{2,1},{3,4},{4,3},{5,6},{6,5},{9,10},{10,9},{11,12},{12,11},... | collective-permute-start | bytes 221192 | tf_op jit(solution)/shard_map/ppermute | solution.py:747
  86.3 5.6 %collective-permute-start.9 = (f32[1,72,256]{2,1,0:T(8,128)S(1)}, f32[1,72,256]{2,1,0:T(8,128)S(1)}, u32[]{:S(2)}, u32[]{:S(2)}) collective-permute-start(f32[1,72,256]{2,1,0:T(8,128)S(1)} %get-tuple-element.38), channel_id=1, source_target_pairs={{0,1},{1,0},{2,3},{3,2},{4,5},{5,4},{6,7},{7,6},{8,9},{9,8},{10,11... | collective-permute-start | bytes 221192 | tf_op jit(solution)/shard_map/ppermute | solution.py:744
  86.4 6.6 %collective-permute-start.10 = (f32[1,72,256]{2,1,0:T(8,128)S(1)}, f32[1,72,256]{2,1,0:T(8,128)S(1)}, u32[]{:S(2)}, u32[]{:S(2)}) collective-permute-start(f32[1,72,256]{2,1,0:T(8,128)S(1)} %get-tuple-element.39), channel_id=1, source_target_pairs={{1,2},{2,1},{3,4},{4,3},{5,6},{6,5},{9,10},{10,9},{11,12},{12,11},... | collective-permute-start | bytes 221192 | tf_op jit(solution)/shard_map/ppermute | solution.py:747
  89.2 12.5 %collective-permute-start.12 = (f32[2,72,256]{2,1,0:T(8,128)S(1)}, f32[2,72,256]{2,1,0:T(8,128)S(1)}, u32[]{:S(2)}, u32[]{:S(2)}) collective-permute-start(f32[2,72,256]{2,1,0:T(8,128)S(1)} %get-tuple-element.43), channel_id=1, source_target_pairs={{0,16},{8,24},{16,0},{24,8},{1,17},{9,25},{17,1},{25,9},{2,18},{10... | collective-permute-start | bytes 442376 | tf_op jit(solution)/shard_map/ppermute | solution.py:832
  89.6 12.1 %collective-permute-start.13 = (f32[2,72,256]{2,1,0:T(8,128)S(1)}, f32[2,72,256]{2,1,0:T(8,128)S(1)}, u32[]{:S(2)}, u32[]{:S(2)}) collective-permute-start(f32[2,72,256]{2,1,0:T(8,128)S(1)} %get-tuple-element.44), channel_id=1, source_target_pairs={{0,24},{16,8},{24,16},{1,25},{17,9},{25,17},{2,26},{18,10},{26,18}... | collective-permute-start | bytes 442376 | tf_op jit(solution)/shard_map/ppermute | solution.py:832
  94.4 10.2 %collective-permute-start.11 = (f32[2,72,256]{2,1,0:T(8,128)S(1)}, f32[2,72,256]{2,1,0:T(8,128)S(1)}, u32[]{:S(2)}, u32[]{:S(2)}) collective-permute-start(f32[2,72,256]{2,1,0:T(8,128)S(1)} %get-tuple-element.42), channel_id=1, source_target_pairs={{0,8},{8,16},{16,24},{24,0},{1,9},{9,17},{17,25},{25,1},{2,10},{10... | collective-permute-start | bytes 442376 | tf_op jit(solution)/shard_map/ppermute | solution.py:832

commit v4 on v3

v4 whole, which is shorter than its diff:
```python
import functools

import jax
import jax.numpy as jnp
from jax import lax
from jax.experimental import pallas as pl
from jax.experimental.pallas import tpu as pltpu
from jax.sharding import PartitionSpec as P


STEPS = 4
courant = 0.15
GAIN = 0.5 * courant
MARGIN = 16
F32 = jnp.float32
VMEM = pltpu.VMEM
MIB = 1024 * 1024
VMEM_LIMITS = {"slices": 50 * MIB, "fine": 50 * MIB, "small": 10 * MIB, "final": 16 * MIB}


def params(limit):
    return pltpu.CompilerParams(vmem_limit_bytes=limit)


def whole(count):
    return [pl.BlockSpec(memory_space=VMEM)] * count


def shape(*dims):
    return jax.ShapeDtypeStruct(dims, F32)


def split_dot(x, selection):
    high = x.astype(jnp.bfloat16)
    rest = x - high.astype(F32)
    middle = rest.astype(jnp.bfloat16)
    low = (rest - middle.astype(F32)).astype(jnp.bfloat16)
    dot = functools.partial(jnp.dot, preferred_element_type=F32)
    return dot(high, selection) + dot(middle, selection) + dot(low, selection)


def pairing(width):
    fine = lax.broadcasted_iota(jnp.int32, (width, width // 2), 0)
    coarse = lax.broadcasted_iota(jnp.int32, (width, width // 2), 1)
    return jnp.where((fine == 2 * coarse) | (fine == 2 * coarse + 1), 1.0, 0.0).astype(jnp.bfloat16)


def spreading(width):
    coarse = lax.broadcasted_iota(jnp.int32, (width // 2, width), 0)
    fine = lax.broadcasted_iota(jnp.int32, (width // 2, width), 1)
    return jnp.where((fine == 2 * coarse) | (fine == 2 * coarse + 1), 1.0, 0.0).astype(jnp.bfloat16)


def natural_mean(first, second, rows_scr, select):
    rows = first.shape[0]
    lanes = split_dot(first + second, select)
    parts = []
    for j in range(lanes.shape[1] // 128):
        rows_scr[j, 0:rows, :] = lanes[:, 128 * j : 128 * j + 128]
        even = rows_scr[j, pl.ds(0, rows // 2, 2), :]
        odd = rows_scr[j, pl.ds(1, rows // 2, 2), :]
        parts.append(0.125 * (even + odd))
    return jnp.concatenate(parts, axis=1)


def tile(i):
    return slice(8 * i, 8 * i + 8)


def dealt_mean(load, tiles, select):
    sums = [
        (load(0, 2 * i) + load(1, 2 * i)) + (load(0, 2 * i + 1) + load(1, 2 * i + 1)) for i in range(tiles // 2)
    ]
    return 0.125 * split_dot(jnp.concatenate(sums, axis=0), select)


def weights_plane(load, store, rows, lanes):
    sub = lax.broadcasted_iota(jnp.int32, (8, 128), 0)
    lane = lax.broadcasted_iota(jnp.int32, (8, 128), 1)
    tiles, blocks = rows // 8, lanes // 128

    def cut(x):
        return [x[:, 128 * j : 128 * j + 128] for j in range(blocks)]

    c = cut(load(0, 0))
    below = [pltpu.roll(x, 1, 0) for x in cut(load(0, tiles - 1))]
    wrapped = [pltpu.roll(x, 7, 0) for x in c]
    for i in range(tiles):
        above = cut(load(0, i + 1)) if i + 1 < tiles else wrapped
        czm, czp = cut(load(-1, i)), cut(load(1, i))
        right = [pltpu.roll(x, 1, 1) for x in c]
        left = [pltpu.roll(x, 127, 1) for x in c]
        w = [[] for _ in range(7)]
        for j in range(blocks):
            mid = c[j]
            xm = mid + jnp.where(lane == 0, right[j - 1] if j else 0.0, right[j])
            xp = mid + jnp.where(lane == 127, left[j + 1] if j + 1 < blocks else 0.0, left[j])
            ym = mid + (jnp.where(sub == 0, 0.0, below[j]) if i == 0 else below[j])
            yp = mid + (jnp.where(sub == 7, 0.0, above[j]) if i + 1 == tiles else above[j])
            zm, zp = mid + czm[j], mid + czp[j]
            w[0].append(1.0 - ((xm + xp) + (ym + yp) + (zm + zp)))
            w[1].append(xm if j else jnp.where(lane == 0, 0.0, xm))
            w[2].append(xp if j + 1 < blocks else jnp.where(lane == 127, 0.0, xp))
            w[3].append(jnp.where(sub == 0, 0.0, ym) if i == 0 else ym)
            w[4].append(jnp.where(sub == 7, 0.0, yp) if i + 1 == tiles else yp)
            inside = mid > 0.0
            w[5].append(jnp.where(inside, zm, 0.0))
            w[6].append(jnp.where(inside, zp, 0.0))
        for k in range(7):
            store(k, i, jnp.concatenate(w[k], axis=1))
        below, c = c, above


def step_plane(weight, load, store, rows, lanes, fields=1):
    tiles = rows // 8
    below = [pltpu.roll(load(f, 0, tiles - 1), 1, 0) for f in range(fields)]
    center = [load(f, 0, 0) for f in range(fields)]
    wrapped = [pltpu.roll(v, 7, 0) for v in center]
    for i in range(tiles):
        w = [weight(k, i) for k in range(7)]
        for f in range(fields):
            mid = center[f]
            above = load(f, 0, i + 1) if i + 1 < tiles else wrapped[f]
            xm = pltpu.roll(mid, 1, 1)
            xp = pltpu.roll(mid, lanes - 1, 1)
            out = w[0] * mid
            out = out + (w[1] * xm + w[2] * xp)
            out = out + (w[3] * below[f] + w[4] * above)
            out = out + (w[5] * load(f, -1, i) + w[6] * load(f, 1, i))
            store(f, i, out)
            below[f], center[f] = mid, above


def at_row(value, step):
    return pl.multiple_of(value * step, 8)


def slice_kernel(c_hbm, iterate_hbm, c_ref, send_ref, sem):
    half = lax.rem(lax.axis_index("tm"), 2)
    own = send_ref.shape[1]
    window = pl.ds(at_row(half, c_hbm.shape[1] - c_ref.shape[1]), c_ref.shape[1])
    send = pltpu.make_async_copy(iterate_hbm.at[:, pl.ds(at_row(1 - half, own), own), :], send_ref, sem.at[0])
    keep = pltpu.make_async_copy(c_hbm.at[:, window, :], c_ref, sem.at[1])
    send.start()
    keep.start()
    send.wait()
    keep.wait()


def fine_kernel(planes, flag_ref, c_hbm, partner_hbm, other_hbm, iterate_hbm, initial_hbm, received_hbm,
                own_ref, to_partner_ref, to_other_ref, cc_scr,
                c_raw, v_raw, c_scr, w_scr, a_scr, b_scr, coarse_ref, keep_scr, c_sem, v_sem):
    half, upper, last = flag_ref[0], flag_ref[1], flag_ref[2]
    depth, rows, lanes = c_scr.shape
    own_rows = rows - MARGIN
    tiles = rows // 8
    columns = [slice(128 * j, 128 * j + 128) for j in range(lanes // 128)]
    select = pairing(lanes)
    coarse_planes, reach = depth // 2, planes // 2
    coarse_rows, coarse_lanes = rows // 2, lanes // 2
    last_plane = depth - 1

    slabs = ((c_hbm, planes), (partner_hbm, upper * (2 * planes)), (other_hbm, (1 - upper) * (2 * planes)))
    c_copies = [
        pltpu.make_async_copy(ref.at[:, :, column], c_raw.at[pl.ds(at, planes), j], c_sem.at[n, j])
        for n, (ref, at) in enumerate(slabs)
        for j, column in enumerate(columns)
    ]
    for copy in c_copies:
        copy.start()
    into = pl.ds(at_row(half, MARGIN), own_rows)
    source = pl.ds(at_row(half, own_rows), own_rows)

    def fetch(ref, f):
        for j in range(len(columns)):
            pltpu.make_async_copy(ref[j], v_raw.at[f, :, j, into, :], v_sem.at[f, j]).start()

    def halves(ref):
        return [ref.at[:, source, column] for column in columns]

    received = [received_hbm.at[:, :, column] for column in columns]

    first_kept = (last == 0) & (half == 0)
    first_got = (last == 0) & (half == 1)
    second_kept = (last == 1) == (half == 0)
    for f, choices in enumerate(
        (
            ((last == 1, halves(initial_hbm)), (first_kept, halves(iterate_hbm)), (first_got, received)),
            ((second_kept, halves(iterate_hbm)), (jnp.logical_not(second_kept), received)),
        )
    ):
        for condition, ref in choices:
            @pl.when(condition)
            def _():
                fetch(ref, f)

    outside = pl.ds(at_row(1 - half, own_rows), MARGIN)
    v_raw[:, :, :, outside, :] = jnp.zeros(v_raw.shape[:3] + (MARGIN, 128), F32)
    idle = jnp.zeros((2,) + a_scr.shape[2:], F32)
    for number in range(STEPS):
        v_in = (a_scr, b_scr)[number % 2]
        v_in[:, planes - 1 - number] = idle
        v_in[:, 2 * planes + number] = idle
    for copy in c_copies:
        copy.wait()

    def deal_c(z, _):
        for j, column in enumerate(columns):
            for i in range(tiles):
                c_scr[z, tile(i), column] = GAIN * c_raw[z, j, pl.ds(i, 8, tiles), :]
        return 0

    lax.fori_loop(0, depth, deal_c, 0)

    def weigh(z, _):
        below, above = jnp.maximum(z - 1, 0), jnp.minimum(z + 1, last_plane)

        def load(dz, i):
            at = z if dz == 0 else (below if dz < 0 else above)
            return c_scr[at, tile(i), :]

        def store(k, i, w):
            w_scr[k, z, tile(i), :] = w

        weights_plane(load, store, rows, lanes)
        return 0

    lax.fori_loop(1, last_plane, weigh, 0)
    for k, z, inner in ((6, 0, 1), (5, last_plane, last_plane - 1)):
        for i in range(tiles):
            c = c_scr[z, tile(i), :]
            w_scr[k, z, tile(i), :] = jnp.where(c > 0.0, c + c_scr[inner, tile(i), :], 0.0)

    def restrict_c(q, _):
        cc_scr[q] = dealt_mean(lambda dz, i: c_scr[2 * q + dz, tile(i), :], tiles, select)
        return 0

    lax.fori_loop(0, coarse_planes, restrict_c, 0)
    for q in range(reach):
        def load(dz, i):
            return cc_scr[reach + q + dz, tile(i), :]

        def store(k, i, w):
            coarse_ref[k, q, tile(i), :] = w

        weights_plane(load, store, coarse_rows, coarse_lanes)

    for f in range(2):
        for j in range(len(columns)):
            pltpu.make_async_copy(received[j], v_raw.at[f, :, j, into, :], v_sem.at[f, j]).wait()

    def deal_v(z, _):
        for f in range(2):
            for j, column in enumerate(columns):
                for i in range(tiles):
                    a_scr[f, planes + z, tile(i), column] = v_raw[f, z, j, pl.ds(i, 8, tiles), :]
        return 0

    lax.fori_loop(0, planes, deal_v, 0)

    def keep(n, _):
        f, q = n // reach, n % reach
        keep_scr[n] = dealt_mean(lambda dz, i: a_scr[f, planes + 2 * q + dz, tile(i), :], tiles, select)
        return 0

    lax.fori_loop(0, 2 * reach, keep, 0)
    for number in range(STEPS):
        v_in, v_out = (a_scr, b_scr) if number % 2 == 0 else (b_scr, a_scr)

        def advance(z, _):
            below, above = jnp.maximum(z - 1, 0), jnp.minimum(z + 1, last_plane)

            def load(f, dz, i):
                at = z if dz == 0 else (below if dz < 0 else above)
                return v_in[f, at, tile(i), :]

            def weight(k, i):
                return w_scr[k, z, tile(i), :]

            def store(f, i, v):
                v_out[f, z, tile(i), :] = v

            step_plane(weight, load, store, rows, lanes, 2)
            return 0

        lax.fori_loop(planes - number, 2 * planes + number, advance, 0)
        for k, z, inner in ((6, planes - 1 - number, planes - number), (5, 2 * planes + number, 2 * planes + number - 1)):
            for i in range(tiles):
                w = w_scr[k, z, tile(i), :]
                for f in range(2):
                    v_out[f, z, tile(i), :] = w * v_in[f, inner, tile(i), :]
    result = a_scr if STEPS % 2 == 0 else b_scr

    scale = jnp.where(last == 1, 0.0, 1.0).astype(F32)
    for q in range(reach):
        keep_scr[q] = keep_scr[q] * scale
    zero = jnp.zeros((8, coarse_lanes), F32)
    for q in range(reach):
        def load(f, dz, i):
            at = q + dz
            return zero if at < 0 or at >= reach else keep_scr[f * reach + at, tile(i), :]

        def weight(k, i):
            return coarse_ref[k, q, tile(i), :]

        def store(f, i, v):
            own_ref[f, q, tile(i), :] = v

        step_plane(weight, load, store, coarse_rows, coarse_lanes, 2)

    def mean_of(f, q):
        return dealt_mean(lambda dz, i: result[f, 2 * q + dz, tile(i), :], tiles, select)

    low_c, high_c = cc_scr[reach - 1], cc_scr[2 * reach]
    low_w = jnp.where(low_c > 0.0, low_c + cc_scr[reach], 0.0)
    high_w = jnp.where(high_c > 0.0, high_c + cc_scr[2 * reach - 1], 0.0)
    for f in range(2):
        for q in range(reach):
            own_ref[f, q] = mean_of(f, reach + q) - own_ref[f, q]
        for q in range(reach):
            low, high = mean_of(f, q), mean_of(f, 2 * reach + q)
            if q == reach - 1:
                low = low - low_w * keep_scr[f * reach]
            if q == 0:
                high = high - high_w * keep_scr[f * reach + reach - 1]

            @pl.when(upper == 1)
            def _():
                to_partner_ref[f, q] = high
                to_other_ref[f, q] = low

            @pl.when(upper == 0)
            def _():
                to_partner_ref[f, q] = low
                to_other_ref[f, q] = high


def weight_kernel(cc_ref, weight_ref):
    planes, rows, lanes = cc_ref.shape
    for q in range(planes - 2):
        def load(dz, i):
            return cc_ref[q + 1 + dz, tile(i), :]

        def store(k, i, w):
            weight_ref[k, q, tile(i), :] = w

        weights_plane(load, store, rows, lanes)


def sum_kernel(flag_ref, own_ref, partner_ref, other_ref, val_ref, extra_ref, to_partner_ref, to_other_ref):
    upper = flag_ref[1]
    planes = val_ref.shape[0]
    val = own_ref[0] + partner_ref[0] + other_ref[0]
    extra = own_ref[1] + partner_ref[1] + other_ref[1]
    val_ref[...] = val
    extra_ref[...] = extra
    to_partner_ref[0:planes] = val
    to_other_ref[0:planes] = val
    to_partner_ref[planes] = jnp.where(upper == 1, extra[-1], extra[0])
    to_other_ref[planes] = jnp.where(upper == 1, extra[0], extra[-1])


def coarse_advance(weight_ref, offset, source, into, count, extra, add, rows, lanes):
    for q in range(count):
        def load(f, dz, i):
            return source[q + 1 + dz, tile(i), :]

        def weight(k, i):
            return weight_ref[k, offset + q, tile(i), :]

        def store(f, i, v):
            into[q, tile(i), :] = v + add * extra[q, tile(i), :]

        step_plane(weight, load, store, rows, lanes)


def double_kernel(slots, flag_ref, weight_ref, partner_ref, other_ref, extra_ref, val_ref,
                  first_ref, second_ref, to_partner_ref, to_other_ref, wide, extra_wide, middle):
    upper = flag_ref[1]
    planes, rows, lanes = val_ref.shape
    extra_wide[1 : planes + 1] = extra_ref[...]
    wide[planes : 2 * planes] = val_ref[...]
    for ref, above in ((partner_ref, upper), (other_ref, 1 - upper)):
        wide[pl.ds(above * (2 * planes), planes)] = ref[0:planes]
        extra_wide[above * (planes + 1)] = ref[planes]
    add = [flag_ref[slot].astype(F32) for slot in slots]
    coarse_advance(weight_ref, 0, wide.at[planes - 2 :], middle, planes + 2, extra_wide, add[0], rows, lanes)
    first_ref[...] = middle[1 : planes + 1]
    coarse_advance(weight_ref, 1, middle, second_ref, planes, extra_ref, add[1], rows, lanes)
    low, high = second_ref[0], second_ref[planes - 1]
    to_partner_ref[0] = jnp.where(upper == 1, high, low)
    to_other_ref[0] = jnp.where(upper == 1, low, high)


def single_kernel(slot, flag_ref, weight_ref, partner_ref, other_ref, extra_ref, val_ref,
                  next_ref, to_partner_ref, to_other_ref, wide):
    upper = flag_ref[1]
    planes, rows, lanes = val_ref.shape
    wide[1 : planes + 1] = val_ref[...]
    wide[upper * (planes + 1)] = partner_ref[0]
    wide[(1 - upper) * (planes + 1)] = other_ref[0]
    coarse_advance(weight_ref, 1, wide, next_ref, planes, extra_ref, flag_ref[slot].astype(F32), rows, lanes)
    low, high = next_ref[0], next_ref[planes - 1]
    to_partner_ref[0] = jnp.where(upper == 1, high, low)
    to_other_ref[0] = jnp.where(upper == 1, low, high)


def pick_kernel(slots, count, flag_ref, *refs):
    for slot, ref in zip(slots, refs[count:]):
        which = flag_ref[slot]

        @pl.when(which < 0)
        def _():
            ref[...] = jnp.zeros(ref.shape, F32)

        for m, source in enumerate(refs[:count]):
            @pl.when(which == m)
            def _():
                ref[...] = source[...]


def base_kernel(iterate_ref, out_ref, rows_scr, fine_scr):
    planes, rows, lanes = iterate_ref.shape
    select, spread = pairing(lanes), spreading(lanes)
    for q in range(planes // 2):
        mean = natural_mean(iterate_ref[2 * q], iterate_ref[2 * q + 1], rows_scr, select)
        wide = split_dot(mean, spread)
        for j in range(lanes // 128):
            column = slice(128 * j, 128 * j + 128)
            fine_scr[j, pl.ds(0, rows // 2, 2), :] = wide[:, column]
            fine_scr[j, pl.ds(1, rows // 2, 2), :] = wide[:, column]
            for part in range(2):
                out_ref[2 * q + part, :, column] = iterate_ref[2 * q + part, :, column] - fine_scr[j]


def final_kernel(slots, flag_ref, base_ref, *refs):
    count = len(slots)
    pieces, out_ref, fine_scr, sum_scr, error_scr = refs[:count], *refs[count:]
    planes, rows, lanes = base_ref.shape
    spread = spreading(lanes)
    piece_rows = pieces[0].shape[1]
    tiles = piece_rows // 8
    sum_scr[...] = jnp.zeros(sum_scr.shape, F32)
    for slot, ref in zip(slots, pieces):
        side = flag_ref[slot]
        sum_scr[side] = sum_scr[side] + ref[...]
    for q in range(planes // 2):
        for j in range(lanes // 256):
            column = slice(128 * j, 128 * j + 128)
            error_scr[j] = jnp.zeros(error_scr.shape[1:], F32)
            for side in range(2):
                first = side * (rows // 2 - piece_rows)
                for i in range(tiles):
                    at = pl.ds(first + i, 8, tiles)
                    error_scr[j, at, :] = error_scr[j, at, :] + sum_scr[side, q, tile(i), column]
        error = jnp.concatenate([error_scr[j] for j in range(lanes // 256)], axis=1)
        wide = split_dot(error, spread)
        for j in range(lanes // 128):
            column = slice(128 * j, 128 * j + 128)
            fine_scr[j, pl.ds(0, rows // 2, 2), :] = wide[:, column]
            fine_scr[j, pl.ds(1, rows // 2, 2), :] = wide[:, column]
            for part in range(2):
                out_ref[2 * q + part, :, column] = base_ref[2 * q + part, :, column] + fine_scr[j]


def swap_pairs(count, first):
    pairs = []
    for i in range(first, count - 1, 2):
        pairs += [(i, i + 1), (i + 1, i)]
    return pairs


def roles(layers):
    last_group = layers // 2 - 1
    rows = []
    for t in range(layers):
        half, last = t % 2, int(t // 2 == last_group)
        adds = [int(number == (layers - 1 if last else 1)) for number in range(1, layers)]
        sends = []
        for shift in range(layers):
            k = (t + shift) % layers
            m = k if last else k - 1 - (t - half)
            sends.append(m if m >= 0 else -1)
        halves = [(t - shift) % layers % 2 for shift in range(layers)]
        rows.append([half, last, *adds, *sends, *halves])
    return rows


def local(initial, iterate, diffusivity):
    layers, slabs = lax.axis_size("tm"), lax.axis_size("space")
    t, s = lax.axis_index("tm"), lax.axis_index("space")
    planes, all_rows, lanes = initial.shape
    assert layers % 2 == 0 and slabs % 2 == 0 and planes == STEPS
    own_rows = all_rows // 2
    rows = own_rows + MARGIN
    coarse_rows, coarse_lanes = rows // 2, lanes // 2
    reach = planes // 2
    upper = 1 - s % 2
    field = iterate[0]

    def partner_swap(x):
        return lax.ppermute(x, "space", swap_pairs(slabs, 0))

    def other_swap(x):
        return lax.ppermute(x, "space", swap_pairs(slabs, 1))

    anywhere = pl.BlockSpec(memory_space=pl.ANY)
    in_hbm = pl.BlockSpec(memory_space=pltpu.HBM)
    c, to_row_partner = pl.pallas_call(
        slice_kernel,
        out_shape=(shape(planes, rows, lanes), shape(planes, own_rows, lanes)),
        in_specs=[in_hbm] * 2,
        out_specs=tuple(whole(2)),
        scratch_shapes=[pltpu.SemaphoreType.DMA((2,))],
        compiler_params=params(VMEM_LIMITS["slices"]),
        name="slices",
    )(diffusivity, field)
    row_pairs = swap_pairs(layers, 0)
    row_pairs.remove((layers - 1, layers - 2))
    received = lax.ppermute(to_row_partner, "tm", row_pairs)
    c_other = other_swap(c)
    c_partner = partner_swap(c)

    table = roles(layers)
    mine = jnp.asarray(table, jnp.int32)[t]
    flags = jnp.concatenate([mine[:1], jnp.reshape(upper, (1,)).astype(jnp.int32), mine[1:]])
    add_at, send_at, half_at = 3, 2 + layers, 2 + 2 * layers
    smem = pl.BlockSpec(memory_space=pltpu.SMEM)

    fields = shape(2, reach, coarse_rows, coarse_lanes)
    blocks = lanes // 128
    own, to_partner, to_other, cc = pl.pallas_call(
        functools.partial(fine_kernel, planes),
        out_shape=(fields, fields, fields, shape(3 * reach, coarse_rows, coarse_lanes)),
        in_specs=[smem] + [anywhere] * 3 + [in_hbm] * 2 + [anywhere],
        out_specs=tuple(whole(4)),
        scratch_shapes=[
            VMEM((3 * planes, blocks, rows, 128), F32),
            VMEM((2, planes, blocks, rows, 128), F32),
            VMEM((3 * planes, rows, lanes), F32),
            VMEM((7, 3 * planes, rows, lanes), F32),
            VMEM((2, 3 * planes, rows, lanes), F32),
            VMEM((2, 3 * planes, rows, lanes), F32),
            VMEM((7, reach, coarse_rows, coarse_lanes), F32),
            VMEM((2 * reach, coarse_rows, coarse_lanes), F32),
            pltpu.SemaphoreType.DMA((3, blocks)),
            pltpu.SemaphoreType.DMA((2, blocks)),
        ],
        compiler_params=params(VMEM_LIMITS["fine"]),
        name="fine",
    )(flags, c, c_partner, c_other, field, initial, received)

    def cost(microseconds):
        return pl.CostEstimate(flops=int(microseconds * 4e6), bytes_accessed=0, transcendentals=0)

    base = pl.pallas_call(
        base_kernel,
        out_shape=shape(planes, all_rows, lanes),
        in_specs=whole(1),
        out_specs=pl.BlockSpec(memory_space=VMEM),
        scratch_shapes=[VMEM((coarse_lanes // 128, all_rows, 128), F32), VMEM((lanes // 128, all_rows, 128), F32)],
        compiler_params=params(VMEM_LIMITS["final"]),
        cost_estimate=cost(4),
        name="base",
    )(field)

    from_other = other_swap(to_other)
    from_partner = partner_swap(to_partner)
    plane = shape(1, coarse_rows, coarse_lanes)
    block = shape(reach, coarse_rows, coarse_lanes)
    thick = shape(reach + 1, coarse_rows, coarse_lanes)
    weights = pl.pallas_call(
        weight_kernel,
        out_shape=shape(7, 3 * reach - 2, coarse_rows, coarse_lanes),
        in_specs=whole(1),
        out_specs=pl.BlockSpec(memory_space=VMEM),
        compiler_params=params(VMEM_LIMITS["small"]),
        cost_estimate=cost(2),
        name="weights",
    )(cc)
    val, extra, to_partner, to_other = pl.pallas_call(
        sum_kernel,
        out_shape=(block, block, thick, thick),
        in_specs=[smem] + whole(3),
        out_specs=tuple(whole(4)),
        compiler_params=params(VMEM_LIMITS["small"]),
        name="gather",
    )(flags, own, from_partner, from_other)

    ready = [max(row[1 + layers + shift] for row in table) for shift in range(layers)]
    arrived = [None] * layers
    values = [val]
    done = -1

    def deliver():
        upto = len(values) - 1
        shifts = [shift for shift in range(layers) if done < max(ready[shift], 0) <= upto]
        if not shifts:
            return upto
        sends = pl.pallas_call(
            functools.partial(pick_kernel, [send_at + shift for shift in shifts], len(values)),
            out_shape=(block,) * len(shifts),
            in_specs=[smem] + whole(len(values)),
            out_specs=tuple(whole(len(shifts))),
            compiler_params=params(VMEM_LIMITS["small"]),
        )(flags, *values)
        for shift, send in zip(shifts, sends):
            pairs = [
                (source, (source + shift) % layers)
                for source in range(layers)
                if table[source][1 + layers + shift] >= 0
            ]
            arrived[shift] = lax.ppermute(send, "tm", pairs) if shift else send
        return upto

    number = 1
    while number < layers:
        from_other = other_swap(to_other)
        from_partner = partner_swap(to_partner)
        if number > 1:
            done = deliver()
        double = number == 1 and number + 1 < layers
        slots = [add_at + number - 1 + n for n in range(1 + double)]
        *made, to_partner, to_other = pl.pallas_call(
            functools.partial(double_kernel, slots) if double else functools.partial(single_kernel, slots[0]),
            out_shape=(*[block] * len(slots), plane, plane),
            in_specs=[smem] + whole(5),
            out_specs=tuple(whole(2 + len(slots))),
            scratch_shapes=[
                VMEM((3 * reach, coarse_rows, coarse_lanes), F32),
                VMEM((reach + 2, coarse_rows, coarse_lanes), F32),
                VMEM((reach + 2, coarse_rows, coarse_lanes), F32),
            ] if double else [VMEM((reach + 2, coarse_rows, coarse_lanes), F32)],
            compiler_params=params(VMEM_LIMITS["small"]),
        )(flags, weights, from_partner, from_other, extra, values[-1])
        values += made
        number += len(slots)
    deliver()

    corrected = pl.pallas_call(
        functools.partial(final_kernel, [half_at + shift for shift in range(layers)]),
        out_shape=shape(planes, all_rows, lanes),
        in_specs=[smem] + whole(1 + layers),
        out_specs=pl.BlockSpec(memory_space=VMEM),
        scratch_shapes=[
            VMEM((lanes // 128, all_rows, 128), F32),
            VMEM((2, reach, coarse_rows, coarse_lanes), F32),
            VMEM((coarse_lanes // 128, all_rows // 2, 128), F32),
        ],
        compiler_params=params(VMEM_LIMITS["final"]),
        name="final",
    )(flags, base, *arrived)
    return corrected[None]


def solution(mesh):
    placed = (P("space", None, None), P("tm", "space", None, None), P("space", None, None))

    return jax.shard_map(local, mesh=mesh, in_specs=placed, out_specs=P("tm", "space", None, None), check_vma=False)
```

time: 110 us -> 100 us (0.909)
  waiting for transfers between devices: 49.6 us -> 45 us
  local copies, waits for them, and re-layouts: 3.96 us -> 0.77 us
  starting transfers between devices: 22 us -> 20 us
    unnamed x8 -> x2, local copies, waits for them, and re-layouts: 3.19 us -> 0.01 us
    ppermute x3, waiting for transfers between devices: 7.82 us -> 5.14 us  [deliver(): arrived[shift] = lax.ppermute(send, 'tm', pairs) if shift else send]
    pallas_call x4 -> x7, Pallas kernels: 3.63 us -> 6.31 us  [the longest x2 2.44 us: local(): pl.pallas_call(functools.partial(double_kernel, slots) if double else fun...]
    pallas_call x1, Pallas kernels: 25 us -> 22.3 us  [local(): pl.pallas_call(functools.partial(fine_kernel, planes), out_shape=(fields,...]
    ppermute x5 -> x4, starting transfers between devices: 14.5 us -> 12.3 us  [other_swap(): return lax.ppermute(x, 'space', swap_pairs(slabs, 1))]
    ppermute x5 -> x4, waiting for transfers between devices: 16.9 us -> 15 us  [other_swap(): return lax.ppermute(x, 'space', swap_pairs(slabs, 1))]
    pallas_call x1, Pallas kernels: 0.2 us -> 1.6 us  [local(): pl.pallas_call(slice_kernel, out_shape=(shape(planes, rows, lanes), shape...]
    pallas_call x1, Pallas kernels: 3.75 us -> 2.52 us  [local(): pl.pallas_call(functools.partial(final_kernel, [half_at + shift for shift...]
  transfers between devices with their start and end apart: 14 -> 12, of which waited for: 7 -> 6; matrix products, arithmetic and copies ran while one was open for 1% -> 1% of each run, Pallas kernels for 1% -> 5%
where the time goes in v4:
time: 100 us; the launch traced here: 98.9 us
  waiting for transfers between devices  45 us (45%)
  Pallas kernels  32.7 us (33%)
  starting transfers between devices  20 us (20%)
    ppermute x1, waiting for transfers between devices, local(): received = lax.ppermute(to_row_partner, 'tm', row_pairs)  24.9 us
    pallas_call x1, Pallas kernels, local(): pl.pallas_call(functools.partial(fine_kernel, planes), out_shape=(fields,...  22.3 us
    ppermute x4, waiting for transfers between devices, other_swap(): return lax.ppermute(x, 'space', swap_pairs(slabs, 1))  15 us
    ppermute x4, starting transfers between devices, other_swap(): return lax.ppermute(x, 'space', swap_pairs(slabs, 1))  12.3 us
    ppermute x3, starting transfers between devices, deliver(): arrived[shift] = lax.ppermute(send, 'tm', pairs) if shift else send  6.15 us
    ppermute x3, waiting for transfers between devices, deliver(): arrived[shift] = lax.ppermute(send, 'tm', pairs) if shift else send  5.14 us
    pallas_call x1, Pallas kernels, local(): pl.pallas_call(functools.partial(final_kernel, [half_at + shift for shift...  2.52 us
    pallas_call x2, Pallas kernels, local(): pl.pallas_call(functools.partial(double_kernel, slots) if double else fun...  2.44 us
  transfers between devices with their start and end apart: 12, of which 6 were waited for; matrix products, arithmetic and copies ran while one was open for 1% of the time, Pallas kernels for 5%

profile of v4, /device:TPU:28, one launch (start us, length us, event | category | flops | bytes accessed | tf_op | source)
XLA Modules:
  0.0 98.9 jit_solution(17343271573661485187)
XLA Ops:
  0.0 1.6 %slices.1 = (f32[4,144,512]{2,1,0:T(8,128)S(1)}, f32[4,128,512]{2,1,0:T(8,128)S(1)}) custom-call(f32[4,256,512]{2,1,0:T(8,128)} %c_hbm.1, f32[4,256,512]{2,1,0:T(8,128)} %bitcast.7), custom_call_target="tpu_custom_call" | custom-call | tf_op jit(solution)/shard_map/slices/pallas_call | solution.py:509
  1.6 0.1 collective-permute-start
  1.7 3.4 %collective-permute-start.1 = (f32[4,144,512]{2,1,0:T(8,128)S(1)}, f32[4,144,512]{2,1,0:T(8,128)}, u32[]{:S(2)}, u32[]{:S(2)}) collective-permute-start(f32[4,144,512]{2,1,0:T(8,128)S(1)} %get-tuple-element.24.c_hbm), channel_id=1, source_target_pairs={{1,2},{2,1},{3,4},{4,3},{5,6},{6,5},{9,10},{10,9},{11,12},{12,11},... | collective-permute-start | bytes 3538952 | tf_op jit(solution)/shard_map/ppermute | solution.py:505
  5.1 1.3 %collective-permute-start.2 = (f32[4,128,512]{2,1,0:T(8,128)S(1)}, f32[4,128,512]{2,1,0:T(8,128)S(1)}, u32[]{:S(2)}, u32[]{:S(2)}) collective-permute-start(f32[4,128,512]{2,1,0:T(8,128)S(1)} %get-tuple-element.25), channel_id=1, source_target_pairs={{0,8},{8,0},{16,24},{1,9},{9,1},{17,25},{2,10},{10,2},{18,26},{3,1... | collective-permute-start | bytes 3145736 | tf_op jit(solution)/shard_map/ppermute | solution.py:520
  6.4 0.7 constant_dynamic-slice_fusion
  7.1 0.1 slice_bitcast_fusion
  7.2 0.1 pad_add_fusion.flag_ref
  7.3 24.9 %collective-permute-done.2.received_hbm = f32[4,128,512]{2,1,0:T(8,128)S(1)} collective-permute-done((f32[4,128,512]{2,1,0:T(8,128)S(1)}, f32[4,128,512]{2,1,0:T(8,128)S(1)}, u32[]{:S(2)}, u32[]{:S(2)}) %collective-permute-start.2) | collective-permute-done | bytes 1048608 | tf_op jit(solution)/shard_map/ppermute | solution.py:520
  32.2 0.0 collective-permute-done.partner_hbm
  32.2 0.4 collective-permute-done.1.other_hbm
  32.6 22.3 %fine.1 = (f32[2,2,72,256]{3,2,1,0:T(8,128)S(1)}, f32[2,2,72,256]{3,2,1,0:T(8,128)S(1)}, f32[2,2,72,256]{3,2,1,0:T(8,128)S(1)}, f32[6,72,256]{2,1,0:T(8,128)S(1)}) custom-call(s32[14]{0:T(128)S(1)} %pad_add_fusion.flag_ref, f32[4,144,512]{2,1,0:T(8,128)S(1)} %get-tuple-element.24.c_hbm, f32[4,144,512]{2,1,0:T(8,128)} %collective-permute-done.partner_hbm, ...), custom_call_target="tpu_custom_call" | custom-call | tf_op jit(solution)/shard_map/fine/pallas_call | solution.py:532
  54.9 0.1 collective-permute-start.3
  55.0 3.2 %collective-permute-start.4 = (f32[2,2,72,256]{3,2,1,0:T(8,128)S(1)}, f32[2,2,72,256]{3,2,1,0:T(8,128)S(1)}, u32[]{:S(2)}, u32[]{:S(2)}) collective-permute-start(f32[2,2,72,256]{3,2,1,0:T(8,128)S(1)} %get-tuple-element.28), channel_id=1, source_target_pairs={{1,2},{2,1},{3,4},{4,3},{5,6},{6,5},{9,10},{10,9},{11,12},{12,11},... | collective-permute-start | bytes 884744 | tf_op jit(solution)/shard_map/ppermute | solution.py:505
  58.1 0.0 collective-permute-done.3.partner_ref
  58.1 8.2 %collective-permute-done.4.other_ref = f32[2,2,72,256]{3,2,1,0:T(8,128)S(1)} collective-permute-done((f32[2,2,72,256]{3,2,1,0:T(8,128)S(1)}, f32[2,2,72,256]{3,2,1,0:T(8,128)S(1)}, u32[]{:S(2)}, u32[]{:S(2)}) %collective-permute-start.4) | collective-permute-done | bytes 294944 | tf_op jit(solution)/shard_map/ppermute | solution.py:505
  66.3 0.6 gather.1
  66.9 0.1 collective-permute-start.5
  67.0 2.4 %collective-permute-start.6 = (f32[3,72,256]{2,1,0:T(8,128)S(1)}, f32[3,72,256]{2,1,0:T(8,128)S(1)}, u32[]{:S(2)}, u32[]{:S(2)}) collective-permute-start(f32[3,72,256]{2,1,0:T(8,128)S(1)} %get-tuple-element.32), channel_id=1, source_target_pairs={{1,2},{2,1},{3,4},{4,3},{5,6},{6,5},{9,10},{10,9},{11,12},{12,11},... | collective-permute-start | bytes 663560 | tf_op jit(solution)/shard_map/ppermute | solution.py:505
  69.5 0.2 weights.1.weight_ref
  69.7 0.0 collective-permute-done.5.partner_ref
  69.7 6.4 %collective-permute-done.6.other_ref = f32[3,72,256]{2,1,0:T(8,128)S(1)} collective-permute-done((f32[3,72,256]{2,1,0:T(8,128)S(1)}, f32[3,72,256]{2,1,0:T(8,128)S(1)}, u32[]{:S(2)}, u32[]{:S(2)}) %collective-permute-start.6) | collective-permute-done | bytes 221216 | tf_op jit(solution)/shard_map/ppermute | solution.py:505
  76.1 1.0 %shard_map.46 = (f32[2,72,256]{2,1,0:T(8,128)S(1)}, f32[2,72,256]{2,1,0:T(8,128)S(1)}, f32[1,72,256]{2,1,0:T(8,128)S(1)}, f32[1,72,256]{2,1,0:T(8,128)S(1)}) custom-call(s32[14]{0:T(128)S(1)} %pad_add_fusion.flag_ref, f32[7,4,72,256]{3,2,1,0:T(8,128)S(1)} %weights.1.weight_ref, f32[3,72,256]{2,1,0:T(8,128)S(1)} %collective-permute-done.5.partner_ref, ...), custom_call_target="tpu_custom_call" | custom-call | tf_op jit(solution)/shard_map/pallas_call | solution.py:624
  77.1 0.0 copy-start
  77.2 0.1 collective-permute-start.7
  77.2 3.3 %collective-permute-start.8 = (f32[1,72,256]{2,1,0:T(8,128)S(1)}, f32[1,72,256]{2,1,0:T(8,128)S(1)}, u32[]{:S(2)}, u32[]{:S(2)}) collective-permute-start(f32[1,72,256]{2,1,0:T(8,128)S(1)} %get-tuple-element.37), channel_id=1, source_target_pairs={{1,2},{2,1},{3,4},{4,3},{5,6},{6,5},{9,10},{10,9},{11,12},{12,11},... | collective-permute-start | bytes 221192 | tf_op jit(solution)/shard_map/ppermute | solution.py:505
  80.5 0.6 shard_map.49
  81.1 0.4 collective-permute-start.10
  81.5 2.3 %collective-permute-start.11 = (f32[2,72,256]{2,1,0:T(8,128)S(1)}, f32[2,72,256]{2,1,0:T(8,128)S(1)}, u32[]{:S(2)}, u32[]{:S(2)}) collective-permute-start(f32[2,72,256]{2,1,0:T(8,128)S(1)} %get-tuple-element.42), channel_id=1, source_target_pairs={{0,24},{16,8},{24,16},{1,25},{17,9},{25,17},{2,26},{18,10},{26,18}... | collective-permute-start | bytes 442376 | tf_op jit(solution)/shard_map/ppermute | solution.py:613
  83.9 0.0 collective-permute-done.7.partner_ref
  83.9 0.0 collective-permute-done.8.other_ref
  83.9 1.4 %shard_map.47 = (f32[2,72,256]{2,1,0:T(8,128)S(1)}, f32[1,72,256]{2,1,0:T(8,128)}, f32[1,72,256]{2,1,0:T(8,128)}) custom-call(s32[14]{0:T(128)S(1)} %pad_add_fusion.flag_ref, f32[7,4,72,256]{3,2,1,0:T(8,128)S(1)} %weights.1.weight_ref, f32[1,72,256]{2,1,0:T(8,128)S(1)} %collective-permute-done.7.partner_ref, ...), custom_call_target="tpu_custom_call" | custom-call | tf_op jit(solution)/shard_map/pallas_call | solution.py:624
  85.3 0.6 shard_map.48
  85.9 3.4 %collective-permute-start.9 = (f32[2,72,256]{2,1,0:T(8,128)S(1)}, f32[2,72,256]{2,1,0:T(8,128)S(1)}, u32[]{:S(2)}, u32[]{:S(2)}) collective-permute-start(f32[2,72,256]{2,1,0:T(8,128)S(1)} %get-tuple-element.40), channel_id=1, source_target_pairs={{0,8},{8,16},{16,24},{24,0},{1,9},{9,17},{17,25},{25,1},{2,10},{10... | collective-permute-start | bytes 442376 | tf_op jit(solution)/shard_map/ppermute | solution.py:613
  89.3 0.0 copy-done
  89.4 1.8 %base.1.base_ref = f32[4,256,512]{2,1,0:T(8,128)S(1)} custom-call(f32[4,256,512]{2,1,0:T(8,128)S(1)} %bitcast.9), custom_call_target="tpu_custom_call" | custom-call | flops 16000000 | tf_op jit(solution)/shard_map/base/pallas_call | solution.py:556
  91.2 2.3 %collective-permute-done.10.refs_2_ = f32[2,72,256]{2,1,0:T(8,128)S(1)} collective-permute-done((f32[2,72,256]{2,1,0:T(8,128)S(1)}, f32[2,72,256]{2,1,0:T(8,128)S(1)}, u32[]{:S(2)}, u32[]{:S(2)}) %collective-permute-start.10) | collective-permute-done | bytes 147488 | tf_op jit(solution)/shard_map/ppermute | solution.py:613
  93.5 0.0 collective-permute-done.11.refs_3_
  93.5 2.8 %collective-permute-done.9.refs_1_ = f32[2,72,256]{2,1,0:T(8,128)S(1)} collective-permute-done((f32[2,72,256]{2,1,0:T(8,128)S(1)}, f32[2,72,256]{2,1,0:T(8,128)S(1)}, u32[]{:S(2)}, u32[]{:S(2)}) %collective-permute-start.9) | collective-permute-done | bytes 147488 | tf_op jit(solution)/shard_map/ppermute | solution.py:613
  96.3 2.5 %final.1 = f32[4,256,512]{2,1,0:T(8,128)} custom-call(s32[14]{0:T(128)S(1)} %pad_add_fusion.flag_ref, f32[4,256,512]{2,1,0:T(8,128)S(1)} %base.1.base_ref, f32[2,72,256]{2,1,0:T(8,128)S(1)} %get-tuple-element.39.refs_0_, f32[2,72,256]{2,1,0:T(8,128)S(1)} %collective-permute-done.9.refs_1_, f32[2,72,256]{2,1,0:T(8,128)S(1)} %collective-permute-done.10.refs_2_, ...), custom_call_target="tpu_custom_call" | custom-call | tf_op jit(solution)/shard_map/final/pallas_call | solution.py:640
Async XLA Ops:
  1.6 30.6 %collective-permute-start = (f32[4,144,512]{2,1,0:T(8,128)S(1)}, f32[4,144,512]{2,1,0:T(8,128)}, u32[]{:S(2)}, u32[]{:S(2)}) collective-permute-start(f32[4,144,512]{2,1,0:T(8,128)S(1)} %get-tuple-element.24.c_hbm), channel_id=1, source_target_pairs={{0,1},{1,0},{2,3},{3,2},{4,5},{5,4},{6,7},{7,6},{8,9},{9,8},{10,11... | collective-permute-start | bytes 3538952 | tf_op jit(solution)/shard_map/ppermute | solution.py:502
  1.7 30.9 %collective-permute-start.1 = (f32[4,144,512]{2,1,0:T(8,128)S(1)}, f32[4,144,512]{2,1,0:T(8,128)}, u32[]{:S(2)}, u32[]{:S(2)}) collective-permute-start(f32[4,144,512]{2,1,0:T(8,128)S(1)} %get-tuple-element.24.c_hbm), channel_id=1, source_target_pairs={{1,2},{2,1},{3,4},{4,3},{5,6},{6,5},{9,10},{10,9},{11,12},{12,11},... | collective-permute-start | bytes 3538952 | tf_op jit(solution)/shard_map/ppermute | solution.py:505
  5.1 27.0 %collective-permute-start.2 = (f32[4,128,512]{2,1,0:T(8,128)S(1)}, f32[4,128,512]{2,1,0:T(8,128)S(1)}, u32[]{:S(2)}, u32[]{:S(2)}) collective-permute-start(f32[4,128,512]{2,1,0:T(8,128)S(1)} %get-tuple-element.25), channel_id=1, source_target_pairs={{0,8},{8,0},{16,24},{1,9},{9,1},{17,25},{2,10},{10,2},{18,26},{3,1... | collective-permute-start | bytes 3145736 | tf_op jit(solution)/shard_map/ppermute | solution.py:520
  54.9 3.2 %collective-permute-start.3 = (f32[2,2,72,256]{3,2,1,0:T(8,128)S(1)}, f32[2,2,72,256]{3,2,1,0:T(8,128)S(1)}, u32[]{:S(2)}, u32[]{:S(2)}) collective-permute-start(f32[2,2,72,256]{3,2,1,0:T(8,128)S(1)} %get-tuple-element.27), channel_id=1, source_target_pairs={{0,1},{1,0},{2,3},{3,2},{4,5},{5,4},{6,7},{7,6},{8,9},{9,8},{10,11... | collective-permute-start | bytes 884744 | tf_op jit(solution)/shard_map/ppermute | solution.py:502
  55.0 11.4 %collective-permute-start.4 = (f32[2,2,72,256]{3,2,1,0:T(8,128)S(1)}, f32[2,2,72,256]{3,2,1,0:T(8,128)S(1)}, u32[]{:S(2)}, u32[]{:S(2)}) collective-permute-start(f32[2,2,72,256]{3,2,1,0:T(8,128)S(1)} %get-tuple-element.28), channel_id=1, source_target_pairs={{1,2},{2,1},{3,4},{4,3},{5,6},{6,5},{9,10},{10,9},{11,12},{12,11},... | collective-permute-start | bytes 884744 | tf_op jit(solution)/shard_map/ppermute | solution.py:505
  66.9 2.8 %collective-permute-start.5 = (f32[3,72,256]{2,1,0:T(8,128)S(1)}, f32[3,72,256]{2,1,0:T(8,128)S(1)}, u32[]{:S(2)}, u32[]{:S(2)}) collective-permute-start(f32[3,72,256]{2,1,0:T(8,128)S(1)} %get-tuple-element.31), channel_id=1, source_target_pairs={{0,1},{1,0},{2,3},{3,2},{4,5},{5,4},{6,7},{7,6},{8,9},{9,8},{10,11... | collective-permute-start | bytes 663560 | tf_op jit(solution)/shard_map/ppermute | solution.py:502
  67.0 9.1 %collective-permute-start.6 = (f32[3,72,256]{2,1,0:T(8,128)S(1)}, f32[3,72,256]{2,1,0:T(8,128)S(1)}, u32[]{:S(2)}, u32[]{:S(2)}) collective-permute-start(f32[3,72,256]{2,1,0:T(8,128)S(1)} %get-tuple-element.32), channel_id=1, source_target_pairs={{1,2},{2,1},{3,4},{4,3},{5,6},{6,5},{9,10},{10,9},{11,12},{12,11},... | collective-permute-start | bytes 663560 | tf_op jit(solution)/shard_map/ppermute | solution.py:505
  77.1 12.2 %copy-start = (f32[1,4,256,512]{3,2,1,0:T(8,128)S(1)}, f32[1,4,256,512]{3,2,1,0:T(8,128)}, u32[]{:S(2)}) copy-start(f32[1,4,256,512]{3,2,1,0:T(8,128)} %param.5) | copy-start | bytes 6291460
  77.2 6.7 %collective-permute-start.7 = (f32[1,72,256]{2,1,0:T(8,128)S(1)}, f32[1,72,256]{2,1,0:T(8,128)S(1)}, u32[]{:S(2)}, u32[]{:S(2)}) collective-permute-start(f32[1,72,256]{2,1,0:T(8,128)S(1)} %get-tuple-element.36), channel_id=1, source_target_pairs={{0,1},{1,0},{2,3},{3,2},{4,5},{5,4},{6,7},{7,6},{8,9},{9,8},{10,11... | collective-permute-start | bytes 221192 | tf_op jit(solution)/shard_map/ppermute | solution.py:502
  77.2 6.7 %collective-permute-start.8 = (f32[1,72,256]{2,1,0:T(8,128)S(1)}, f32[1,72,256]{2,1,0:T(8,128)S(1)}, u32[]{:S(2)}, u32[]{:S(2)}) collective-permute-start(f32[1,72,256]{2,1,0:T(8,128)S(1)} %get-tuple-element.37), channel_id=1, source_target_pairs={{1,2},{2,1},{3,4},{4,3},{5,6},{6,5},{9,10},{10,9},{11,12},{12,11},... | collective-permute-start | bytes 221192 | tf_op jit(solution)/shard_map/ppermute | solution.py:505
  81.1 12.4 %collective-permute-start.10 = (f32[2,72,256]{2,1,0:T(8,128)S(1)}, f32[2,72,256]{2,1,0:T(8,128)S(1)}, u32[]{:S(2)}, u32[]{:S(2)}) collective-permute-start(f32[2,72,256]{2,1,0:T(8,128)S(1)} %get-tuple-element.41), channel_id=1, source_target_pairs={{0,16},{8,24},{16,0},{24,8},{1,17},{9,25},{17,1},{25,9},{2,18},{10... | collective-permute-start | bytes 442376 | tf_op jit(solution)/shard_map/ppermute | solution.py:613
  81.5 12.0 %collective-permute-start.11 = (f32[2,72,256]{2,1,0:T(8,128)S(1)}, f32[2,72,256]{2,1,0:T(8,128)S(1)}, u32[]{:S(2)}, u32[]{:S(2)}) collective-permute-start(f32[2,72,256]{2,1,0:T(8,128)S(1)} %get-tuple-element.42), channel_id=1, source_target_pairs={{0,24},{16,8},{24,16},{1,25},{17,9},{25,17},{2,26},{18,10},{26,18}... | collective-permute-start | bytes 442376 | tf_op jit(solution)/shard_map/ppermute | solution.py:613
  85.9 10.4 %collective-permute-start.9 = (f32[2,72,256]{2,1,0:T(8,128)S(1)}, f32[2,72,256]{2,1,0:T(8,128)S(1)}, u32[]{:S(2)}, u32[]{:S(2)}) collective-permute-start(f32[2,72,256]{2,1,0:T(8,128)S(1)} %get-tuple-element.40), channel_id=1, source_target_pairs={{0,8},{8,16},{16,24},{24,0},{1,9},{9,17},{17,25},{25,1},{2,10},{10... | collective-permute-start | bytes 442376 | tf_op jit(solution)/shard_map/ppermute | solution.py:613

commit v5 on v4

--- a/solution.py
+++ b/solution.py
@@ -67,11 +67,23 @@
     return slice(8 * i, 8 * i + 8)
 
 
-def dealt_mean(load, tiles, select):
-    sums = [
-        (load(0, 2 * i) + load(1, 2 * i)) + (load(0, 2 * i + 1) + load(1, 2 * i + 1)) for i in range(tiles // 2)
-    ]
-    return 0.125 * split_dot(jnp.concatenate(sums, axis=0), select)
+def pair_lanes(blocks):
+    lane = lax.broadcasted_iota(jnp.int32, (8, 128), 1)
+    place = 2 * (lane % 64)
+    out = []
+    for first, second in zip(blocks[::2], blocks[1::2]):
+        halves = [
+            jnp.take_along_axis(x + pltpu.roll(x, 127, 1), place, axis=1, mode="promise_in_bounds") for x in (first, second)
+        ]
+        out.append(jnp.where(lane < 64, *halves))
+    return out
+
+
+def dealt_mean(load, tiles, store):
+    for i in range(tiles // 2):
+        total = (load(0, 2 * i) + load(1, 2 * i)) + (load(0, 2 * i + 1) + load(1, 2 * i + 1))
+        blocks = [total[:, 128 * j : 128 * j + 128] for j in range(total.shape[1] // 128)]
+        store(i, 0.125 * jnp.concatenate(pair_lanes(blocks), axis=1))
 
 
 def weights_plane(load, store, rows, lanes):
@@ -155,7 +167,6 @@
     own_rows = rows - MARGIN
     tiles = rows // 8
     columns = [slice(128 * j, 128 * j + 128) for j in range(lanes // 128)]
-    select = pairing(lanes)
     coarse_planes, reach = depth // 2, planes // 2
     coarse_rows, coarse_lanes = rows // 2, lanes // 2
     last_plane = depth - 1
@@ -231,11 +242,17 @@
             c = c_scr[z, tile(i), :]
             w_scr[k, z, tile(i), :] = jnp.where(c > 0.0, c + c_scr[inner, tile(i), :], 0.0)
 
-    def restrict_c(q, _):
-        cc_scr[q] = dealt_mean(lambda dz, i: c_scr[2 * q + dz, tile(i), :], tiles, select)
+    def restrict_c(n, _):
+        for q in range(reach):
+            at = n * reach + q
+
+            def store(i, mean):
+                cc_scr[at, tile(i), :] = mean
+
+            dealt_mean(lambda dz, i: c_scr[2 * at + dz, tile(i), :], tiles, store)
         return 0
 
-    lax.fori_loop(0, coarse_planes, restrict_c, 0)
+    lax.fori_loop(0, coarse_planes // reach, restrict_c, 0)
     for q in range(reach):
         def load(dz, i):
             return cc_scr[reach + q + dz, tile(i), :]
@@ -258,12 +275,15 @@
 
     lax.fori_loop(0, planes, deal_v, 0)
 
-    def keep(n, _):
-        f, q = n // reach, n % reach
-        keep_scr[n] = dealt_mean(lambda dz, i: a_scr[f, planes + 2 * q + dz, tile(i), :], tiles, select)
+    def keep(f, _):
+        for q in range(reach):
+            def store(i, mean):
+                keep_scr[f * reach + q, tile(i), :] = mean
+
+            dealt_mean(lambda dz, i: a_scr[f, planes + 2 * q + dz, tile(i), :], tiles, store)
         return 0
 
-    lax.fori_loop(0, 2 * reach, keep, 0)
+    lax.fori_loop(0, 2, keep, 0)
     for number in range(STEPS):
         v_in, v_out = (a_scr, b_scr) if number % 2 == 0 else (b_scr, a_scr)
 
@@ -308,31 +328,45 @@
 
         step_plane(weight, load, store, coarse_rows, coarse_lanes, 2)
 
-    def mean_of(f, q):
-        return dealt_mean(lambda dz, i: result[f, 2 * q + dz, tile(i), :], tiles, select)
+    def finish(f, q, put):
+        dealt_mean(lambda dz, i: result[f, 2 * q + dz, tile(i), :], tiles, put)
 
     low_c, high_c = cc_scr[reach - 1], cc_scr[2 * reach]
-    low_w = jnp.where(low_c > 0.0, low_c + cc_scr[reach], 0.0)
-    high_w = jnp.where(high_c > 0.0, high_c + cc_scr[2 * reach - 1], 0.0)
-    for f in range(2):
+    coarse_ref[0, 0] = jnp.where(low_c > 0.0, low_c + cc_scr[reach], 0.0)
+    coarse_ref[0, 1] = jnp.where(high_c > 0.0, high_c + cc_scr[2 * reach - 1], 0.0)
+
+    def own_planes(f, _):
         for q in range(reach):
-            own_ref[f, q] = mean_of(f, reach + q) - own_ref[f, q]
-        for q in range(reach):
-            low, high = mean_of(f, q), mean_of(f, 2 * reach + q)
-            if q == reach - 1:
-                low = low - low_w * keep_scr[f * reach]
-            if q == 0:
-                high = high - high_w * keep_scr[f * reach + reach - 1]
-
-            @pl.when(upper == 1)
-            def _():
-                to_partner_ref[f, q] = high
-                to_other_ref[f, q] = low
-
-            @pl.when(upper == 0)
-            def _():
-                to_partner_ref[f, q] = low
-                to_other_ref[f, q] = high
+            def put(i, mean):
+                own_ref[f, q, tile(i), :] = mean - own_ref[f, q, tile(i), :]
+
+            finish(f, reach + q, put)
+        return 0
+
+    lax.fori_loop(0, 2, own_planes, 0)
+
+    def far_planes(into_ref, side, base, edge, kept):
+        def one(f, _):
+            for q in range(reach):
+                def put(i, mean):
+                    into_ref[f, q, tile(i), :] = mean
+
+                finish(f, base + q, put)
+            return 0
+
+        lax.fori_loop(0, 2, one, 0)
+        for f in range(2):
+            into_ref[f, edge] = into_ref[f, edge] - coarse_ref[0, side] * keep_scr[f * reach + kept]
+
+    @pl.when(upper == 1)
+    def _():
+        far_planes(to_partner_ref, 1, 2 * reach, 0, reach - 1)
+        far_planes(to_other_ref, 0, 0, reach - 1, 0)
+
+    @pl.when(upper == 0)
+    def _():
+        far_planes(to_partner_ref, 0, 0, reach - 1, 0)
+        far_planes(to_other_ref, 1, 2 * reach, 0, reach - 1)
 
 
 def weight_kernel(cc_ref, weight_ref):
@@ -374,49 +408,50 @@
         step_plane(weight, load, store, rows, lanes)
 
 
-def double_kernel(slots, flag_ref, weight_ref, partner_ref, other_ref, extra_ref, val_ref,
-                  first_ref, second_ref, to_partner_ref, to_other_ref, wide, extra_wide, middle):
-    upper = flag_ref[1]
-    planes, rows, lanes = val_ref.shape
-    extra_wide[1 : planes + 1] = extra_ref[...]
-    wide[planes : 2 * planes] = val_ref[...]
-    for ref, above in ((partner_ref, upper), (other_ref, 1 - upper)):
-        wide[pl.ds(above * (2 * planes), planes)] = ref[0:planes]
-        extra_wide[above * (planes + 1)] = ref[planes]
-    add = [flag_ref[slot].astype(F32) for slot in slots]
-    coarse_advance(weight_ref, 0, wide.at[planes - 2 :], middle, planes + 2, extra_wide, add[0], rows, lanes)
-    first_ref[...] = middle[1 : planes + 1]
-    coarse_advance(weight_ref, 1, middle, second_ref, planes, extra_ref, add[1], rows, lanes)
-    low, high = second_ref[0], second_ref[planes - 1]
-    to_partner_ref[0] = jnp.where(upper == 1, high, low)
-    to_other_ref[0] = jnp.where(upper == 1, low, high)
-
-
-def single_kernel(slot, flag_ref, weight_ref, partner_ref, other_ref, extra_ref, val_ref,
-                  next_ref, to_partner_ref, to_other_ref, wide):
-    upper = flag_ref[1]
-    planes, rows, lanes = val_ref.shape
-    wide[1 : planes + 1] = val_ref[...]
-    wide[upper * (planes + 1)] = partner_ref[0]
-    wide[(1 - upper) * (planes + 1)] = other_ref[0]
-    coarse_advance(weight_ref, 1, wide, next_ref, planes, extra_ref, flag_ref[slot].astype(F32), rows, lanes)
-    low, high = next_ref[0], next_ref[planes - 1]
-    to_partner_ref[0] = jnp.where(upper == 1, high, low)
-    to_other_ref[0] = jnp.where(upper == 1, low, high)
-
-
-def pick_kernel(slots, count, flag_ref, *refs):
-    for slot, ref in zip(slots, refs[count:]):
+def pick(flag_ref, slots, sources, sends):
+    for slot, ref in zip(slots, sends):
         which = flag_ref[slot]
 
         @pl.when(which < 0)
         def _():
             ref[...] = jnp.zeros(ref.shape, F32)
 
-        for m, source in enumerate(refs[:count]):
+        for m, source in enumerate(sources):
             @pl.when(which == m)
             def _():
                 ref[...] = source[...]
+
+
+def chain_kernel(slots, send_slots, count, edges, flag_ref, weight_ref, partner_ref, other_ref, extra_ref, *refs):
+    upper = flag_ref[1]
+    refs = list(refs)
+    values = refs[:count]
+    made = refs[count : count + len(slots)]
+    rest = refs[count + len(slots) :]
+    to_sides, rest = rest[: 2 * edges], rest[2 * edges :]
+    sends, (wide, extra_wide, middle) = rest[: len(send_slots)], rest[len(send_slots) :]
+    val_ref = values[-1]
+    planes, rows, lanes = val_ref.shape
+    add = [flag_ref[slot].astype(F32) for slot in slots]
+    wide[planes : 2 * planes] = val_ref[...]
+    sides = ((partner_ref, upper), (other_ref, 1 - upper))
+    if len(slots) == 2:
+        extra_wide[1 : planes + 1] = extra_ref[...]
+        for ref, above in sides:
+            wide[pl.ds(above * (2 * planes), planes)] = ref[0:planes]
+            extra_wide[above * (planes + 1)] = ref[planes]
+        coarse_advance(weight_ref, 0, wide.at[planes - 2 :], middle, planes + 2, extra_wide, add[0], rows, lanes)
+        made[0][...] = middle[1 : planes + 1]
+        coarse_advance(weight_ref, 1, middle, made[1], planes, extra_ref, add[1], rows, lanes)
+    else:
+        for ref, above in sides:
+            wide[planes - 1 + above * (planes + 1)] = ref[0]
+        coarse_advance(weight_ref, 1, wide.at[planes - 1 :], made[0], planes, extra_ref, add[0], rows, lanes)
+    if edges:
+        low, high = made[-1][0], made[-1][planes - 1]
+        to_sides[0][0] = jnp.where(upper == 1, high, low)
+        to_sides[1][0] = jnp.where(upper == 1, low, high)
+    pick(flag_ref, send_slots, values + made, sends)
 
 
 def base_kernel(iterate_ref, out_ref, rows_scr, fine_scr):
@@ -590,52 +625,43 @@
     ready = [max(row[1 + layers + shift] for row in table) for shift in range(layers)]
     arrived = [None] * layers
     values = [val]
-    done = -1
-
-    def deliver():
-        upto = len(values) - 1
-        shifts = [shift for shift in range(layers) if done < max(ready[shift], 0) <= upto]
-        if not shifts:
-            return upto
-        sends = pl.pallas_call(
-            functools.partial(pick_kernel, [send_at + shift for shift in shifts], len(values)),
-            out_shape=(block,) * len(shifts),
-            in_specs=[smem] + whole(len(values)),
-            out_specs=tuple(whole(len(shifts))),
-            compiler_params=params(VMEM_LIMITS["small"]),
-        )(flags, *values)
-        for shift, send in zip(shifts, sends):
+    sent = []
+    while len(values) < layers:
+        from_other = other_swap(to_other)
+        from_partner = partner_swap(to_partner)
+        for shift, send in sent:
             pairs = [
                 (source, (source + shift) % layers)
                 for source in range(layers)
                 if table[source][1 + layers + shift] >= 0
             ]
             arrived[shift] = lax.ppermute(send, "tm", pairs) if shift else send
-        return upto
-
-    number = 1
-    while number < layers:
-        from_other = other_swap(to_other)
-        from_partner = partner_swap(to_partner)
-        if number > 1:
-            done = deliver()
-        double = number == 1 and number + 1 < layers
-        slots = [add_at + number - 1 + n for n in range(1 + double)]
-        *made, to_partner, to_other = pl.pallas_call(
-            functools.partial(double_kernel, slots) if double else functools.partial(single_kernel, slots[0]),
-            out_shape=(*[block] * len(slots), plane, plane),
-            in_specs=[smem] + whole(5),
-            out_specs=tuple(whole(2 + len(slots))),
+        count = len(values)
+        steps = 2 if count == 1 and layers > 2 else 1
+        more = count + steps < layers
+        slots = [add_at + count - 1 + n for n in range(steps)]
+        shifts = [shift for shift in range(layers) if arrived[shift] is None and ready[shift] < count + steps]
+        made = pl.pallas_call(
+            functools.partial(chain_kernel, slots, [send_at + shift for shift in shifts], count, int(more)),
+            out_shape=(*[block] * steps, *[plane] * (2 * more), *[block] * len(shifts)),
+            in_specs=[smem] + whole(4 + count),
+            out_specs=tuple(whole(steps + 2 * more + len(shifts))),
             scratch_shapes=[
                 VMEM((3 * reach, coarse_rows, coarse_lanes), F32),
                 VMEM((reach + 2, coarse_rows, coarse_lanes), F32),
                 VMEM((reach + 2, coarse_rows, coarse_lanes), F32),
-            ] if double else [VMEM((reach + 2, coarse_rows, coarse_lanes), F32)],
+            ],
             compiler_params=params(VMEM_LIMITS["small"]),
-        )(flags, weights, from_partner, from_other, extra, values[-1])
-        values += made
-        number += len(slots)
-    deliver()
+        )(flags, weights, from_partner, from_other, extra, *values)
+        values += made[:steps]
+        if more:
+            to_partner, to_other = made[steps : steps + 2]
+        sent = list(zip(shifts, made[steps + 2 * more :]))
+    for shift, send in sent:
+        pairs = [
+            (source, (source + shift) % layers) for source in range(layers) if table[source][1 + layers + shift] >= 0
+        ]
+        arrived[shift] = lax.ppermute(send, "tm", pairs) if shift else send
 
     corrected = pl.pallas_call(
         functools.partial(final_kernel, [half_at + shift for shift in range(layers)]),

time: 100 us -> 98.1 us (0.981)
  Pallas kernels: 32.7 us -> 30.1 us
  waiting for transfers between devices: 45 us -> 46.3 us
    pallas_call x1, Pallas kernels: 22.3 us -> 20.7 us  [local(): pl.pallas_call(functools.partial(fine_kernel, planes), out_shape=(fields,...]
    pallas_call x4 -> x2, Pallas kernels: 3.64 us -> 2.55 us  [local(): pl.pallas_call(functools.partial(chain_kernel, slots, [send_at + shift fo...]
  transfers between devices with their start and end apart: 12 -> 12, of which waited for: 6 -> 7; matrix products, arithmetic and copies ran while one was open for 1% -> 1% of each run, Pallas kernels for 5% -> 4%
where the time goes in v5:
time: 98.1 us; the launch traced here: 96.8 us
  waiting for transfers between devices  46.3 us (47%)
  Pallas kernels  30.1 us (31%)
  starting transfers between devices  19.3 us (20%)
    ppermute x1, waiting for transfers between devices, local(): received = lax.ppermute(to_row_partner, 'tm', row_pairs)  24.9 us
    pallas_call x1, Pallas kernels, local(): pl.pallas_call(functools.partial(fine_kernel, planes), out_shape=(fields,...  20.7 us
    ppermute x4, waiting for transfers between devices, other_swap(): return lax.ppermute(x, 'space', swap_pairs(slabs, 1))  15.7 us
    ppermute x4, starting transfers between devices, other_swap(): return lax.ppermute(x, 'space', swap_pairs(slabs, 1))  12.3 us
    ppermute x3, waiting for transfers between devices, local(): arrived[shift] = lax.ppermute(send, 'tm', pairs) if shift else send  5.78 us
    ppermute x3, starting transfers between devices, local(): arrived[shift] = lax.ppermute(send, 'tm', pairs) if shift else send  5.46 us
    pallas_call x2, Pallas kernels, local(): pl.pallas_call(functools.partial(chain_kernel, slots, [send_at + shift fo...  2.55 us
    pallas_call x1, Pallas kernels, local(): pl.pallas_call(functools.partial(final_kernel, [half_at + shift for shift...  2.52 us
  transfers between devices with their start and end apart: 12, of which 7 were waited for; matrix products, arithmetic and copies ran while one was open for 1% of the time, Pallas kernels for 4%

profile of v5, /device:TPU:28, one launch (start us, length us, event | category | flops | bytes accessed | tf_op | source)
XLA Modules:
  0.0 96.8 jit_solution(41806496819129653)
XLA Ops:
  0.0 1.6 %slices.1 = (f32[4,144,512]{2,1,0:T(8,128)S(1)}, f32[4,128,512]{2,1,0:T(8,128)S(1)}) custom-call(f32[4,256,512]{2,1,0:T(8,128)} %c_hbm.1, f32[4,256,512]{2,1,0:T(8,128)} %bitcast.7), custom_call_target="tpu_custom_call" | custom-call | tf_op jit(solution)/shard_map/slices/pallas_call | solution.py:544
  1.6 0.1 collective-permute-start
  1.7 3.4 %collective-permute-start.1 = (f32[4,144,512]{2,1,0:T(8,128)S(1)}, f32[4,144,512]{2,1,0:T(8,128)}, u32[]{:S(2)}, u32[]{:S(2)}) collective-permute-start(f32[4,144,512]{2,1,0:T(8,128)S(1)} %get-tuple-element.23.c_hbm), channel_id=1, source_target_pairs={{1,2},{2,1},{3,4},{4,3},{5,6},{6,5},{9,10},{10,9},{11,12},{12,11},... | collective-permute-start | bytes 3538952 | tf_op jit(solution)/shard_map/ppermute | solution.py:540
  5.1 1.3 %collective-permute-start.2 = (f32[4,128,512]{2,1,0:T(8,128)S(1)}, f32[4,128,512]{2,1,0:T(8,128)S(1)}, u32[]{:S(2)}, u32[]{:S(2)}) collective-permute-start(f32[4,128,512]{2,1,0:T(8,128)S(1)} %get-tuple-element.24), channel_id=1, source_target_pairs={{0,8},{8,0},{16,24},{1,9},{9,1},{17,25},{2,10},{10,2},{18,26},{3,1... | collective-permute-start | bytes 3145736 | tf_op jit(solution)/shard_map/ppermute | solution.py:555
  6.4 0.7 constant_dynamic-slice_fusion
  7.1 0.1 slice_bitcast_fusion
  7.2 0.1 pad_add_fusion.flag_ref
  7.3 24.9 %collective-permute-done.2.received_hbm = f32[4,128,512]{2,1,0:T(8,128)S(1)} collective-permute-done((f32[4,128,512]{2,1,0:T(8,128)S(1)}, f32[4,128,512]{2,1,0:T(8,128)S(1)}, u32[]{:S(2)}, u32[]{:S(2)}) %collective-permute-start.2) | collective-permute-done | bytes 1048608 | tf_op jit(solution)/shard_map/ppermute | solution.py:555
  32.2 0.0 collective-permute-done.partner_hbm
  32.2 0.4 collective-permute-done.1.other_hbm
  32.6 20.7 %fine.1 = (f32[2,2,72,256]{3,2,1,0:T(8,128)S(1)}, f32[2,2,72,256]{3,2,1,0:T(8,128)S(1)}, f32[2,2,72,256]{3,2,1,0:T(8,128)S(1)}, f32[6,72,256]{2,1,0:T(8,128)S(1)}) custom-call(s32[14]{0:T(128)S(1)} %pad_add_fusion.flag_ref, f32[4,144,512]{2,1,0:T(8,128)S(1)} %get-tuple-element.23.c_hbm, f32[4,144,512]{2,1,0:T(8,128)} %collective-permute-done.partner_hbm, ...), custom_call_target="tpu_custom_call" | custom-call | tf_op jit(solution)/shard_map/fine/pallas_call | solution.py:567
  53.3 0.1 collective-permute-start.3
  53.4 3.1 %collective-permute-start.4 = (f32[2,2,72,256]{3,2,1,0:T(8,128)S(1)}, f32[2,2,72,256]{3,2,1,0:T(8,128)S(1)}, u32[]{:S(2)}, u32[]{:S(2)}) collective-permute-start(f32[2,2,72,256]{3,2,1,0:T(8,128)S(1)} %get-tuple-element.28), channel_id=1, source_target_pairs={{1,2},{2,1},{3,4},{4,3},{5,6},{6,5},{9,10},{10,9},{11,12},{12,11},... | collective-permute-start | bytes 884744 | tf_op jit(solution)/shard_map/ppermute | solution.py:540
  56.5 0.0 collective-permute-done.3.partner_ref
  56.5 8.2 %collective-permute-done.4.other_ref = f32[2,2,72,256]{3,2,1,0:T(8,128)S(1)} collective-permute-done((f32[2,2,72,256]{3,2,1,0:T(8,128)S(1)}, f32[2,2,72,256]{3,2,1,0:T(8,128)S(1)}, u32[]{:S(2)}, u32[]{:S(2)}) %collective-permute-start.4) | collective-permute-done | bytes 294944 | tf_op jit(solution)/shard_map/ppermute | solution.py:540
  64.7 0.6 gather.1
  65.3 0.1 collective-permute-start.5
  65.4 2.5 %collective-permute-start.6 = (f32[3,72,256]{2,1,0:T(8,128)S(1)}, f32[3,72,256]{2,1,0:T(8,128)S(1)}, u32[]{:S(2)}, u32[]{:S(2)}) collective-permute-start(f32[3,72,256]{2,1,0:T(8,128)S(1)} %get-tuple-element.30), channel_id=1, source_target_pairs={{1,2},{2,1},{3,4},{4,3},{5,6},{6,5},{9,10},{10,9},{11,12},{12,11},... | collective-permute-start | bytes 663560 | tf_op jit(solution)/shard_map/ppermute | solution.py:540
  67.9 0.2 weights.1.weight_ref
  68.1 0.0 collective-permute-done.5.partner_ref
  68.2 6.4 %collective-permute-done.6.other_ref = f32[3,72,256]{2,1,0:T(8,128)S(1)} collective-permute-done((f32[3,72,256]{2,1,0:T(8,128)S(1)}, f32[3,72,256]{2,1,0:T(8,128)S(1)}, u32[]{:S(2)}, u32[]{:S(2)}) %collective-permute-start.6) | collective-permute-done | bytes 221216 | tf_op jit(solution)/shard_map/ppermute | solution.py:540
  74.5 1.1 %shard_map.46 = (f32[2,72,256]{2,1,0:T(8,128)S(1)}, f32[2,72,256]{2,1,0:T(8,128)S(1)}, f32[1,72,256]{2,1,0:T(8,128)S(1)}, f32[1,72,256]{2,1,0:T(8,128)S(1)}, f32...) custom-call(s32[14]{0:T(128)S(1)} %pad_add_fusion.flag_ref, f32[7,4,72,256]{3,2,1,0:T(8,128)S(1)} %weights.1.weight_ref, ...), custom_call_target="tpu_custom_call" | custom-call | tf_op jit(solution)/shard_map/pallas_call | solution.py:644
  75.7 0.0 copy-start
  75.7 0.1 collective-permute-start.7
  75.7 3.2 %collective-permute-start.8 = (f32[1,72,256]{2,1,0:T(8,128)S(1)}, f32[1,72,256]{2,1,0:T(8,128)S(1)}, u32[]{:S(2)}, u32[]{:S(2)}) collective-permute-start(f32[1,72,256]{2,1,0:T(8,128)S(1)} %get-tuple-element.34), channel_id=1, source_target_pairs={{1,2},{2,1},{3,4},{4,3},{5,6},{6,5},{9,10},{10,9},{11,12},{12,11},... | collective-permute-start | bytes 221192 | tf_op jit(solution)/shard_map/ppermute | solution.py:540
  79.0 0.4 collective-permute-start.10
  79.4 2.3 %collective-permute-start.11 = (f32[2,72,256]{2,1,0:T(8,128)S(1)}, f32[2,72,256]{2,1,0:T(8,128)S(1)}, u32[]{:S(2)}, u32[]{:S(2)}) collective-permute-start(f32[2,72,256]{2,1,0:T(8,128)S(1)} %get-tuple-element.40), channel_id=1, source_target_pairs={{0,24},{16,8},{24,16},{1,25},{17,9},{25,17},{2,26},{18,10},{26,18}... | collective-permute-start | bytes 442376 | tf_op jit(solution)/shard_map/ppermute | solution.py:638
  81.8 0.0 collective-permute-done.7.partner_ref
  81.8 0.7 collective-permute-done.8.other_ref
  82.4 1.4 %shard_map.47 = (f32[2,72,256]{2,1,0:T(8,128)}, f32[2,72,256]{2,1,0:T(8,128)S(1)}, f32[2,72,256]{2,1,0:T(8,128)S(1)}) custom-call(s32[14]{0:T(128)S(1)} %pad_add_fusion.flag_ref, f32[7,4,72,256]{3,2,1,0:T(8,128)S(1)} %weights.1.weight_ref, f32[1,72,256]{2,1,0:T(8,128)S(1)} %collective-permute-done.7.partner_ref, ...), custom_call_target="tpu_custom_call" | custom-call | tf_op jit(solution)/shard_map/pallas_call | solution.py:644
  83.9 2.7 %collective-permute-start.9 = (f32[2,72,256]{2,1,0:T(8,128)S(1)}, f32[2,72,256]{2,1,0:T(8,128)S(1)}, u32[]{:S(2)}, u32[]{:S(2)}) collective-permute-start(f32[2,72,256]{2,1,0:T(8,128)S(1)} %get-tuple-element.38), channel_id=1, source_target_pairs={{0,8},{8,16},{16,24},{24,0},{1,9},{9,17},{17,25},{25,1},{2,10},{10... | collective-permute-start | bytes 442376 | tf_op jit(solution)/shard_map/ppermute | solution.py:664
  86.6 0.0 copy-done
  86.6 1.8 %base.1.base_ref = f32[4,256,512]{2,1,0:T(8,128)S(1)} custom-call(f32[4,256,512]{2,1,0:T(8,128)S(1)} %bitcast.9), custom_call_target="tpu_custom_call" | custom-call | flops 16000000 | tf_op jit(solution)/shard_map/base/pallas_call | solution.py:591
  88.5 2.9 %collective-permute-done.10.refs_2_ = f32[2,72,256]{2,1,0:T(8,128)S(1)} collective-permute-done((f32[2,72,256]{2,1,0:T(8,128)S(1)}, f32[2,72,256]{2,1,0:T(8,128)S(1)}, u32[]{:S(2)}, u32[]{:S(2)}) %collective-permute-start.10) | collective-permute-done | bytes 147488 | tf_op jit(solution)/shard_map/ppermute | solution.py:638
  91.4 0.0 collective-permute-done.11.refs_3_
  91.4 2.9 %collective-permute-done.9.refs_1_ = f32[2,72,256]{2,1,0:T(8,128)S(1)} collective-permute-done((f32[2,72,256]{2,1,0:T(8,128)S(1)}, f32[2,72,256]{2,1,0:T(8,128)S(1)}, u32[]{:S(2)}, u32[]{:S(2)}) %collective-permute-start.9) | collective-permute-done | bytes 147488 | tf_op jit(solution)/shard_map/ppermute | solution.py:664
  94.2 2.5 %final.1 = f32[4,256,512]{2,1,0:T(8,128)} custom-call(s32[14]{0:T(128)S(1)} %pad_add_fusion.flag_ref, f32[4,256,512]{2,1,0:T(8,128)S(1)} %base.1.base_ref, f32[2,72,256]{2,1,0:T(8,128)S(1)} %get-tuple-element.37.refs_0_, f32[2,72,256]{2,1,0:T(8,128)S(1)} %collective-permute-done.9.refs_1_, f32[2,72,256]{2,1,0:T(8,128)S(1)} %collective-permute-done.10.refs_2_, ...), custom_call_target="tpu_custom_call" | custom-call | tf_op jit(solution)/shard_map/final/pallas_call | solution.py:666
Async XLA Ops:
  1.6 30.6 %collective-permute-start = (f32[4,144,512]{2,1,0:T(8,128)S(1)}, f32[4,144,512]{2,1,0:T(8,128)}, u32[]{:S(2)}, u32[]{:S(2)}) collective-permute-start(f32[4,144,512]{2,1,0:T(8,128)S(1)} %get-tuple-element.23.c_hbm), channel_id=1, source_target_pairs={{0,1},{1,0},{2,3},{3,2},{4,5},{5,4},{6,7},{7,6},{8,9},{9,8},{10,11... | collective-permute-start | bytes 3538952 | tf_op jit(solution)/shard_map/ppermute | solution.py:537
  1.7 30.9 %collective-permute-start.1 = (f32[4,144,512]{2,1,0:T(8,128)S(1)}, f32[4,144,512]{2,1,0:T(8,128)}, u32[]{:S(2)}, u32[]{:S(2)}) collective-permute-start(f32[4,144,512]{2,1,0:T(8,128)S(1)} %get-tuple-element.23.c_hbm), channel_id=1, source_target_pairs={{1,2},{2,1},{3,4},{4,3},{5,6},{6,5},{9,10},{10,9},{11,12},{12,11},... | collective-permute-start | bytes 3538952 | tf_op jit(solution)/shard_map/ppermute | solution.py:540
  5.1 27.0 %collective-permute-start.2 = (f32[4,128,512]{2,1,0:T(8,128)S(1)}, f32[4,128,512]{2,1,0:T(8,128)S(1)}, u32[]{:S(2)}, u32[]{:S(2)}) collective-permute-start(f32[4,128,512]{2,1,0:T(8,128)S(1)} %get-tuple-element.24), channel_id=1, source_target_pairs={{0,8},{8,0},{16,24},{1,9},{9,1},{17,25},{2,10},{10,2},{18,26},{3,1... | collective-permute-start | bytes 3145736 | tf_op jit(solution)/shard_map/ppermute | solution.py:555
  53.3 3.2 %collective-permute-start.3 = (f32[2,2,72,256]{3,2,1,0:T(8,128)S(1)}, f32[2,2,72,256]{3,2,1,0:T(8,128)S(1)}, u32[]{:S(2)}, u32[]{:S(2)}) collective-permute-start(f32[2,2,72,256]{3,2,1,0:T(8,128)S(1)} %get-tuple-element.27), channel_id=1, source_target_pairs={{0,1},{1,0},{2,3},{3,2},{4,5},{5,4},{6,7},{7,6},{8,9},{9,8},{10,11... | collective-permute-start | bytes 884744 | tf_op jit(solution)/shard_map/ppermute | solution.py:537
  53.4 11.3 %collective-permute-start.4 = (f32[2,2,72,256]{3,2,1,0:T(8,128)S(1)}, f32[2,2,72,256]{3,2,1,0:T(8,128)S(1)}, u32[]{:S(2)}, u32[]{:S(2)}) collective-permute-start(f32[2,2,72,256]{3,2,1,0:T(8,128)S(1)} %get-tuple-element.28), channel_id=1, source_target_pairs={{1,2},{2,1},{3,4},{4,3},{5,6},{6,5},{9,10},{10,9},{11,12},{12,11},... | collective-permute-start | bytes 884744 | tf_op jit(solution)/shard_map/ppermute | solution.py:540
  65.3 2.8 %collective-permute-start.5 = (f32[3,72,256]{2,1,0:T(8,128)S(1)}, f32[3,72,256]{2,1,0:T(8,128)S(1)}, u32[]{:S(2)}, u32[]{:S(2)}) collective-permute-start(f32[3,72,256]{2,1,0:T(8,128)S(1)} %get-tuple-element.29), channel_id=1, source_target_pairs={{0,1},{1,0},{2,3},{3,2},{4,5},{5,4},{6,7},{7,6},{8,9},{9,8},{10,11... | collective-permute-start | bytes 663560 | tf_op jit(solution)/shard_map/ppermute | solution.py:537
  65.4 9.1 %collective-permute-start.6 = (f32[3,72,256]{2,1,0:T(8,128)S(1)}, f32[3,72,256]{2,1,0:T(8,128)S(1)}, u32[]{:S(2)}, u32[]{:S(2)}) collective-permute-start(f32[3,72,256]{2,1,0:T(8,128)S(1)} %get-tuple-element.30), channel_id=1, source_target_pairs={{1,2},{2,1},{3,4},{4,3},{5,6},{6,5},{9,10},{10,9},{11,12},{12,11},... | collective-permute-start | bytes 663560 | tf_op jit(solution)/shard_map/ppermute | solution.py:540
  75.7 11.0 %copy-start = (f32[1,4,256,512]{3,2,1,0:T(8,128)S(1)}, f32[1,4,256,512]{3,2,1,0:T(8,128)}, u32[]{:S(2)}) copy-start(f32[1,4,256,512]{3,2,1,0:T(8,128)} %param.5) | copy-start | bytes 6291460
  75.7 6.1 %collective-permute-start.7 = (f32[1,72,256]{2,1,0:T(8,128)S(1)}, f32[1,72,256]{2,1,0:T(8,128)S(1)}, u32[]{:S(2)}, u32[]{:S(2)}) collective-permute-start(f32[1,72,256]{2,1,0:T(8,128)S(1)} %get-tuple-element.33), channel_id=1, source_target_pairs={{0,1},{1,0},{2,3},{3,2},{4,5},{5,4},{6,7},{7,6},{8,9},{9,8},{10,11... | collective-permute-start | bytes 221192 | tf_op jit(solution)/shard_map/ppermute | solution.py:537
  75.7 6.7 %collective-permute-start.8 = (f32[1,72,256]{2,1,0:T(8,128)S(1)}, f32[1,72,256]{2,1,0:T(8,128)S(1)}, u32[]{:S(2)}, u32[]{:S(2)}) collective-permute-start(f32[1,72,256]{2,1,0:T(8,128)S(1)} %get-tuple-element.34), channel_id=1, source_target_pairs={{1,2},{2,1},{3,4},{4,3},{5,6},{6,5},{9,10},{10,9},{11,12},{12,11},... | collective-permute-start | bytes 221192 | tf_op jit(solution)/shard_map/ppermute | solution.py:540
  79.0 12.4 %collective-permute-start.10 = (f32[2,72,256]{2,1,0:T(8,128)S(1)}, f32[2,72,256]{2,1,0:T(8,128)S(1)}, u32[]{:S(2)}, u32[]{:S(2)}) collective-permute-start(f32[2,72,256]{2,1,0:T(8,128)S(1)} %get-tuple-element.39), channel_id=1, source_target_pairs={{0,16},{8,24},{16,0},{24,8},{1,17},{9,25},{17,1},{25,9},{2,18},{10... | collective-permute-start | bytes 442376 | tf_op jit(solution)/shard_map/ppermute | solution.py:638
  79.4 12.0 %collective-permute-start.11 = (f32[2,72,256]{2,1,0:T(8,128)S(1)}, f32[2,72,256]{2,1,0:T(8,128)S(1)}, u32[]{:S(2)}, u32[]{:S(2)}) collective-permute-start(f32[2,72,256]{2,1,0:T(8,128)S(1)} %get-tuple-element.40), channel_id=1, source_target_pairs={{0,24},{16,8},{24,16},{1,25},{17,9},{25,17},{2,26},{18,10},{26,18}... | collective-permute-start | bytes 442376 | tf_op jit(solution)/shard_map/ppermute | solution.py:638
  83.9 10.3 %collective-permute-start.9 = (f32[2,72,256]{2,1,0:T(8,128)S(1)}, f32[2,72,256]{2,1,0:T(8,128)S(1)}, u32[]{:S(2)}, u32[]{:S(2)}) collective-permute-start(f32[2,72,256]{2,1,0:T(8,128)S(1)} %get-tuple-element.38), channel_id=1, source_target_pairs={{0,8},{8,16},{16,24},{24,0},{1,9},{9,17},{17,25},{25,1},{2,10},{10... | collective-permute-start | bytes 442376 | tf_op jit(solution)/shard_map/ppermute | solution.py:664

commit v6 on v5

--- a/solution.py
+++ b/solution.py
@@ -15,7 +15,7 @@
 F32 = jnp.float32
 VMEM = pltpu.VMEM
 MIB = 1024 * 1024
-VMEM_LIMITS = {"slices": 50 * MIB, "fine": 50 * MIB, "small": 10 * MIB, "final": 16 * MIB}
+VMEM_LIMITS = {"slices": 50 * MIB, "near": 6 * MIB, "fine": 34 * MIB, "small": 10 * MIB, "final": 16 * MIB}
 
 
 def params(limit):
@@ -159,23 +159,99 @@
     keep.wait()
 
 
-def fine_kernel(planes, flag_ref, c_hbm, partner_hbm, other_hbm, iterate_hbm, initial_hbm, received_hbm,
-                own_ref, to_partner_ref, to_other_ref, cc_scr,
-                c_raw, v_raw, c_scr, w_scr, a_scr, b_scr, coarse_ref, keep_scr, c_sem, v_sem):
+def weigh_planes(c_ref, w_refs, shift, count):
+    planes, rows, lanes = c_ref.shape
+    tiles = rows // 8
+
+    def one(n, _):
+        def load(dz, i):
+            return c_ref[n + 1 + dz, tile(i), :]
+
+        def store(k, i, w):
+            w_refs[k][n + 1 - shift, tile(i), :] = w
+
+        weights_plane(load, store, rows, lanes)
+        return 0
+
+    lax.fori_loop(0, count, one, 0)
+
+    def edge(k, z, inner, at):
+        for i in range(tiles):
+            c = c_ref[z, tile(i), :]
+            w_refs[k][at, tile(i), :] = jnp.where(c > 0.0, c + c_ref[inner, tile(i), :], 0.0)
+
+    @pl.when(shift == 1)
+    def _():
+        edge(5, planes - 1, planes - 2, planes - 2)
+
+    @pl.when(shift == 0)
+    def _():
+        edge(6, 0, 1, 0)
+
+
+def deal_planes(raw, c_ref, start, count):
+    tiles, blocks = c_ref.shape[1] // 8, raw.shape[1]
+
+    def one(z, _):
+        for j in range(blocks):
+            for i in range(tiles):
+                c_ref[start + z, tile(i), 128 * j : 128 * j + 128] = GAIN * raw[z, j, pl.ds(i, 8, tiles), :]
+        return 0
+
+    lax.fori_loop(0, count, one, 0)
+
+
+def coarse_means(c_ref, c_start, cc_ref, cc_start, count, reach):
+    tiles = c_ref.shape[1] // 8
+
+    def one(n, _):
+        for q in range(reach):
+            at = n * reach + q
+
+            def store(i, mean):
+                cc_ref[cc_start + at, tile(i), :] = mean
+
+            dealt_mean(lambda dz, i: c_ref[c_start + 2 * at + dz, tile(i), :], tiles, store)
+        return 0
+
+    lax.fori_loop(0, count // reach, one, 0)
+
+
+def near_kernel(planes, flag_ref, c_hbm, partner_hbm, *refs):
+    w_refs, (edge_ref, cc_ref, c_ref, raw, sem) = refs[:7], refs[7:]
+    upper = flag_ref[1]
+    blocks, reach = raw.shape[1], planes // 2
+    copies = [
+        pltpu.make_async_copy(ref.at[:, :, 128 * j : 128 * j + 128], raw.at[planes * n : planes * (n + 1), j], sem.at[n, j])
+        for n, ref in enumerate((c_hbm, partner_hbm))
+        for j in range(blocks)
+    ]
+    for copy in copies:
+        copy.start()
+    for copy in copies:
+        copy.wait()
+    deal_planes(raw.at[0:planes], c_ref, (1 - upper) * planes, planes)
+    deal_planes(raw.at[planes:], c_ref, upper * planes, planes)
+    weigh_planes(c_ref, w_refs, upper, 2 * planes - 2)
+    coarse_means(c_ref, 0, cc_ref, 0, 2 * reach, reach)
+    edge_ref[...] = c_ref[pl.ds((1 - upper) * (2 * planes - 2), 2)]
+
+
+def fine_kernel(planes, flag_ref, other_hbm, iterate_hbm, initial_hbm, received_hbm, *refs):
+    near_w, (edge_c, near_cc), refs = refs[:7], refs[7:9], refs[9:]
+    own_ref, to_partner_ref, to_other_ref, cc_scr, c_raw, v_raw, far_c, far_w, a_scr, b_scr = refs[:10]
+    coarse_ref, keep_scr, c_sem, v_sem = refs[10:]
+    far_w = [far_w.at[k] for k in range(7)]
     half, upper, last = flag_ref[0], flag_ref[1], flag_ref[2]
-    depth, rows, lanes = c_scr.shape
+    rows, lanes = edge_c.shape[1:]
     own_rows = rows - MARGIN
     tiles = rows // 8
     columns = [slice(128 * j, 128 * j + 128) for j in range(lanes // 128)]
-    coarse_planes, reach = depth // 2, planes // 2
+    reach = planes // 2
     coarse_rows, coarse_lanes = rows // 2, lanes // 2
-    last_plane = depth - 1
-
-    slabs = ((c_hbm, planes), (partner_hbm, upper * (2 * planes)), (other_hbm, (1 - upper) * (2 * planes)))
+
     c_copies = [
-        pltpu.make_async_copy(ref.at[:, :, column], c_raw.at[pl.ds(at, planes), j], c_sem.at[n, j])
-        for n, (ref, at) in enumerate(slabs)
-        for j, column in enumerate(columns)
+        pltpu.make_async_copy(other_hbm.at[:, :, column], c_raw.at[:, j], c_sem.at[j]) for j, column in enumerate(columns)
     ]
     for copy in c_copies:
         copy.start()
@@ -215,44 +291,11 @@
     for copy in c_copies:
         copy.wait()
 
-    def deal_c(z, _):
-        for j, column in enumerate(columns):
-            for i in range(tiles):
-                c_scr[z, tile(i), column] = GAIN * c_raw[z, j, pl.ds(i, 8, tiles), :]
-        return 0
-
-    lax.fori_loop(0, depth, deal_c, 0)
-
-    def weigh(z, _):
-        below, above = jnp.maximum(z - 1, 0), jnp.minimum(z + 1, last_plane)
-
-        def load(dz, i):
-            at = z if dz == 0 else (below if dz < 0 else above)
-            return c_scr[at, tile(i), :]
-
-        def store(k, i, w):
-            w_scr[k, z, tile(i), :] = w
-
-        weights_plane(load, store, rows, lanes)
-        return 0
-
-    lax.fori_loop(1, last_plane, weigh, 0)
-    for k, z, inner in ((6, 0, 1), (5, last_plane, last_plane - 1)):
-        for i in range(tiles):
-            c = c_scr[z, tile(i), :]
-            w_scr[k, z, tile(i), :] = jnp.where(c > 0.0, c + c_scr[inner, tile(i), :], 0.0)
-
-    def restrict_c(n, _):
-        for q in range(reach):
-            at = n * reach + q
-
-            def store(i, mean):
-                cc_scr[at, tile(i), :] = mean
-
-            dealt_mean(lambda dz, i: c_scr[2 * at + dz, tile(i), :], tiles, store)
-        return 0
-
-    lax.fori_loop(0, coarse_planes // reach, restrict_c, 0)
+    deal_planes(c_raw, far_c, (1 - upper) * 2, planes)
+    far_c[pl.ds(upper * planes, 2)] = edge_c[...]
+    weigh_planes(far_c, far_w, 1 - upper, planes)
+    cc_scr[pl.ds(upper * reach, 2 * reach)] = near_cc[...]
+    coarse_means(far_c, (1 - upper) * 2, cc_scr, (1 - upper) * (2 * reach), reach, reach)
     for q in range(reach):
         def load(dz, i):
             return cc_scr[reach + q + dz, tile(i), :]
@@ -284,31 +327,48 @@
         return 0
 
     lax.fori_loop(0, 2, keep, 0)
+    near_at, far_at = upper * (planes + 1), (1 - upper) * (2 * planes - 1)
     for number in range(STEPS):
         v_in, v_out = (a_scr, b_scr) if number % 2 == 0 else (b_scr, a_scr)
-
-        def advance(z, _):
-            below, above = jnp.maximum(z - 1, 0), jnp.minimum(z + 1, last_plane)
-
-            def load(f, dz, i):
-                at = z if dz == 0 else (below if dz < 0 else above)
-                return v_in[f, at, tile(i), :]
-
-            def weight(k, i):
-                return w_scr[k, z, tile(i), :]
-
-            def store(f, i, v):
-                v_out[f, z, tile(i), :] = v
-
-            step_plane(weight, load, store, rows, lanes, 2)
-            return 0
-
-        lax.fori_loop(planes - number, 2 * planes + number, advance, 0)
-        for k, z, inner in ((6, planes - 1 - number, planes - number), (5, 2 * planes + number, 2 * planes + number - 1)):
+        low, high = planes - number, 2 * planes + number
+
+        def advance_all(w_refs, w_at, start, count):
+            def advance(n, _):
+                z = start + n
+
+                def load(f, dz, i):
+                    return v_in[f, z + dz, tile(i), :]
+
+                def weight(k, i):
+                    return w_refs[k][z - w_at, tile(i), :]
+
+                def store(f, i, v):
+                    v_out[f, z, tile(i), :] = v
+
+                step_plane(weight, load, store, rows, lanes, 2)
+                return 0
+
+            lax.fori_loop(0, count, advance, 0)
+
+        advance_all(near_w, near_at, jnp.where(upper == 1, planes + 1, low), planes - 1 + number)
+        advance_all(far_w, far_at, jnp.where(upper == 1, low, 2 * planes - 1), 1 + number)
+
+        def reach_out(w_ref, w_at, z, inner):
             for i in range(tiles):
-                w = w_scr[k, z, tile(i), :]
+                w = w_ref[z - w_at, tile(i), :]
                 for f in range(2):
                     v_out[f, z, tile(i), :] = w * v_in[f, inner, tile(i), :]
+
+        @pl.when(upper == 1)
+        def _():
+            reach_out(far_w[6], 0, low - 1, low)
+            reach_out(near_w[5], planes + 1, high, high - 1)
+
+        @pl.when(upper == 0)
+        def _():
+            reach_out(near_w[6], 0, low - 1, low)
+            reach_out(far_w[5], 2 * planes - 1, high, high - 1)
+
     result = a_scr if STEPS % 2 == 0 else b_scr
 
     scale = jnp.where(last == 1, 0.0, 1.0).astype(F32)
@@ -562,31 +622,49 @@
     add_at, send_at, half_at = 3, 2 + layers, 2 + 2 * layers
     smem = pl.BlockSpec(memory_space=pltpu.SMEM)
 
+    def cost(microseconds):
+        return pl.CostEstimate(flops=int(microseconds * 4e6), bytes_accessed=0, transcendentals=0)
+
     fields = shape(2, reach, coarse_rows, coarse_lanes)
     blocks = lanes // 128
+    prepared = pl.pallas_call(
+        functools.partial(near_kernel, planes),
+        out_shape=(
+            *[shape(2 * planes - 1, rows, lanes)] * 7,
+            shape(2, rows, lanes),
+            shape(2 * reach, coarse_rows, coarse_lanes),
+        ),
+        in_specs=[smem] + [anywhere] * 2,
+        out_specs=tuple(whole(9)),
+        scratch_shapes=[
+            VMEM((2 * planes, rows, lanes), F32),
+            VMEM((2 * planes, blocks, rows, 128), F32),
+            pltpu.SemaphoreType.DMA((2, blocks)),
+        ],
+        compiler_params=params(VMEM_LIMITS["near"]),
+        cost_estimate=cost(6),
+        name="near",
+    )(flags, c, c_partner)
     own, to_partner, to_other, cc = pl.pallas_call(
         functools.partial(fine_kernel, planes),
         out_shape=(fields, fields, fields, shape(3 * reach, coarse_rows, coarse_lanes)),
-        in_specs=[smem] + [anywhere] * 3 + [in_hbm] * 2 + [anywhere],
+        in_specs=[smem] + [anywhere] + [in_hbm] * 2 + [anywhere] + whole(9),
         out_specs=tuple(whole(4)),
         scratch_shapes=[
-            VMEM((3 * planes, blocks, rows, 128), F32),
+            VMEM((planes, blocks, rows, 128), F32),
             VMEM((2, planes, blocks, rows, 128), F32),
-            VMEM((3 * planes, rows, lanes), F32),
-            VMEM((7, 3 * planes, rows, lanes), F32),
+            VMEM((planes + 2, rows, lanes), F32),
+            VMEM((7, planes + 1, rows, lanes), F32),
             VMEM((2, 3 * planes, rows, lanes), F32),
             VMEM((2, 3 * planes, rows, lanes), F32),
             VMEM((7, reach, coarse_rows, coarse_lanes), F32),
             VMEM((2 * reach, coarse_rows, coarse_lanes), F32),
-            pltpu.SemaphoreType.DMA((3, blocks)),
+            pltpu.SemaphoreType.DMA((blocks,)),
             pltpu.SemaphoreType.DMA((2, blocks)),
         ],
         compiler_params=params(VMEM_LIMITS["fine"]),
         name="fine",
-    )(flags, c, c_partner, c_other, field, initial, received)
-
-    def cost(microseconds):
-        return pl.CostEstimate(flops=int(microseconds * 4e6), bytes_accessed=0, transcendentals=0)
+    )(flags, c_other, field, initial, received, *prepared)
 
     base = pl.pallas_call(
         base_kernel,

time: 98.1 us -> 96.5 us (0.984)
  waiting for transfers between devices: 46.3 us -> 42.5 us
  Pallas kernels: 30.1 us -> 32 us
    pallas_call x0 -> x1, Pallas kernels: none -> 3.41 us  [local(): pl.pallas_call(functools.partial(near_kernel, planes), out_shape=(*[shape...]
    ppermute x1, waiting for transfers between devices: 24.9 us -> 21.7 us  [local(): received = lax.ppermute(to_row_partner, 'tm', row_pairs)]
    pallas_call x1, Pallas kernels: 20.7 us -> 18.3 us  [local(): pl.pallas_call(functools.partial(fine_kernel, planes), out_shape=(fields,...]
  transfers between devices with their start and end apart: 12 -> 12, of which waited for: 7 -> 6; matrix products, arithmetic and copies ran while one was open for 1% -> 1% of each run, Pallas kernels for 4% -> 7%
where the time goes in v6:
time: 96.5 us; the launch traced here: 95.2 us
  waiting for transfers between devices  42.5 us (44%)
  Pallas kernels  32 us (33%)
  starting transfers between devices  19.5 us (20%)
    ppermute x1, waiting for transfers between devices, local(): received = lax.ppermute(to_row_partner, 'tm', row_pairs)  21.7 us
    pallas_call x1, Pallas kernels, local(): pl.pallas_call(functools.partial(fine_kernel, planes), out_shape=(fields,...  18.3 us
    ppermute x4, waiting for transfers between devices, other_swap(): return lax.ppermute(x, 'space', swap_pairs(slabs, 1))  15 us
    ppermute x4, starting transfers between devices, other_swap(): return lax.ppermute(x, 'space', swap_pairs(slabs, 1))  12.6 us
    ppermute x3, waiting for transfers between devices, local(): arrived[shift] = lax.ppermute(send, 'tm', pairs) if shift else send  5.8 us
    ppermute x3, starting transfers between devices, local(): arrived[shift] = lax.ppermute(send, 'tm', pairs) if shift else send  5.42 us
    pallas_call x1, Pallas kernels, local(): pl.pallas_call(functools.partial(near_kernel, planes), out_shape=(*[shape...  3.41 us
    pallas_call x1, Pallas kernels, local(): pl.pallas_call(slice_kernel, out_shape=(shape(planes, rows, lanes), shape...  2.57 us
  transfers between devices with their start and end apart: 12, of which 6 were waited for; matrix products, arithmetic and copies ran while one was open for 1% of the time, Pallas kernels for 7%

profile of v6, /device:TPU:28, one launch (start us, length us, event | category | flops | bytes accessed | tf_op | source)
XLA Modules:
  0.0 95.2 jit_solution(9884459777122285335)
XLA Ops:
  0.0 2.6 %slices.1 = (f32[4,144,512]{2,1,0:T(8,128)S(1)}, f32[4,128,512]{2,1,0:T(8,128)}) custom-call(f32[4,256,512]{2,1,0:T(8,128)} %c_hbm.1, f32[4,256,512]{2,1,0:T(8,128)} %bitcast.7), custom_call_target="tpu_custom_call" | custom-call | tf_op jit(solution)/shard_map/slices/pallas_call | solution.py:604
  2.6 0.1 collective-permute-start.2
  2.7 3.4 %collective-permute-start = (f32[4,144,512]{2,1,0:T(8,128)S(1)}, f32[4,144,512]{2,1,0:T(8,128)S(1)}, u32[]{:S(2)}, u32[]{:S(2)}) collective-permute-start(f32[4,144,512]{2,1,0:T(8,128)S(1)} %get-tuple-element.32.c_hbm), channel_id=1, source_target_pairs={{1,2},{2,1},{3,4},{4,3},{5,6},{6,5},{9,10},{10,9},{11,12},{12,11},... | collective-permute-start | bytes 3538952 | tf_op jit(solution)/shard_map/ppermute | solution.py:600
  6.1 1.3 %collective-permute-start.1 = (f32[4,128,512]{2,1,0:T(8,128)}, f32[4,128,512]{2,1,0:T(8,128)}, u32[]{:S(2)}, u32[]{:S(2)}) collective-permute-start(f32[4,128,512]{2,1,0:T(8,128)} %get-tuple-element.33), channel_id=1, source_target_pairs={{0,8},{8,0},{16,24},{1,9},{9,1},{17,25},{2,10},{10,2},{18,26},{3,1... | collective-permute-start | bytes 3145736 | tf_op jit(solution)/shard_map/ppermute | solution.py:615
  7.4 0.7 constant_dynamic-slice_fusion
  8.1 0.1 slice_bitcast_fusion
  8.2 0.1 pad_add_fusion.flag_ref
  8.3 0.0 collective-permute-done.2.partner_hbm
  8.3 3.4 %near.1 = (f32[7,144,512]{2,1,0:T(8,128)S(1)}, f32[7,144,512]{2,1,0:T(8,128)S(1)}, f32[7,144,512]{2,1,0:T(8,128)S(1)}, f32[7,144,512]{2,1,0:T(8,128)S(1)}, f32[7...) custom-call(s32[14]{0:T(128)S(1)} %pad_add_fusion.flag_ref, ...), custom_call_target="tpu_custom_call" | custom-call | flops 24000000 | tf_op jit(solution)/shard_map/near/pallas_call | solution.py:630
  11.7 21.7 %collective-permute-done.1.received_hbm = f32[4,128,512]{2,1,0:T(8,128)} collective-permute-done((f32[4,128,512]{2,1,0:T(8,128)}, f32[4,128,512]{2,1,0:T(8,128)}, u32[]{:S(2)}, u32[]{:S(2)}) %collective-permute-start.1) | collective-permute-done | bytes 1048608 | tf_op jit(solution)/shard_map/ppermute | solution.py:615
  33.5 0.0 collective-permute-done.other_hbm
  33.5 18.3 %fine.1 = (f32[2,2,72,256]{3,2,1,0:T(8,128)S(1)}, f32[2,2,72,256]{3,2,1,0:T(8,128)S(1)}, f32[2,2,72,256]{3,2,1,0:T(8,128)S(1)}, f32[6,72,256]{2,1,0:T(8,128)S(1)}) custom-call(s32[14]{0:T(128)S(1)} %pad_add_fusion.flag_ref, f32[4,144,512]{2,1,0:T(8,128)S(1)} %collective-permute-done.other_hbm, f32[4,256,512]{2,1,0:T(8,128)} %bitcast.8, ...), custom_call_target="tpu_custom_call" | custom-call | tf_op jit(solution)/shard_map/fine/pallas_call | solution.py:648
  51.8 0.1 collective-permute-start.3
  51.8 3.4 %collective-permute-start.4 = (f32[2,2,72,256]{3,2,1,0:T(8,128)S(1)}, f32[2,2,72,256]{3,2,1,0:T(8,128)S(1)}, u32[]{:S(2)}, u32[]{:S(2)}) collective-permute-start(f32[2,2,72,256]{3,2,1,0:T(8,128)S(1)} %get-tuple-element.46), channel_id=1, source_target_pairs={{1,2},{2,1},{3,4},{4,3},{5,6},{6,5},{9,10},{10,9},{11,12},{12,11},... | collective-permute-start | bytes 884744 | tf_op jit(solution)/shard_map/ppermute | solution.py:600
  55.3 0.0 collective-permute-done.3.partner_ref
  55.3 7.9 %collective-permute-done.4.other_ref = f32[2,2,72,256]{3,2,1,0:T(8,128)S(1)} collective-permute-done((f32[2,2,72,256]{3,2,1,0:T(8,128)S(1)}, f32[2,2,72,256]{3,2,1,0:T(8,128)S(1)}, u32[]{:S(2)}, u32[]{:S(2)}) %collective-permute-start.4) | collective-permute-done | bytes 294944 | tf_op jit(solution)/shard_map/ppermute | solution.py:600
  63.1 0.6 gather.1
  63.7 0.1 collective-permute-start.5
  63.8 2.5 %collective-permute-start.6 = (f32[3,72,256]{2,1,0:T(8,128)S(1)}, f32[3,72,256]{2,1,0:T(8,128)S(1)}, u32[]{:S(2)}, u32[]{:S(2)}) collective-permute-start(f32[3,72,256]{2,1,0:T(8,128)S(1)} %get-tuple-element.48), channel_id=1, source_target_pairs={{1,2},{2,1},{3,4},{4,3},{5,6},{6,5},{9,10},{10,9},{11,12},{12,11},... | collective-permute-start | bytes 663560 | tf_op jit(solution)/shard_map/ppermute | solution.py:600
  66.4 0.2 weights.1.weight_ref
  66.6 0.0 collective-permute-done.5.partner_ref
  66.6 6.4 %collective-permute-done.6.other_ref = f32[3,72,256]{2,1,0:T(8,128)S(1)} collective-permute-done((f32[3,72,256]{2,1,0:T(8,128)S(1)}, f32[3,72,256]{2,1,0:T(8,128)S(1)}, u32[]{:S(2)}, u32[]{:S(2)}) %collective-permute-start.6) | collective-permute-done | bytes 221216 | tf_op jit(solution)/shard_map/ppermute | solution.py:600
  73.0 1.1 %shard_map.46 = (f32[2,72,256]{2,1,0:T(8,128)S(1)}, f32[2,72,256]{2,1,0:T(8,128)S(1)}, f32[1,72,256]{2,1,0:T(8,128)S(1)}, f32[1,72,256]{2,1,0:T(8,128)S(1)}, f32...) custom-call(s32[14]{0:T(128)S(1)} %pad_add_fusion.flag_ref, f32[7,4,72,256]{3,2,1,0:T(8,128)S(1)} %weights.1.weight_ref, ...), custom_call_target="tpu_custom_call" | custom-call | tf_op jit(solution)/shard_map/pallas_call | solution.py:722
  74.1 0.0 copy-start
  74.1 0.1 collective-permute-start.7
  74.2 3.2 %collective-permute-start.8 = (f32[1,72,256]{2,1,0:T(8,128)S(1)}, f32[1,72,256]{2,1,0:T(8,128)S(1)}, u32[]{:S(2)}, u32[]{:S(2)}) collective-permute-start(f32[1,72,256]{2,1,0:T(8,128)S(1)} %get-tuple-element.52), channel_id=1, source_target_pairs={{1,2},{2,1},{3,4},{4,3},{5,6},{6,5},{9,10},{10,9},{11,12},{12,11},... | collective-permute-start | bytes 221192 | tf_op jit(solution)/shard_map/ppermute | solution.py:600
  77.4 0.4 collective-permute-start.10
  77.8 2.3 %collective-permute-start.11 = (f32[2,72,256]{2,1,0:T(8,128)S(1)}, f32[2,72,256]{2,1,0:T(8,128)S(1)}, u32[]{:S(2)}, u32[]{:S(2)}) collective-permute-start(f32[2,72,256]{2,1,0:T(8,128)S(1)} %get-tuple-element.58), channel_id=1, source_target_pairs={{0,24},{16,8},{24,16},{1,25},{17,9},{25,17},{2,26},{18,10},{26,18}... | collective-permute-start | bytes 442376 | tf_op jit(solution)/shard_map/ppermute | solution.py:716
  80.2 0.0 collective-permute-done.7.partner_ref
  80.2 0.7 collective-permute-done.8.other_ref
  80.9 1.4 %shard_map.47 = (f32[2,72,256]{2,1,0:T(8,128)}, f32[2,72,256]{2,1,0:T(8,128)S(1)}, f32[2,72,256]{2,1,0:T(8,128)S(1)}) custom-call(s32[14]{0:T(128)S(1)} %pad_add_fusion.flag_ref, f32[7,4,72,256]{3,2,1,0:T(8,128)S(1)} %weights.1.weight_ref, f32[1,72,256]{2,1,0:T(8,128)S(1)} %collective-permute-done.7.partner_ref, ...), custom_call_target="tpu_custom_call" | custom-call | tf_op jit(solution)/shard_map/pallas_call | solution.py:722
  82.3 2.7 %collective-permute-start.9 = (f32[2,72,256]{2,1,0:T(8,128)S(1)}, f32[2,72,256]{2,1,0:T(8,128)S(1)}, u32[]{:S(2)}, u32[]{:S(2)}) collective-permute-start(f32[2,72,256]{2,1,0:T(8,128)S(1)} %get-tuple-element.56), channel_id=1, source_target_pairs={{0,8},{8,16},{16,24},{24,0},{1,9},{9,17},{17,25},{25,1},{2,10},{10... | collective-permute-start | bytes 442376 | tf_op jit(solution)/shard_map/ppermute | solution.py:742
  85.0 0.0 copy-done
  85.0 1.8 %base.1.base_ref = f32[4,256,512]{2,1,0:T(8,128)S(1)} custom-call(f32[4,256,512]{2,1,0:T(8,128)S(1)} %bitcast.9), custom_call_target="tpu_custom_call" | custom-call | flops 16000000 | tf_op jit(solution)/shard_map/base/pallas_call | solution.py:669
  86.9 2.9 %collective-permute-done.10.refs_2_ = f32[2,72,256]{2,1,0:T(8,128)S(1)} collective-permute-done((f32[2,72,256]{2,1,0:T(8,128)S(1)}, f32[2,72,256]{2,1,0:T(8,128)S(1)}, u32[]{:S(2)}, u32[]{:S(2)}) %collective-permute-start.10) | collective-permute-done | bytes 147488 | tf_op jit(solution)/shard_map/ppermute | solution.py:716
  89.8 0.0 collective-permute-done.11.refs_3_
  89.8 2.9 %collective-permute-done.9.refs_1_ = f32[2,72,256]{2,1,0:T(8,128)S(1)} collective-permute-done((f32[2,72,256]{2,1,0:T(8,128)S(1)}, f32[2,72,256]{2,1,0:T(8,128)S(1)}, u32[]{:S(2)}, u32[]{:S(2)}) %collective-permute-start.9) | collective-permute-done | bytes 147488 | tf_op jit(solution)/shard_map/ppermute | solution.py:742
  92.6 2.5 %final.1 = f32[4,256,512]{2,1,0:T(8,128)} custom-call(s32[14]{0:T(128)S(1)} %pad_add_fusion.flag_ref, f32[4,256,512]{2,1,0:T(8,128)S(1)} %base.1.base_ref, f32[2,72,256]{2,1,0:T(8,128)S(1)} %get-tuple-element.55.refs_0_, f32[2,72,256]{2,1,0:T(8,128)S(1)} %collective-permute-done.9.refs_1_, f32[2,72,256]{2,1,0:T(8,128)S(1)} %collective-permute-done.10.refs_2_, ...), custom_call_target="tpu_custom_call" | custom-call | tf_op jit(solution)/shard_map/final/pallas_call | solution.py:744
Async XLA Ops:
  2.6 5.7 %collective-permute-start.2 = (f32[4,144,512]{2,1,0:T(8,128)S(1)}, f32[4,144,512]{2,1,0:T(8,128)S(1)}, u32[]{:S(2)}, u32[]{:S(2)}) collective-permute-start(f32[4,144,512]{2,1,0:T(8,128)S(1)} %get-tuple-element.32.c_hbm), channel_id=1, source_target_pairs={{0,1},{1,0},{2,3},{3,2},{4,5},{5,4},{6,7},{7,6},{8,9},{9,8},{10,11... | collective-permute-start | bytes 3538952 | tf_op jit(solution)/shard_map/ppermute | solution.py:597
  2.7 30.8 %collective-permute-start = (f32[4,144,512]{2,1,0:T(8,128)S(1)}, f32[4,144,512]{2,1,0:T(8,128)S(1)}, u32[]{:S(2)}, u32[]{:S(2)}) collective-permute-start(f32[4,144,512]{2,1,0:T(8,128)S(1)} %get-tuple-element.32.c_hbm), channel_id=1, source_target_pairs={{1,2},{2,1},{3,4},{4,3},{5,6},{6,5},{9,10},{10,9},{11,12},{12,11},... | collective-permute-start | bytes 3538952 | tf_op jit(solution)/shard_map/ppermute | solution.py:600
  6.1 27.4 %collective-permute-start.1 = (f32[4,128,512]{2,1,0:T(8,128)}, f32[4,128,512]{2,1,0:T(8,128)}, u32[]{:S(2)}, u32[]{:S(2)}) collective-permute-start(f32[4,128,512]{2,1,0:T(8,128)} %get-tuple-element.33), channel_id=1, source_target_pairs={{0,8},{8,0},{16,24},{1,9},{9,1},{17,25},{2,10},{10,2},{18,26},{3,1... | collective-permute-start | bytes 3145736 | tf_op jit(solution)/shard_map/ppermute | solution.py:615
  51.8 3.5 %collective-permute-start.3 = (f32[2,2,72,256]{3,2,1,0:T(8,128)S(1)}, f32[2,2,72,256]{3,2,1,0:T(8,128)S(1)}, u32[]{:S(2)}, u32[]{:S(2)}) collective-permute-start(f32[2,2,72,256]{3,2,1,0:T(8,128)S(1)} %get-tuple-element.45), channel_id=1, source_target_pairs={{0,1},{1,0},{2,3},{3,2},{4,5},{5,4},{6,7},{7,6},{8,9},{9,8},{10,11... | collective-permute-start | bytes 884744 | tf_op jit(solution)/shard_map/ppermute | solution.py:597
  51.8 11.3 %collective-permute-start.4 = (f32[2,2,72,256]{3,2,1,0:T(8,128)S(1)}, f32[2,2,72,256]{3,2,1,0:T(8,128)S(1)}, u32[]{:S(2)}, u32[]{:S(2)}) collective-permute-start(f32[2,2,72,256]{3,2,1,0:T(8,128)S(1)} %get-tuple-element.46), channel_id=1, source_target_pairs={{1,2},{2,1},{3,4},{4,3},{5,6},{6,5},{9,10},{10,9},{11,12},{12,11},... | collective-permute-start | bytes 884744 | tf_op jit(solution)/shard_map/ppermute | solution.py:600
  63.7 2.8 %collective-permute-start.5 = (f32[3,72,256]{2,1,0:T(8,128)S(1)}, f32[3,72,256]{2,1,0:T(8,128)S(1)}, u32[]{:S(2)}, u32[]{:S(2)}) collective-permute-start(f32[3,72,256]{2,1,0:T(8,128)S(1)} %get-tuple-element.47), channel_id=1, source_target_pairs={{0,1},{1,0},{2,3},{3,2},{4,5},{5,4},{6,7},{7,6},{8,9},{9,8},{10,11... | collective-permute-start | bytes 663560 | tf_op jit(solution)/shard_map/ppermute | solution.py:597
  63.8 9.2 %collective-permute-start.6 = (f32[3,72,256]{2,1,0:T(8,128)S(1)}, f32[3,72,256]{2,1,0:T(8,128)S(1)}, u32[]{:S(2)}, u32[]{:S(2)}) collective-permute-start(f32[3,72,256]{2,1,0:T(8,128)S(1)} %get-tuple-element.48), channel_id=1, source_target_pairs={{1,2},{2,1},{3,4},{4,3},{5,6},{6,5},{9,10},{10,9},{11,12},{12,11},... | collective-permute-start | bytes 663560 | tf_op jit(solution)/shard_map/ppermute | solution.py:600
  74.1 10.9 %copy-start = (f32[1,4,256,512]{3,2,1,0:T(8,128)S(1)}, f32[1,4,256,512]{3,2,1,0:T(8,128)}, u32[]{:S(2)}) copy-start(f32[1,4,256,512]{3,2,1,0:T(8,128)} %param.5) | copy-start | bytes 6291460
  74.1 6.0 %collective-permute-start.7 = (f32[1,72,256]{2,1,0:T(8,128)S(1)}, f32[1,72,256]{2,1,0:T(8,128)S(1)}, u32[]{:S(2)}, u32[]{:S(2)}) collective-permute-start(f32[1,72,256]{2,1,0:T(8,128)S(1)} %get-tuple-element.51), channel_id=1, source_target_pairs={{0,1},{1,0},{2,3},{3,2},{4,5},{5,4},{6,7},{7,6},{8,9},{9,8},{10,11... | collective-permute-start | bytes 221192 | tf_op jit(solution)/shard_map/ppermute | solution.py:597
  74.2 6.7 %collective-permute-start.8 = (f32[1,72,256]{2,1,0:T(8,128)S(1)}, f32[1,72,256]{2,1,0:T(8,128)S(1)}, u32[]{:S(2)}, u32[]{:S(2)}) collective-permute-start(f32[1,72,256]{2,1,0:T(8,128)S(1)} %get-tuple-element.52), channel_id=1, source_target_pairs={{1,2},{2,1},{3,4},{4,3},{5,6},{6,5},{9,10},{10,9},{11,12},{12,11},... | collective-permute-start | bytes 221192 | tf_op jit(solution)/shard_map/ppermute | solution.py:600
  77.4 12.4 %collective-permute-start.10 = (f32[2,72,256]{2,1,0:T(8,128)S(1)}, f32[2,72,256]{2,1,0:T(8,128)S(1)}, u32[]{:S(2)}, u32[]{:S(2)}) collective-permute-start(f32[2,72,256]{2,1,0:T(8,128)S(1)} %get-tuple-element.57), channel_id=1, source_target_pairs={{0,16},{8,24},{16,0},{24,8},{1,17},{9,25},{17,1},{25,9},{2,18},{10... | collective-permute-start | bytes 442376 | tf_op jit(solution)/shard_map/ppermute | solution.py:716
  77.8 12.0 %collective-permute-start.11 = (f32[2,72,256]{2,1,0:T(8,128)S(1)}, f32[2,72,256]{2,1,0:T(8,128)S(1)}, u32[]{:S(2)}, u32[]{:S(2)}) collective-permute-start(f32[2,72,256]{2,1,0:T(8,128)S(1)} %get-tuple-element.58), channel_id=1, source_target_pairs={{0,24},{16,8},{24,16},{1,25},{17,9},{25,17},{2,26},{18,10},{26,18}... | collective-permute-start | bytes 442376 | tf_op jit(solution)/shard_map/ppermute | solution.py:716
  82.3 10.3 %collective-permute-start.9 = (f32[2,72,256]{2,1,0:T(8,128)S(1)}, f32[2,72,256]{2,1,0:T(8,128)S(1)}, u32[]{:S(2)}, u32[]{:S(2)}) collective-permute-start(f32[2,72,256]{2,1,0:T(8,128)S(1)} %get-tuple-element.56), channel_id=1, source_target_pairs={{0,8},{8,16},{16,24},{24,0},{1,9},{9,17},{17,25},{25,1},{2,10},{10... | collective-permute-start | bytes 442376 | tf_op jit(solution)/shard_map/ppermute | solution.py:742

commit v7 on v6

--- a/solution.py
+++ b/solution.py
@@ -147,16 +147,20 @@
     return pl.multiple_of(value * step, 8)
 
 
-def slice_kernel(c_hbm, iterate_hbm, c_ref, send_ref, sem):
+def window_kernel(c_hbm, c_ref, sem):
+    half = lax.rem(lax.axis_index("tm"), 2)
+    window = pl.ds(at_row(half, c_hbm.shape[1] - c_ref.shape[1]), c_ref.shape[1])
+    copy = pltpu.make_async_copy(c_hbm.at[:, window, :], c_ref, sem)
+    copy.start()
+    copy.wait()
+
+
+def send_kernel(iterate_hbm, send_ref, sem):
     half = lax.rem(lax.axis_index("tm"), 2)
     own = send_ref.shape[1]
-    window = pl.ds(at_row(half, c_hbm.shape[1] - c_ref.shape[1]), c_ref.shape[1])
-    send = pltpu.make_async_copy(iterate_hbm.at[:, pl.ds(at_row(1 - half, own), own), :], send_ref, sem.at[0])
-    keep = pltpu.make_async_copy(c_hbm.at[:, window, :], c_ref, sem.at[1])
-    send.start()
-    keep.start()
-    send.wait()
-    keep.wait()
+    copy = pltpu.make_async_copy(iterate_hbm.at[:, pl.ds(at_row(1 - half, own), own), :], send_ref, sem)
+    copy.start()
+    copy.wait()
 
 
 def weigh_planes(c_ref, w_refs, shift, count):
@@ -486,12 +490,15 @@
     upper = flag_ref[1]
     refs = list(refs)
     values = refs[:count]
-    made = refs[count : count + len(slots)]
-    rest = refs[count + len(slots) :]
+    outs = len(slots) if edges else len(slots) - 1
+    made = refs[count : count + outs]
+    rest = refs[count + outs :]
     to_sides, rest = rest[: 2 * edges], rest[2 * edges :]
-    sends, (wide, extra_wide, middle) = rest[: len(send_slots)], rest[len(send_slots) :]
+    sends, (wide, extra_wide, middle, final_scr) = rest[: len(send_slots)], rest[len(send_slots) :]
     val_ref = values[-1]
     planes, rows, lanes = val_ref.shape
+    if not edges:
+        made = [*made, final_scr]
     add = [flag_ref[slot].astype(F32) for slot in slots]
     wide[planes : 2 * planes] = val_ref[...]
     sides = ((partner_ref, upper), (other_ref, 1 - upper))
@@ -601,15 +608,19 @@
 
     anywhere = pl.BlockSpec(memory_space=pl.ANY)
     in_hbm = pl.BlockSpec(memory_space=pltpu.HBM)
-    c, to_row_partner = pl.pallas_call(
-        slice_kernel,
-        out_shape=(shape(planes, rows, lanes), shape(planes, own_rows, lanes)),
-        in_specs=[in_hbm] * 2,
-        out_specs=tuple(whole(2)),
-        scratch_shapes=[pltpu.SemaphoreType.DMA((2,))],
-        compiler_params=params(VMEM_LIMITS["slices"]),
-        name="slices",
-    )(diffusivity, field)
+
+    def cut(kernel, count, source):
+        return pl.pallas_call(
+            kernel,
+            out_shape=shape(planes, count, lanes),
+            in_specs=[in_hbm],
+            out_specs=pl.BlockSpec(memory_space=VMEM),
+            scratch_shapes=[pltpu.SemaphoreType.DMA],
+            compiler_params=params(VMEM_LIMITS["slices"]),
+        )(source)
+
+    c = cut(window_kernel, rows, diffusivity)
+    to_row_partner = cut(send_kernel, own_rows, field)
     row_pairs = swap_pairs(layers, 0)
     row_pairs.remove((layers - 1, layers - 2))
     received = lax.ppermute(to_row_partner, "tm", row_pairs)
@@ -717,24 +728,26 @@
         count = len(values)
         steps = 2 if count == 1 and layers > 2 else 1
         more = count + steps < layers
+        kept = steps if more else steps - 1
         slots = [add_at + count - 1 + n for n in range(steps)]
         shifts = [shift for shift in range(layers) if arrived[shift] is None and ready[shift] < count + steps]
         made = pl.pallas_call(
             functools.partial(chain_kernel, slots, [send_at + shift for shift in shifts], count, int(more)),
-            out_shape=(*[block] * steps, *[plane] * (2 * more), *[block] * len(shifts)),
+            out_shape=(*[block] * kept, *[plane] * (2 * more), *[block] * len(shifts)),
             in_specs=[smem] + whole(4 + count),
-            out_specs=tuple(whole(steps + 2 * more + len(shifts))),
+            out_specs=tuple(whole(kept + 2 * more + len(shifts))),
             scratch_shapes=[
                 VMEM((3 * reach, coarse_rows, coarse_lanes), F32),
                 VMEM((reach + 2, coarse_rows, coarse_lanes), F32),
                 VMEM((reach + 2, coarse_rows, coarse_lanes), F32),
+                VMEM((reach, coarse_rows, coarse_lanes), F32),
             ],
             compiler_params=params(VMEM_LIMITS["small"]),
         )(flags, weights, from_partner, from_other, extra, *values)
-        values += made[:steps]
+        values += made[:kept] if more else [None] * steps
         if more:
-            to_partner, to_other = made[steps : steps + 2]
-        sent = list(zip(shifts, made[steps + 2 * more :]))
+            to_partner, to_other = made[kept : kept + 2]
+        sent = list(zip(shifts, made[kept + 2 * more :]))
     for shift, send in sent:
         pairs = [
             (source, (source + shift) % layers) for source in range(layers) if table[source][1 + layers + shift] >= 0

time: 96.5 us -> 96.6 us (level)
  local copies, waits for them, and re-layouts: 0.77 us -> 2.52 us
    unnamed x2 -> x6, local copies, waits for them, and re-layouts: 0.01 us -> 1.75 us
    pallas_call x1 -> x2, Pallas kernels: 2.57 us -> 1.18 us  [cut(): pl.pallas_call(kernel, out_shape=shape(planes, count, lanes), in_specs=[i...]
    ppermute x1, waiting for transfers between devices: 21.7 us -> 20.6 us  [local(): received = lax.ppermute(to_row_partner, 'tm', row_pairs)]
    pallas_call x1, Pallas kernels: 3.41 us -> 4.5 us  [local(): pl.pallas_call(functools.partial(near_kernel, planes), out_shape=(*[shape...]
  transfers between devices with their start and end apart: 12 -> 12, of which waited for: 6 -> 6; matrix products, arithmetic and copies ran while one was open for 1% -> 1% of each run, Pallas kernels for 7% -> 9%
where the time goes in v7:
time: 96.6 us; the launch traced here: 95.3 us
  waiting for transfers between devices  41.7 us (43%)
  Pallas kernels  31.7 us (33%)
  starting transfers between devices  19.1 us (20%)
  local copies, waits for them, and re-layouts  2.52 us (3%)
    ppermute x1, waiting for transfers between devices, local(): received = lax.ppermute(to_row_partner, 'tm', row_pairs)  20.6 us
    pallas_call x1, Pallas kernels, local(): pl.pallas_call(functools.partial(fine_kernel, planes), out_shape=(fields,...  19 us
    ppermute x4, waiting for transfers between devices, other_swap(): return lax.ppermute(x, 'space', swap_pairs(slabs, 1))  15.4 us
    ppermute x4, starting transfers between devices, other_swap(): return lax.ppermute(x, 'space', swap_pairs(slabs, 1))  12.6 us
    ppermute x3, waiting for transfers between devices, local(): arrived[shift] = lax.ppermute(send, 'tm', pairs) if shift else send  5.68 us
    ppermute x3, starting transfers between devices, local(): arrived[shift] = lax.ppermute(send, 'tm', pairs) if shift else send  4.98 us
    pallas_call x1, Pallas kernels, local(): pl.pallas_call(functools.partial(near_kernel, planes), out_shape=(*[shape...  4.5 us
    pallas_call x1, Pallas kernels, local(): pl.pallas_call(functools.partial(final_kernel, [half_at + shift for shift...  2.52 us
  transfers between devices with their start and end apart: 12, of which 6 were waited for; matrix products, arithmetic and copies ran while one was open for 1% of the time, Pallas kernels for 9%

profile of v7, /device:TPU:28, one launch (start us, length us, event | category | flops | bytes accessed | tf_op | source)
XLA Modules:
  0.0 95.3 jit_solution(3993460254476902501)
XLA Ops:
  0.0 0.0 copy-start
  0.0 0.0 copy-start.2
  0.0 1.7 %copy-done.2 = f32[4,256,512]{2,1,0:T(8,128)S(1)} copy-done((f32[4,256,512]{2,1,0:T(8,128)S(1)}, f32[4,256,512]{2,1,0:T(8,128)}, u32[]{:S(2)}) %copy-start.2) | copy-done | bytes 2097176
  1.7 0.1 shard_map.46.c_hbm
  1.9 0.1 collective-permute-start.2
  2.0 3.4 %collective-permute-start = (f32[4,144,512]{2,1,0:T(8,128)S(1)}, f32[4,144,512]{2,1,0:T(8,128)}, u32[]{:S(2)}, u32[]{:S(2)}) collective-permute-start(f32[4,144,512]{2,1,0:T(8,128)S(1)} %shard_map.46.c_hbm), channel_id=1, source_target_pairs={{1,2},{2,1},{3,4},{4,3},{5,6},{6,5},{9,10},{10,9},{11,12},{12,11},... | collective-permute-start | bytes 3538952 | tf_op jit(solution)/shard_map/ppermute | solution.py:607
  5.4 0.0 copy-done
  5.4 1.1 %shard_map.47 = f32[4,128,512]{2,1,0:T(8,128)} custom-call(f32[4,256,512]{2,1,0:T(8,128)S(1)} %bitcast.8), custom_call_target="tpu_custom_call" | custom-call | tf_op jit(solution)/shard_map/pallas_call | solution.py:613
  6.5 1.3 %collective-permute-start.1 = (f32[4,128,512]{2,1,0:T(8,128)}, f32[4,128,512]{2,1,0:T(8,128)S(1)}, u32[]{:S(2)}, u32[]{:S(2)}) collective-permute-start(f32[4,128,512]{2,1,0:T(8,128)} %shard_map.47), channel_id=1, source_target_pairs={{0,8},{8,0},{16,24},{1,9},{9,1},{17,25},{2,10},{10,2},{18,26},{3,1... | collective-permute-start | bytes 3145736 | tf_op jit(solution)/shard_map/ppermute | solution.py:626
  7.8 0.7 constant_dynamic-slice_fusion
  8.5 0.1 slice_bitcast_fusion
  8.6 0.1 pad_add_fusion.flag_ref
  8.7 0.0 collective-permute-done.2.partner_hbm
  8.7 4.5 %near.1 = (f32[7,144,512]{2,1,0:T(8,128)S(1)}, f32[7,144,512]{2,1,0:T(8,128)S(1)}, f32[7,144,512]{2,1,0:T(8,128)S(1)}, f32[7,144,512]{2,1,0:T(8,128)S(1)}, f32[7...) custom-call(s32[14]{0:T(128)S(1)} %pad_add_fusion.flag_ref, ...), custom_call_target="tpu_custom_call" | custom-call | flops 24000000 | tf_op jit(solution)/shard_map/near/pallas_call | solution.py:641
  13.2 20.6 %collective-permute-done.1.received_hbm = f32[4,128,512]{2,1,0:T(8,128)S(1)} collective-permute-done((f32[4,128,512]{2,1,0:T(8,128)}, f32[4,128,512]{2,1,0:T(8,128)S(1)}, u32[]{:S(2)}, u32[]{:S(2)}) %collective-permute-start.1) | collective-permute-done | bytes 1048608 | tf_op jit(solution)/shard_map/ppermute | solution.py:626
  33.7 0.0 collective-permute-done.other_hbm
  33.7 19.0 %fine.1 = (f32[2,2,72,256]{3,2,1,0:T(8,128)S(1)}, f32[2,2,72,256]{3,2,1,0:T(8,128)S(1)}, f32[2,2,72,256]{3,2,1,0:T(8,128)S(1)}, f32[6,72,256]{2,1,0:T(8,128)S(1)}) custom-call(s32[14]{0:T(128)S(1)} %pad_add_fusion.flag_ref, f32[4,144,512]{2,1,0:T(8,128)} %collective-permute-done.other_hbm, f32[4,256,512]{2,1,0:T(8,128)} %bitcast.7, ...), custom_call_target="tpu_custom_call" | custom-call | tf_op jit(solution)/shard_map/fine/pallas_call | solution.py:659
  52.7 0.1 collective-permute-start.3
  52.8 3.4 %collective-permute-start.4 = (f32[2,2,72,256]{3,2,1,0:T(8,128)S(1)}, f32[2,2,72,256]{3,2,1,0:T(8,128)S(1)}, u32[]{:S(2)}, u32[]{:S(2)}) collective-permute-start(f32[2,2,72,256]{3,2,1,0:T(8,128)S(1)} %get-tuple-element.42), channel_id=1, source_target_pairs={{1,2},{2,1},{3,4},{4,3},{5,6},{6,5},{9,10},{10,9},{11,12},{12,11},... | collective-permute-start | bytes 884744 | tf_op jit(solution)/shard_map/ppermute | solution.py:607
  56.2 0.0 collective-permute-done.3.partner_ref
  56.2 7.8 %collective-permute-done.4.other_ref = f32[2,2,72,256]{3,2,1,0:T(8,128)S(1)} collective-permute-done((f32[2,2,72,256]{3,2,1,0:T(8,128)S(1)}, f32[2,2,72,256]{3,2,1,0:T(8,128)S(1)}, u32[]{:S(2)}, u32[]{:S(2)}) %collective-permute-start.4) | collective-permute-done | bytes 294944 | tf_op jit(solution)/shard_map/ppermute | solution.py:607
  64.0 0.6 gather.1
  64.6 0.1 collective-permute-start.5
  64.7 2.6 %collective-permute-start.6 = (f32[3,72,256]{2,1,0:T(8,128)S(1)}, f32[3,72,256]{2,1,0:T(8,128)S(1)}, u32[]{:S(2)}, u32[]{:S(2)}) collective-permute-start(f32[3,72,256]{2,1,0:T(8,128)S(1)} %get-tuple-element.44), channel_id=1, source_target_pairs={{1,2},{2,1},{3,4},{4,3},{5,6},{6,5},{9,10},{10,9},{11,12},{12,11},... | collective-permute-start | bytes 663560 | tf_op jit(solution)/shard_map/ppermute | solution.py:607
  67.3 0.2 weights.1.weight_ref
  67.5 0.0 collective-permute-done.5.partner_ref
  67.5 6.4 %collective-permute-done.6.other_ref = f32[3,72,256]{2,1,0:T(8,128)S(1)} collective-permute-done((f32[3,72,256]{2,1,0:T(8,128)S(1)}, f32[3,72,256]{2,1,0:T(8,128)S(1)}, u32[]{:S(2)}, u32[]{:S(2)}) %collective-permute-start.6) | collective-permute-done | bytes 221216 | tf_op jit(solution)/shard_map/ppermute | solution.py:607
  73.9 1.1 %shard_map.48 = (f32[2,72,256]{2,1,0:T(8,128)S(1)}, f32[2,72,256]{2,1,0:T(8,128)S(1)}, f32[1,72,256]{2,1,0:T(8,128)S(1)}, f32[1,72,256]{2,1,0:T(8,128)S(1)}, f32...) custom-call(s32[14]{0:T(128)S(1)} %pad_add_fusion.flag_ref, f32[7,4,72,256]{3,2,1,0:T(8,128)S(1)} %weights.1.weight_ref, ...), custom_call_target="tpu_custom_call" | custom-call | tf_op jit(solution)/shard_map/pallas_call | solution.py:734
  75.0 0.0 copy-start.1
  75.0 0.1 collective-permute-start.7
  75.1 3.2 %collective-permute-start.8 = (f32[1,72,256]{2,1,0:T(8,128)S(1)}, f32[1,72,256]{2,1,0:T(8,128)S(1)}, u32[]{:S(2)}, u32[]{:S(2)}) collective-permute-start(f32[1,72,256]{2,1,0:T(8,128)S(1)} %get-tuple-element.48), channel_id=1, source_target_pairs={{1,2},{2,1},{3,4},{4,3},{5,6},{6,5},{9,10},{10,9},{11,12},{12,11},... | collective-permute-start | bytes 221192 | tf_op jit(solution)/shard_map/ppermute | solution.py:607
  78.3 0.4 collective-permute-start.10
  78.7 1.9 %collective-permute-start.11 = (f32[2,72,256]{2,1,0:T(8,128)S(1)}, f32[2,72,256]{2,1,0:T(8,128)S(1)}, u32[]{:S(2)}, u32[]{:S(2)}) collective-permute-start(f32[2,72,256]{2,1,0:T(8,128)S(1)} %get-tuple-element.54), channel_id=1, source_target_pairs={{0,24},{16,8},{24,16},{1,25},{17,9},{25,17},{2,26},{18,10},{26,18}... | collective-permute-start | bytes 442376 | tf_op jit(solution)/shard_map/ppermute | solution.py:727
  80.6 0.0 collective-permute-done.7.partner_ref
  80.6 1.2 %collective-permute-done.8.other_ref = f32[1,72,256]{2,1,0:T(8,128)S(1)} collective-permute-done((f32[1,72,256]{2,1,0:T(8,128)S(1)}, f32[1,72,256]{2,1,0:T(8,128)S(1)}, u32[]{:S(2)}, u32[]{:S(2)}) %collective-permute-start.8) | collective-permute-done | bytes 73760 | tf_op jit(solution)/shard_map/ppermute | solution.py:607
  81.8 0.8 shard_map.49
  82.6 2.7 %collective-permute-start.9 = (f32[2,72,256]{2,1,0:T(8,128)S(1)}, f32[2,72,256]{2,1,0:T(8,128)S(1)}, u32[]{:S(2)}, u32[]{:S(2)}) collective-permute-start(f32[2,72,256]{2,1,0:T(8,128)S(1)} %get-tuple-element.52), channel_id=1, source_target_pairs={{0,8},{8,16},{16,24},{24,0},{1,9},{9,17},{17,25},{25,1},{2,10},{10... | collective-permute-start | bytes 442376 | tf_op jit(solution)/shard_map/ppermute | solution.py:755
  85.3 0.0 copy-done.1
  85.3 1.8 %base.1.base_ref = f32[4,256,512]{2,1,0:T(8,128)S(1)} custom-call(f32[4,256,512]{2,1,0:T(8,128)S(1)} %bitcast.9), custom_call_target="tpu_custom_call" | custom-call | flops 16000000 | tf_op jit(solution)/shard_map/base/pallas_call | solution.py:680
  87.1 2.7 %collective-permute-done.10.refs_2_ = f32[2,72,256]{2,1,0:T(8,128)S(1)} collective-permute-done((f32[2,72,256]{2,1,0:T(8,128)S(1)}, f32[2,72,256]{2,1,0:T(8,128)S(1)}, u32[]{:S(2)}, u32[]{:S(2)}) %collective-permute-start.10) | collective-permute-done | bytes 147488 | tf_op jit(solution)/shard_map/ppermute | solution.py:727
  89.9 0.0 collective-permute-done.11.refs_3_
  89.9 2.9 %collective-permute-done.9.refs_1_ = f32[2,72,256]{2,1,0:T(8,128)S(1)} collective-permute-done((f32[2,72,256]{2,1,0:T(8,128)S(1)}, f32[2,72,256]{2,1,0:T(8,128)S(1)}, u32[]{:S(2)}, u32[]{:S(2)}) %collective-permute-start.9) | collective-permute-done | bytes 147488 | tf_op jit(solution)/shard_map/ppermute | solution.py:755
  92.8 2.5 %final.1 = f32[4,256,512]{2,1,0:T(8,128)} custom-call(s32[14]{0:T(128)S(1)} %pad_add_fusion.flag_ref, f32[4,256,512]{2,1,0:T(8,128)S(1)} %base.1.base_ref, f32[2,72,256]{2,1,0:T(8,128)S(1)} %get-tuple-element.51.refs_0_, f32[2,72,256]{2,1,0:T(8,128)S(1)} %collective-permute-done.9.refs_1_, f32[2,72,256]{2,1,0:T(8,128)S(1)} %collective-permute-done.10.refs_2_, ...), custom_call_target="tpu_custom_call" | custom-call | tf_op jit(solution)/shard_map/final/pallas_call | solution.py:757
Async XLA Ops:
  0.0 5.4 %copy-start = (f32[1,4,256,512]{3,2,1,0:T(8,128)S(1)}, f32[1,4,256,512]{3,2,1,0:T(8,128)}, u32[]{:S(2)}) copy-start(f32[1,4,256,512]{3,2,1,0:T(8,128)} %param.5) | copy-start | bytes 6291460
  0.0 1.7 %copy-start.2 = (f32[4,256,512]{2,1,0:T(8,128)S(1)}, f32[4,256,512]{2,1,0:T(8,128)}, u32[]{:S(2)}) copy-start(f32[4,256,512]{2,1,0:T(8,128)} %c_hbm.1) | copy-start | bytes 6291460
  1.9 6.8 %collective-permute-start.2 = (f32[4,144,512]{2,1,0:T(8,128)S(1)}, f32[4,144,512]{2,1,0:T(8,128)}, u32[]{:S(2)}, u32[]{:S(2)}) collective-permute-start(f32[4,144,512]{2,1,0:T(8,128)S(1)} %shard_map.46.c_hbm), channel_id=1, source_target_pairs={{0,1},{1,0},{2,3},{3,2},{4,5},{5,4},{6,7},{7,6},{8,9},{9,8},{10,11... | collective-permute-start | bytes 3538952 | tf_op jit(solution)/shard_map/ppermute | solution.py:604
  2.0 31.8 %collective-permute-start = (f32[4,144,512]{2,1,0:T(8,128)S(1)}, f32[4,144,512]{2,1,0:T(8,128)}, u32[]{:S(2)}, u32[]{:S(2)}) collective-permute-start(f32[4,144,512]{2,1,0:T(8,128)S(1)} %shard_map.46.c_hbm), channel_id=1, source_target_pairs={{1,2},{2,1},{3,4},{4,3},{5,6},{6,5},{9,10},{10,9},{11,12},{12,11},... | collective-permute-start | bytes 3538952 | tf_op jit(solution)/shard_map/ppermute | solution.py:607
  6.5 27.3 %collective-permute-start.1 = (f32[4,128,512]{2,1,0:T(8,128)}, f32[4,128,512]{2,1,0:T(8,128)S(1)}, u32[]{:S(2)}, u32[]{:S(2)}) collective-permute-start(f32[4,128,512]{2,1,0:T(8,128)} %shard_map.47), channel_id=1, source_target_pairs={{0,8},{8,0},{16,24},{1,9},{9,1},{17,25},{2,10},{10,2},{18,26},{3,1... | collective-permute-start | bytes 3145736 | tf_op jit(solution)/shard_map/ppermute | solution.py:626
  52.7 3.5 %collective-permute-start.3 = (f32[2,2,72,256]{3,2,1,0:T(8,128)S(1)}, f32[2,2,72,256]{3,2,1,0:T(8,128)S(1)}, u32[]{:S(2)}, u32[]{:S(2)}) collective-permute-start(f32[2,2,72,256]{3,2,1,0:T(8,128)S(1)} %get-tuple-element.41), channel_id=1, source_target_pairs={{0,1},{1,0},{2,3},{3,2},{4,5},{5,4},{6,7},{7,6},{8,9},{9,8},{10,11... | collective-permute-start | bytes 884744 | tf_op jit(solution)/shard_map/ppermute | solution.py:604
  52.8 11.2 %collective-permute-start.4 = (f32[2,2,72,256]{3,2,1,0:T(8,128)S(1)}, f32[2,2,72,256]{3,2,1,0:T(8,128)S(1)}, u32[]{:S(2)}, u32[]{:S(2)}) collective-permute-start(f32[2,2,72,256]{3,2,1,0:T(8,128)S(1)} %get-tuple-element.42), channel_id=1, source_target_pairs={{1,2},{2,1},{3,4},{4,3},{5,6},{6,5},{9,10},{10,9},{11,12},{12,11},... | collective-permute-start | bytes 884744 | tf_op jit(solution)/shard_map/ppermute | solution.py:607
  64.6 2.9 %collective-permute-start.5 = (f32[3,72,256]{2,1,0:T(8,128)S(1)}, f32[3,72,256]{2,1,0:T(8,128)S(1)}, u32[]{:S(2)}, u32[]{:S(2)}) collective-permute-start(f32[3,72,256]{2,1,0:T(8,128)S(1)} %get-tuple-element.43), channel_id=1, source_target_pairs={{0,1},{1,0},{2,3},{3,2},{4,5},{5,4},{6,7},{7,6},{8,9},{9,8},{10,11... | collective-permute-start | bytes 663560 | tf_op jit(solution)/shard_map/ppermute | solution.py:604
  64.7 9.2 %collective-permute-start.6 = (f32[3,72,256]{2,1,0:T(8,128)S(1)}, f32[3,72,256]{2,1,0:T(8,128)S(1)}, u32[]{:S(2)}, u32[]{:S(2)}) collective-permute-start(f32[3,72,256]{2,1,0:T(8,128)S(1)} %get-tuple-element.44), channel_id=1, source_target_pairs={{1,2},{2,1},{3,4},{4,3},{5,6},{6,5},{9,10},{10,9},{11,12},{12,11},... | collective-permute-start | bytes 663560 | tf_op jit(solution)/shard_map/ppermute | solution.py:607
  75.0 10.3 %copy-start.1 = (f32[1,4,256,512]{3,2,1,0:T(8,128)S(1)}, f32[1,4,256,512]{3,2,1,0:T(8,128)}, u32[]{:S(2)}) copy-start(f32[1,4,256,512]{3,2,1,0:T(8,128)} %param.5) | copy-start | bytes 6291460
  75.0 5.6 %collective-permute-start.7 = (f32[1,72,256]{2,1,0:T(8,128)S(1)}, f32[1,72,256]{2,1,0:T(8,128)S(1)}, u32[]{:S(2)}, u32[]{:S(2)}) collective-permute-start(f32[1,72,256]{2,1,0:T(8,128)S(1)} %get-tuple-element.47), channel_id=1, source_target_pairs={{0,1},{1,0},{2,3},{3,2},{4,5},{5,4},{6,7},{7,6},{8,9},{9,8},{10,11... | collective-permute-start | bytes 221192 | tf_op jit(solution)/shard_map/ppermute | solution.py:604
  75.1 6.7 %collective-permute-start.8 = (f32[1,72,256]{2,1,0:T(8,128)S(1)}, f32[1,72,256]{2,1,0:T(8,128)S(1)}, u32[]{:S(2)}, u32[]{:S(2)}) collective-permute-start(f32[1,72,256]{2,1,0:T(8,128)S(1)} %get-tuple-element.48), channel_id=1, source_target_pairs={{1,2},{2,1},{3,4},{4,3},{5,6},{6,5},{9,10},{10,9},{11,12},{12,11},... | collective-permute-start | bytes 221192 | tf_op jit(solution)/shard_map/ppermute | solution.py:607
  78.3 11.6 %collective-permute-start.10 = (f32[2,72,256]{2,1,0:T(8,128)S(1)}, f32[2,72,256]{2,1,0:T(8,128)S(1)}, u32[]{:S(2)}, u32[]{:S(2)}) collective-permute-start(f32[2,72,256]{2,1,0:T(8,128)S(1)} %get-tuple-element.53), channel_id=1, source_target_pairs={{0,16},{8,24},{16,0},{24,8},{1,17},{9,25},{17,1},{25,9},{2,18},{10... | collective-permute-start | bytes 442376 | tf_op jit(solution)/shard_map/ppermute | solution.py:727
  78.7 11.2 %collective-permute-start.11 = (f32[2,72,256]{2,1,0:T(8,128)S(1)}, f32[2,72,256]{2,1,0:T(8,128)S(1)}, u32[]{:S(2)}, u32[]{:S(2)}) collective-permute-start(f32[2,72,256]{2,1,0:T(8,128)S(1)} %get-tuple-element.54), channel_id=1, source_target_pairs={{0,24},{16,8},{24,16},{1,25},{17,9},{25,17},{2,26},{18,10},{26,18}... | collective-permute-start | bytes 442376 | tf_op jit(solution)/shard_map/ppermute | solution.py:727
  82.6 10.2 %collective-permute-start.9 = (f32[2,72,256]{2,1,0:T(8,128)S(1)}, f32[2,72,256]{2,1,0:T(8,128)S(1)}, u32[]{:S(2)}, u32[]{:S(2)}) collective-permute-start(f32[2,72,256]{2,1,0:T(8,128)S(1)} %get-tuple-element.52), channel_id=1, source_target_pairs={{0,8},{8,16},{16,24},{24,0},{1,9},{9,17},{17,25},{25,1},{2,10},{10... | collective-permute-start | bytes 442376 | tf_op jit(solution)/shard_map/ppermute | solution.py:755

commit v8 on v6

--- a/solution.py
+++ b/solution.py
@@ -486,12 +486,15 @@
     upper = flag_ref[1]
     refs = list(refs)
     values = refs[:count]
-    made = refs[count : count + len(slots)]
-    rest = refs[count + len(slots) :]
+    outs = len(slots) if edges else len(slots) - 1
+    made = refs[count : count + outs]
+    rest = refs[count + outs :]
     to_sides, rest = rest[: 2 * edges], rest[2 * edges :]
-    sends, (wide, extra_wide, middle) = rest[: len(send_slots)], rest[len(send_slots) :]
+    sends, (wide, extra_wide, middle, final_scr) = rest[: len(send_slots)], rest[len(send_slots) :]
     val_ref = values[-1]
     planes, rows, lanes = val_ref.shape
+    if not edges:
+        made = [*made, final_scr]
     add = [flag_ref[slot].astype(F32) for slot in slots]
     wide[planes : 2 * planes] = val_ref[...]
     sides = ((partner_ref, upper), (other_ref, 1 - upper))
@@ -717,24 +720,26 @@
         count = len(values)
         steps = 2 if count == 1 and layers > 2 else 1
         more = count + steps < layers
+        kept = steps if more else steps - 1
         slots = [add_at + count - 1 + n for n in range(steps)]
         shifts = [shift for shift in range(layers) if arrived[shift] is None and ready[shift] < count + steps]
         made = pl.pallas_call(
             functools.partial(chain_kernel, slots, [send_at + shift for shift in shifts], count, int(more)),
-            out_shape=(*[block] * steps, *[plane] * (2 * more), *[block] * len(shifts)),
+            out_shape=(*[block] * kept, *[plane] * (2 * more), *[block] * len(shifts)),
             in_specs=[smem] + whole(4 + count),
-            out_specs=tuple(whole(steps + 2 * more + len(shifts))),
+            out_specs=tuple(whole(kept + 2 * more + len(shifts))),
             scratch_shapes=[
                 VMEM((3 * reach, coarse_rows, coarse_lanes), F32),
                 VMEM((reach + 2, coarse_rows, coarse_lanes), F32),
                 VMEM((reach + 2, coarse_rows, coarse_lanes), F32),
+                VMEM((reach, coarse_rows, coarse_lanes), F32),
             ],
             compiler_params=params(VMEM_LIMITS["small"]),
         )(flags, weights, from_partner, from_other, extra, *values)
-        values += made[:steps]
+        values += made[:kept] if more else [None] * steps
         if more:
-            to_partner, to_other = made[steps : steps + 2]
-        sent = list(zip(shifts, made[steps + 2 * more :]))
+            to_partner, to_other = made[kept : kept + 2]
+        sent = list(zip(shifts, made[kept + 2 * more :]))
     for shift, send in sent:
         pairs = [
             (source, (source + shift) % layers) for source in range(layers) if table[source][1 + layers + shift] >= 0

time: 96.5 us -> 96.5 us (level)
  no operation moved by 1% of the time
where the time goes in v8:
time: 96.5 us; the launch traced here: 95.2 us
  waiting for transfers between devices  43.1 us (45%)
  Pallas kernels  31.4 us (33%)
  starting transfers between devices  19.6 us (20%)
    ppermute x1, waiting for transfers between devices, local(): received = lax.ppermute(to_row_partner, 'tm', row_pairs)  21.7 us
    pallas_call x1, Pallas kernels, local(): pl.pallas_call(functools.partial(fine_kernel, planes), out_shape=(fields,...  18.3 us
    ppermute x4, waiting for transfers between devices, other_swap(): return lax.ppermute(x, 'space', swap_pairs(slabs, 1))  15 us
    ppermute x4, starting transfers between devices, other_swap(): return lax.ppermute(x, 'space', swap_pairs(slabs, 1))  12.6 us
    ppermute x3, waiting for transfers between devices, local(): arrived[shift] = lax.ppermute(send, 'tm', pairs) if shift else send  6.4 us
    ppermute x3, starting transfers between devices, local(): arrived[shift] = lax.ppermute(send, 'tm', pairs) if shift else send  5.47 us
    pallas_call x1, Pallas kernels, local(): pl.pallas_call(functools.partial(near_kernel, planes), out_shape=(*[shape...  3.41 us
    pallas_call x1, Pallas kernels, local(): pl.pallas_call(slice_kernel, out_shape=(shape(planes, rows, lanes), shape...  2.57 us
  transfers between devices with their start and end apart: 12, of which 6 were waited for; matrix products, arithmetic and copies ran while one was open for 1% of the time, Pallas kernels for 7%

profile of v8, /device:TPU:28, one launch (start us, length us, event | category | flops | bytes accessed | tf_op | source)
XLA Modules:
  0.0 95.2 jit_solution(8116214240716250385)
XLA Ops:
  0.0 2.6 %slices.1 = (f32[4,144,512]{2,1,0:T(8,128)S(1)}, f32[4,128,512]{2,1,0:T(8,128)}) custom-call(f32[4,256,512]{2,1,0:T(8,128)} %c_hbm.1, f32[4,256,512]{2,1,0:T(8,128)} %bitcast.7), custom_call_target="tpu_custom_call" | custom-call | tf_op jit(solution)/shard_map/slices/pallas_call | solution.py:607
  2.6 0.1 collective-permute-start.2
  2.7 3.4 %collective-permute-start = (f32[4,144,512]{2,1,0:T(8,128)S(1)}, f32[4,144,512]{2,1,0:T(8,128)S(1)}, u32[]{:S(2)}, u32[]{:S(2)}) collective-permute-start(f32[4,144,512]{2,1,0:T(8,128)S(1)} %get-tuple-element.32.c_hbm), channel_id=1, source_target_pairs={{1,2},{2,1},{3,4},{4,3},{5,6},{6,5},{9,10},{10,9},{11,12},{12,11},... | collective-permute-start | bytes 3538952 | tf_op jit(solution)/shard_map/ppermute | solution.py:603
  6.1 1.3 %collective-permute-start.1 = (f32[4,128,512]{2,1,0:T(8,128)}, f32[4,128,512]{2,1,0:T(8,128)}, u32[]{:S(2)}, u32[]{:S(2)}) collective-permute-start(f32[4,128,512]{2,1,0:T(8,128)} %get-tuple-element.33), channel_id=1, source_target_pairs={{0,8},{8,0},{16,24},{1,9},{9,1},{17,25},{2,10},{10,2},{18,26},{3,1... | collective-permute-start | bytes 3145736 | tf_op jit(solution)/shard_map/ppermute | solution.py:618
  7.4 0.7 constant_dynamic-slice_fusion
  8.1 0.1 slice_bitcast_fusion
  8.2 0.1 pad_add_fusion.flag_ref
  8.3 0.0 collective-permute-done.2.partner_hbm
  8.3 3.4 %near.1 = (f32[7,144,512]{2,1,0:T(8,128)S(1)}, f32[7,144,512]{2,1,0:T(8,128)S(1)}, f32[7,144,512]{2,1,0:T(8,128)S(1)}, f32[7,144,512]{2,1,0:T(8,128)S(1)}, f32[7...) custom-call(s32[14]{0:T(128)S(1)} %pad_add_fusion.flag_ref, ...), custom_call_target="tpu_custom_call" | custom-call | flops 24000000 | tf_op jit(solution)/shard_map/near/pallas_call | solution.py:633
  11.7 21.7 %collective-permute-done.1.received_hbm = f32[4,128,512]{2,1,0:T(8,128)} collective-permute-done((f32[4,128,512]{2,1,0:T(8,128)}, f32[4,128,512]{2,1,0:T(8,128)}, u32[]{:S(2)}, u32[]{:S(2)}) %collective-permute-start.1) | collective-permute-done | bytes 1048608 | tf_op jit(solution)/shard_map/ppermute | solution.py:618
  33.5 0.0 collective-permute-done.other_hbm
  33.5 18.3 %fine.1 = (f32[2,2,72,256]{3,2,1,0:T(8,128)S(1)}, f32[2,2,72,256]{3,2,1,0:T(8,128)S(1)}, f32[2,2,72,256]{3,2,1,0:T(8,128)S(1)}, f32[6,72,256]{2,1,0:T(8,128)S(1)}) custom-call(s32[14]{0:T(128)S(1)} %pad_add_fusion.flag_ref, f32[4,144,512]{2,1,0:T(8,128)S(1)} %collective-permute-done.other_hbm, f32[4,256,512]{2,1,0:T(8,128)} %bitcast.8, ...), custom_call_target="tpu_custom_call" | custom-call | tf_op jit(solution)/shard_map/fine/pallas_call | solution.py:651
  51.8 0.1 collective-permute-start.3
  51.8 3.4 %collective-permute-start.4 = (f32[2,2,72,256]{3,2,1,0:T(8,128)S(1)}, f32[2,2,72,256]{3,2,1,0:T(8,128)S(1)}, u32[]{:S(2)}, u32[]{:S(2)}) collective-permute-start(f32[2,2,72,256]{3,2,1,0:T(8,128)S(1)} %get-tuple-element.46), channel_id=1, source_target_pairs={{1,2},{2,1},{3,4},{4,3},{5,6},{6,5},{9,10},{10,9},{11,12},{12,11},... | collective-permute-start | bytes 884744 | tf_op jit(solution)/shard_map/ppermute | solution.py:603
  55.3 0.0 collective-permute-done.3.partner_ref
  55.3 7.9 %collective-permute-done.4.other_ref = f32[2,2,72,256]{3,2,1,0:T(8,128)S(1)} collective-permute-done((f32[2,2,72,256]{3,2,1,0:T(8,128)S(1)}, f32[2,2,72,256]{3,2,1,0:T(8,128)S(1)}, u32[]{:S(2)}, u32[]{:S(2)}) %collective-permute-start.4) | collective-permute-done | bytes 294944 | tf_op jit(solution)/shard_map/ppermute | solution.py:603
  63.1 0.6 gather.1
  63.7 0.1 collective-permute-start.5
  63.8 2.5 %collective-permute-start.6 = (f32[3,72,256]{2,1,0:T(8,128)S(1)}, f32[3,72,256]{2,1,0:T(8,128)S(1)}, u32[]{:S(2)}, u32[]{:S(2)}) collective-permute-start(f32[3,72,256]{2,1,0:T(8,128)S(1)} %get-tuple-element.48), channel_id=1, source_target_pairs={{1,2},{2,1},{3,4},{4,3},{5,6},{6,5},{9,10},{10,9},{11,12},{12,11},... | collective-permute-start | bytes 663560 | tf_op jit(solution)/shard_map/ppermute | solution.py:603
  66.4 0.2 weights.1.weight_ref
  66.6 0.0 collective-permute-done.5.partner_ref
  66.6 6.4 %collective-permute-done.6.other_ref = f32[3,72,256]{2,1,0:T(8,128)S(1)} collective-permute-done((f32[3,72,256]{2,1,0:T(8,128)S(1)}, f32[3,72,256]{2,1,0:T(8,128)S(1)}, u32[]{:S(2)}, u32[]{:S(2)}) %collective-permute-start.6) | collective-permute-done | bytes 221216 | tf_op jit(solution)/shard_map/ppermute | solution.py:603
  73.0 1.1 %shard_map.46 = (f32[2,72,256]{2,1,0:T(8,128)S(1)}, f32[2,72,256]{2,1,0:T(8,128)S(1)}, f32[1,72,256]{2,1,0:T(8,128)S(1)}, f32[1,72,256]{2,1,0:T(8,128)S(1)}, f32...) custom-call(s32[14]{0:T(128)S(1)} %pad_add_fusion.flag_ref, f32[7,4,72,256]{3,2,1,0:T(8,128)S(1)} %weights.1.weight_ref, ...), custom_call_target="tpu_custom_call" | custom-call | tf_op jit(solution)/shard_map/pallas_call | solution.py:726
  74.1 0.0 copy-start
  74.1 0.1 collective-permute-start.7
  74.2 3.2 %collective-permute-start.8 = (f32[1,72,256]{2,1,0:T(8,128)S(1)}, f32[1,72,256]{2,1,0:T(8,128)S(1)}, u32[]{:S(2)}, u32[]{:S(2)}) collective-permute-start(f32[1,72,256]{2,1,0:T(8,128)S(1)} %get-tuple-element.52), channel_id=1, source_target_pairs={{1,2},{2,1},{3,4},{4,3},{5,6},{6,5},{9,10},{10,9},{11,12},{12,11},... | collective-permute-start | bytes 221192 | tf_op jit(solution)/shard_map/ppermute | solution.py:603
  77.4 0.4 collective-permute-start.10
  77.8 2.3 %collective-permute-start.11 = (f32[2,72,256]{2,1,0:T(8,128)S(1)}, f32[2,72,256]{2,1,0:T(8,128)S(1)}, u32[]{:S(2)}, u32[]{:S(2)}) collective-permute-start(f32[2,72,256]{2,1,0:T(8,128)S(1)} %get-tuple-element.58), channel_id=1, source_target_pairs={{0,24},{16,8},{24,16},{1,25},{17,9},{25,17},{2,26},{18,10},{26,18}... | collective-permute-start | bytes 442376 | tf_op jit(solution)/shard_map/ppermute | solution.py:719
  80.2 0.0 collective-permute-done.7.partner_ref
  80.2 0.7 collective-permute-done.8.other_ref
  80.9 0.8 shard_map.47
  81.7 2.7 %collective-permute-start.9 = (f32[2,72,256]{2,1,0:T(8,128)S(1)}, f32[2,72,256]{2,1,0:T(8,128)S(1)}, u32[]{:S(2)}, u32[]{:S(2)}) collective-permute-start(f32[2,72,256]{2,1,0:T(8,128)S(1)} %get-tuple-element.56), channel_id=1, source_target_pairs={{0,8},{8,16},{16,24},{24,0},{1,9},{9,17},{17,25},{25,1},{2,10},{10... | collective-permute-start | bytes 442376 | tf_op jit(solution)/shard_map/ppermute | solution.py:747
  84.4 0.0 copy-done
  84.4 1.8 %base.1.base_ref = f32[4,256,512]{2,1,0:T(8,128)S(1)} custom-call(f32[4,256,512]{2,1,0:T(8,128)S(1)} %bitcast.9), custom_call_target="tpu_custom_call" | custom-call | flops 16000000 | tf_op jit(solution)/shard_map/base/pallas_call | solution.py:672
  86.3 3.5 %collective-permute-done.10.refs_2_ = f32[2,72,256]{2,1,0:T(8,128)S(1)} collective-permute-done((f32[2,72,256]{2,1,0:T(8,128)S(1)}, f32[2,72,256]{2,1,0:T(8,128)S(1)}, u32[]{:S(2)}, u32[]{:S(2)}) %collective-permute-start.10) | collective-permute-done | bytes 147488 | tf_op jit(solution)/shard_map/ppermute | solution.py:719
  89.8 0.0 collective-permute-done.11.refs_3_
  89.8 2.9 %collective-permute-done.9.refs_1_ = f32[2,72,256]{2,1,0:T(8,128)S(1)} collective-permute-done((f32[2,72,256]{2,1,0:T(8,128)S(1)}, f32[2,72,256]{2,1,0:T(8,128)S(1)}, u32[]{:S(2)}, u32[]{:S(2)}) %collective-permute-start.9) | collective-permute-done | bytes 147488 | tf_op jit(solution)/shard_map/ppermute | solution.py:747
  92.6 2.5 %final.1 = f32[4,256,512]{2,1,0:T(8,128)} custom-call(s32[14]{0:T(128)S(1)} %pad_add_fusion.flag_ref, f32[4,256,512]{2,1,0:T(8,128)S(1)} %base.1.base_ref, f32[2,72,256]{2,1,0:T(8,128)S(1)} %get-tuple-element.55.refs_0_, f32[2,72,256]{2,1,0:T(8,128)S(1)} %collective-permute-done.9.refs_1_, f32[2,72,256]{2,1,0:T(8,128)S(1)} %collective-permute-done.10.refs_2_, ...), custom_call_target="tpu_custom_call" | custom-call | tf_op jit(solution)/shard_map/final/pallas_call | solution.py:749
Async XLA Ops:
  2.6 5.7 %collective-permute-start.2 = (f32[4,144,512]{2,1,0:T(8,128)S(1)}, f32[4,144,512]{2,1,0:T(8,128)S(1)}, u32[]{:S(2)}, u32[]{:S(2)}) collective-permute-start(f32[4,144,512]{2,1,0:T(8,128)S(1)} %get-tuple-element.32.c_hbm), channel_id=1, source_target_pairs={{0,1},{1,0},{2,3},{3,2},{4,5},{5,4},{6,7},{7,6},{8,9},{9,8},{10,11... | collective-permute-start | bytes 3538952 | tf_op jit(solution)/shard_map/ppermute | solution.py:600
  2.7 30.8 %collective-permute-start = (f32[4,144,512]{2,1,0:T(8,128)S(1)}, f32[4,144,512]{2,1,0:T(8,128)S(1)}, u32[]{:S(2)}, u32[]{:S(2)}) collective-permute-start(f32[4,144,512]{2,1,0:T(8,128)S(1)} %get-tuple-element.32.c_hbm), channel_id=1, source_target_pairs={{1,2},{2,1},{3,4},{4,3},{5,6},{6,5},{9,10},{10,9},{11,12},{12,11},... | collective-permute-start | bytes 3538952 | tf_op jit(solution)/shard_map/ppermute | solution.py:603
  6.1 27.4 %collective-permute-start.1 = (f32[4,128,512]{2,1,0:T(8,128)}, f32[4,128,512]{2,1,0:T(8,128)}, u32[]{:S(2)}, u32[]{:S(2)}) collective-permute-start(f32[4,128,512]{2,1,0:T(8,128)} %get-tuple-element.33), channel_id=1, source_target_pairs={{0,8},{8,0},{16,24},{1,9},{9,1},{17,25},{2,10},{10,2},{18,26},{3,1... | collective-permute-start | bytes 3145736 | tf_op jit(solution)/shard_map/ppermute | solution.py:618
  51.8 3.5 %collective-permute-start.3 = (f32[2,2,72,256]{3,2,1,0:T(8,128)S(1)}, f32[2,2,72,256]{3,2,1,0:T(8,128)S(1)}, u32[]{:S(2)}, u32[]{:S(2)}) collective-permute-start(f32[2,2,72,256]{3,2,1,0:T(8,128)S(1)} %get-tuple-element.45), channel_id=1, source_target_pairs={{0,1},{1,0},{2,3},{3,2},{4,5},{5,4},{6,7},{7,6},{8,9},{9,8},{10,11... | collective-permute-start | bytes 884744 | tf_op jit(solution)/shard_map/ppermute | solution.py:600
  51.8 11.3 %collective-permute-start.4 = (f32[2,2,72,256]{3,2,1,0:T(8,128)S(1)}, f32[2,2,72,256]{3,2,1,0:T(8,128)S(1)}, u32[]{:S(2)}, u32[]{:S(2)}) collective-permute-start(f32[2,2,72,256]{3,2,1,0:T(8,128)S(1)} %get-tuple-element.46), channel_id=1, source_target_pairs={{1,2},{2,1},{3,4},{4,3},{5,6},{6,5},{9,10},{10,9},{11,12},{12,11},... | collective-permute-start | bytes 884744 | tf_op jit(solution)/shard_map/ppermute | solution.py:603
  63.7 2.8 %collective-permute-start.5 = (f32[3,72,256]{2,1,0:T(8,128)S(1)}, f32[3,72,256]{2,1,0:T(8,128)S(1)}, u32[]{:S(2)}, u32[]{:S(2)}) collective-permute-start(f32[3,72,256]{2,1,0:T(8,128)S(1)} %get-tuple-element.47), channel_id=1, source_target_pairs={{0,1},{1,0},{2,3},{3,2},{4,5},{5,4},{6,7},{7,6},{8,9},{9,8},{10,11... | collective-permute-start | bytes 663560 | tf_op jit(solution)/shard_map/ppermute | solution.py:600
  63.8 9.2 %collective-permute-start.6 = (f32[3,72,256]{2,1,0:T(8,128)S(1)}, f32[3,72,256]{2,1,0:T(8,128)S(1)}, u32[]{:S(2)}, u32[]{:S(2)}) collective-permute-start(f32[3,72,256]{2,1,0:T(8,128)S(1)} %get-tuple-element.48), channel_id=1, source_target_pairs={{1,2},{2,1},{3,4},{4,3},{5,6},{6,5},{9,10},{10,9},{11,12},{12,11},... | collective-permute-start | bytes 663560 | tf_op jit(solution)/shard_map/ppermute | solution.py:603
  74.1 10.3 %copy-start = (f32[1,4,256,512]{3,2,1,0:T(8,128)S(1)}, f32[1,4,256,512]{3,2,1,0:T(8,128)}, u32[]{:S(2)}) copy-start(f32[1,4,256,512]{3,2,1,0:T(8,128)} %param.5) | copy-start | bytes 6291460
  74.1 6.0 %collective-permute-start.7 = (f32[1,72,256]{2,1,0:T(8,128)S(1)}, f32[1,72,256]{2,1,0:T(8,128)S(1)}, u32[]{:S(2)}, u32[]{:S(2)}) collective-permute-start(f32[1,72,256]{2,1,0:T(8,128)S(1)} %get-tuple-element.51), channel_id=1, source_target_pairs={{0,1},{1,0},{2,3},{3,2},{4,5},{5,4},{6,7},{7,6},{8,9},{9,8},{10,11... | collective-permute-start | bytes 221192 | tf_op jit(solution)/shard_map/ppermute | solution.py:600
  74.2 6.7 %collective-permute-start.8 = (f32[1,72,256]{2,1,0:T(8,128)S(1)}, f32[1,72,256]{2,1,0:T(8,128)S(1)}, u32[]{:S(2)}, u32[]{:S(2)}) collective-permute-start(f32[1,72,256]{2,1,0:T(8,128)S(1)} %get-tuple-element.52), channel_id=1, source_target_pairs={{1,2},{2,1},{3,4},{4,3},{5,6},{6,5},{9,10},{10,9},{11,12},{12,11},... | collective-permute-start | bytes 221192 | tf_op jit(solution)/shard_map/ppermute | solution.py:603
  77.4 12.4 %collective-permute-start.10 = (f32[2,72,256]{2,1,0:T(8,128)S(1)}, f32[2,72,256]{2,1,0:T(8,128)S(1)}, u32[]{:S(2)}, u32[]{:S(2)}) collective-permute-start(f32[2,72,256]{2,1,0:T(8,128)S(1)} %get-tuple-element.57), channel_id=1, source_target_pairs={{0,16},{8,24},{16,0},{24,8},{1,17},{9,25},{17,1},{25,9},{2,18},{10... | collective-permute-start | bytes 442376 | tf_op jit(solution)/shard_map/ppermute | solution.py:719
  77.8 12.0 %collective-permute-start.11 = (f32[2,72,256]{2,1,0:T(8,128)S(1)}, f32[2,72,256]{2,1,0:T(8,128)S(1)}, u32[]{:S(2)}, u32[]{:S(2)}) collective-permute-start(f32[2,72,256]{2,1,0:T(8,128)S(1)} %get-tuple-element.58), channel_id=1, source_target_pairs={{0,24},{16,8},{24,16},{1,25},{17,9},{25,17},{2,26},{18,10},{26,18}... | collective-permute-start | bytes 442376 | tf_op jit(solution)/shard_map/ppermute | solution.py:719
  81.7 11.0 %collective-permute-start.9 = (f32[2,72,256]{2,1,0:T(8,128)S(1)}, f32[2,72,256]{2,1,0:T(8,128)S(1)}, u32[]{:S(2)}, u32[]{:S(2)}) collective-permute-start(f32[2,72,256]{2,1,0:T(8,128)S(1)} %get-tuple-element.56), channel_id=1, source_target_pairs={{0,8},{8,16},{16,24},{24,0},{1,9},{9,17},{17,25},{25,1},{2,10},{10... | collective-permute-start | bytes 442376 | tf_op jit(solution)/shard_map/ppermute | solution.py:747
